TPU v7x, 128 devices: a whole 4x4x4 slice. The times are simulated.
128 devices in a mesh: gx: 8 (over z, core), gy: 4 (over x), lev: 4 (over y).
Axes of the slice: x: 4, y: 4, z: 4, core: 2. Of those that a mesh axis runs over, the one named last changes fastest.
Arguments:
- u_wind: float32 [256, 128, 512], P('lev', 'gx', 'gy'), may hold values from -6 to 6
- v_wind: float32 [256, 128, 512], P('lev', 'gx', 'gy'), may hold values from -6 to 6
- w_wind: float32 [256, 128, 512], P('lev', 'gx', 'gy'), may hold values from -4 to 4
- pressure: float32 [256, 128, 512], P('lev', 'gx', 'gy'), may hold values from -6 to 6
- buoyancy: float32 [256, 128, 512], P('lev', 'gx', 'gy'), may hold values from 0.5 to 2
- stiffness: float32 [256, 128, 512], P('lev', 'gx', 'gy'), may hold values from 0.5 to 2
Outputs:
- u_final: float32 [256, 128, 512], P('lev', 'gx', 'gy')
- v_final: float32 [256, 128, 512], P('lev', 'gx', 'gy')
- w_final: float32 [256, 128, 512], P('lev', 'gx', 'gy')
- p_final: float32 [256, 128, 512], P('lev', 'gx', 'gy')
All inputs are finite; a program needn't handle non-finite values.
Results may differ from a plain program's by a relative error of at most 0.002.
Values sent between devices are 32-bit elements; how exact they have to be, the bound alone decides.
No kernel may reach another device: no remote copies, remote signals or barrier semaphores. Data moves between devices by JAX's collectives and lax.ppermute only.
A program may use at most 128 MiB of HBM per device.

v0:
```python
import functools

import jax
import jax.numpy as jnp
from jax import lax
from jax.experimental import pallas as pl
from jax.experimental.pallas import tpu as pltpu
from jax.sharding import PartitionSpec as P

SUBSTEPS = 3

courant_h = 0.3
vertical_gain = 4096.0

F32 = jnp.float32
NI, NK, NL = 16, 64, 128
TK = NK // 8


def level(k):
    return pl.ds(NI * k, NI)


def level_ik(k):
    return pl.ds(k, NI, stride=NK)


def row(i):
    return pl.ds(NK * i, NK)


def row_ki(i):
    return pl.ds(i, NK, stride=NI)


def vmem(*shape):
    return pltpu.VMEM(shape, F32)


BLOCK = (NI * NK, NL)
PACK = (4 * 8, NL)


def call(body, outs, args, name):
    whole = pl.BlockSpec(memory_space=pltpu.VMEM)
    args = [pltpu.with_memory_space_constraint(x, pltpu.VMEM) for x in args]
    return pl.pallas_call(
        body,
        out_shape=tuple(vmem(*shape) for shape in outs),
        in_specs=[whole] * len(args),
        out_specs=(whole,) * len(outs),
        name=name,
        compiler_params=pltpu.CompilerParams(vmem_limit_bytes=2 << 20),
    )(*args)


def pack_edges(field, pack, at):
    lane = lax.broadcasted_iota(jnp.int32, (8, NL), 1) // 4
    for group in range(4):
        packed = jnp.zeros((8, NL), F32)
        for tile in range(32):
            i, kt = group * 4 + tile // 8, tile % 8
            rolled = pltpu.roll(field[pl.ds(NK * i + 8 * kt, 8), :], 4 * tile + 2, 1)
            packed = jnp.where(lane == tile, rolled, packed)
        pack[pl.ds(at + 8 * group, 8), :] = packed


def unpacked(packs, i):
    source = packs[8 * (i // 4) : 8 * (i // 4) + 8]
    parts = []
    for kt in range(TK):
        base = 4 * ((i % 4) * 8 + kt) + 2
        parts.append(pltpu.roll(source, (NL - base) % NL, 1))
    return jnp.concatenate(parts, 0)


def prologue(p_in, u_in, v_in, b_in, p, u, v, b, to_up, to_down, edges):
    for source, target in ((p_in, p), (u_in, u), (v_in, v), (b_in, b)):
        for i in range(NI):
            target[row(i), :] = source[row_ki(i), :]
    for at, (field, i) in enumerate(((p, 14), (p, 15), (u, 15), (b, 15))):
        to_up[row(at), :] = field[row(i), :]
    for at, (field, i) in enumerate(((p, 0), (p, 1), (u, 0), (b, 0))):
        to_down[row(at), :] = field[row(i), :]
    for at, field in enumerate((p, v, b)):
        pack_edges(field, edges, 32 * at)


def factor(b_in, s_in, w_in, s, theta, rest, g_out, eta, inv, t1, y1, a_p, top_p, a_w, top_w, statics, sums):
    for i in range(NI):
        s[row(i), :] = s_in[row_ki(i), :]
    first = s_in[level(0), :]
    passed = first
    held = None
    for k in range(NK):
        g = 1.0 / (vertical_gain * b_in[level(k), :])
        g_out[level(k), :] = g
        if k == 0:
            c = first
        else:
            stiff = s_in[level(k), :]
            ratio = 1.0 / (held + stiff)
            th = held * ratio
            rs = stiff * ratio
            theta[level(k), :] = th
            rest[level(k), :] = rs
            c = stiff * th
            passed = passed * rs
        held = g + c
        ic = 1.0 / held
        inv[level(k), :] = ic
        eta[level(k), :] = c * ic
        t1[level(k), :] = (g * ic) * passed
        y1[level(k), :] = passed * ic
    theta[level(0), :] = jnp.ones((NI, NL), F32)
    rest[level(0), :] = jnp.zeros((NI, NL), F32)
    statics[level(1), :] = passed
    statics[level(2), :] = held
    weight = jnp.ones((NI, NL), F32)
    above = jnp.zeros((NI, NL), F32)
    reply_above = None
    sum_a = jnp.zeros((NI, NL), F32)
    sum_t = jnp.zeros((NI, NL), F32)
    for k in range(NK - 1, -1, -1):
        g = g_out[level(k), :]
        w = w_in[level(k), :]
        top_p[level_ik(k), :] = theta[level(k), :] * weight
        gw = g * weight
        top_w[level(k), :] = gw
        sum_t = sum_t + gw * w
        weight = weight * rest[level(k), :]
        reply = y1[level(k), :] - inv[level(k), :] * above
        above = t1[level(k), :] + eta[level(k), :] * above
        gr = g * reply
        a_w[level(k), :] = gr
        sum_a = sum_a - gr * w
        if reply_above is not None:
            a_p[level_ik(k + 1), :] = reply - reply_above
        reply_above = reply
    a_p[level_ik(0), :] = 1.0 - reply_above
    statics[level(0), :] = above
    sums[level(0), :] = sum_a
    sums[level(1), :] = sum_t


def explicit(first, last, *refs):
    (p, u, v, b, s, a_p, top_p, sums, own, low, high, left, right, low0, high0, left0, right0), refs = refs[:17], refs[17:]
    if first:
        statics, refs = refs[0], refs[1:]
        u_low, u_high = low0[row(2), :], high0[row(2), :]
    else:
        (u_halo, v_halo), refs = refs[:2], refs[2:]
        u_low, u_high = u_halo[row(0), :], u_halo[row(1), :]
    u_new, v_new, p_star, message = refs[:4]
    u_next = list(refs[4:])
    lane = lax.broadcasted_iota(jnp.int32, PACK, 1) % 4
    low_slot = lane == 2
    joined = lambda from_left, from_right, by: jnp.where(
        low_slot, pltpu.roll(from_left, by, 1), pltpu.roll(from_right, NL - by, 1)
    )
    near = joined(left[0:32, :], right[0:32, :], 1)
    far = joined(left[0:32, :], right[0:32, :], 2)
    b_side = joined(left0[64:96, :], right0[64:96, :], 1)
    v_side = joined(left0[32:64, :], right0[32:64, :], 1) if first else v_halo[...]
    gap = own[0:32, :] - far
    v_side = v_side - courant_h * b_side * jnp.where(low_slot, gap, -gap)
    p_low2, p_low1 = low[row(0), :], low[row(1), :]
    p_high1, p_high2 = high[row(0), :], high[row(1), :]
    u_low = u_low - courant_h * low0[row(3), :] * (p[row(0), :] - p_low2)
    u_high = u_high - courant_h * high0[row(3), :] * (p_high2 - p[row(NI - 1), :])
    if not last:
        u_next[0][row(0), :] = u_low
        u_next[0][row(1), :] = u_high
        u_next[1][...] = v_side
    lane = lax.broadcasted_iota(jnp.int32, (NK, NL), 1)
    ends = (lane == 0, lane == NL - 1)

    def difference(x, halo):
        up = jnp.where(ends[1], halo, pltpu.roll(x, NL - 1, 1))
        down = jnp.where(ends[0], halo, pltpu.roll(x, 1, 1))
        return up - down

    def u_row(i):
        above = p_high1 if i == NI - 1 else p[row(i + 1), :]
        below = p_low1 if i == 0 else p[row(i - 1), :]
        return u[row(i), :] - courant_h * b[row(i), :] * (above - below)

    before, here = u_low, u_row(0)
    for i in range(NI):
        after = u_high if i == NI - 1 else u_row(i + 1)
        pressure = p[row(i), :]
        vn = v[row(i), :] - courant_h * b[row(i), :] * difference(pressure, unpacked(near, i))
        divergence = (after - before) + difference(vn, unpacked(v_side, i))
        star = pressure - courant_h * s[row(i), :] * divergence
        if last:
            u_new[row_ki(i), :] = here
            v_new[row_ki(i), :] = vn
        else:
            u_new[row(i), :] = here
            v_new[row(i), :] = vn
        p_star[row_ki(i), :] = star
        message[pl.ds(i, 1), :] = sums[pl.ds(i, 1), :] + jnp.sum(a_p[row(i), :] * star, 0, keepdims=True)
        message[pl.ds(NI + i, 1), :] = sums[pl.ds(NI + i, 1), :] + jnp.sum(top_p[row(i), :] * star, 0, keepdims=True)
        before, here = here, after
    if first:
        message[pl.ds(2 * NI, 3 * NI), :] = statics[...]


def upward(p_star, w, theta, rest, g_in, eta, inv, t0, y0):
    carried = None
    for k in range(NK):
        star = p_star[level(k), :]
        gw = g_in[level(k), :] * w[level(k), :]
        if k == 0:
            carried = star
        else:
            carried = theta[level(k), :] * star + rest[level(k), :] * (carried + held_gw)
        held_gw = gw
        e = eta[level(k), :]
        t0[level(k), :] = carried - e * (carried + gw)
        y0[level(k), :] = (carried + gw) * inv[level(k), :]


def interface(position, by_group, statics):
    a = [x[0:NI] for x in by_group]
    top = [x[NI : 2 * NI] for x in by_group]
    kappa, scale, shifted, reach, conduct = statics
    tops = [top[0]]
    for m in range(2):
        tops.append(scale[m] * top[m + 1] + shifted[m] * (tops[m] - a[m + 1]))
    y_above = jnp.zeros((NI, NL), F32)
    xs, ys = [None] * 3, [None] * 3
    for m in (2, 1, 0):
        xs[m] = kappa[m] * (tops[m] - a[m + 1] - (reach[m] * y_above if m < 2 else 0.0))
        ys[m] = tops[m] - conduct[m] * xs[m]
        y_above = ys[m]
    zero = jnp.zeros((NI, NL), F32)
    w_low = jnp.where(position == 0, zero, jnp.where(position == 1, xs[0], jnp.where(position == 2, xs[1], xs[2])))
    p_high = jnp.where(position == 3, zero, jnp.where(position == 2, ys[2], jnp.where(position == 1, ys[1], ys[0])))
    return w_low, p_high


def reduced_statics(by_group):
    beta = [x[2 * NI : 3 * NI] for x in by_group]
    phi = [x[3 * NI : 4 * NI] for x in by_group]
    grounded = [x[4 * NI : 5 * NI] for x in by_group]
    conduct = [grounded[0]]
    kappa, scale, shifted, reach = [], [], [], []
    for m in range(3):
        kappa.append(1.0 / (conduct[m] + beta[m + 1]))
        reach.append(phi[m + 1] / grounded[m + 1])
        if m < 2:
            coupled = phi[m + 1] * kappa[m]
            scale.append(1.0 / (1.0 + coupled * reach[m]))
            shifted.append(coupled * scale[m])
            conduct.append(grounded[m + 1] * scale[m])
    return kappa, scale, shifted, reach, conduct


COUNTS = (3, 2, 2, 3, 3)


def implicit(first, last, *refs):
    (t0, y0, t1, y1, eta, inv, own, by1, by2, by3), refs = refs[:10], refs[10:]
    if not first:
        kept, refs = refs[0], refs[1:]
    if not last:
        (a_w, top_w), refs = refs[:2], refs[2:]
    w, p = refs[:2]
    if not last:
        sums, to_up, to_down, edges = refs[2:6]
    position = lax.axis_index("lev")
    others = [ref[...] for ref in (own, by1, by2, by3)]
    by_group = []
    for group in range(4):
        mask = position ^ group
        by_group.append(
            jnp.where(mask == 0, others[0], jnp.where(mask == 1, others[1], jnp.where(mask == 2, others[2], others[3])))
        )
    if first:
        statics = reduced_statics(by_group)
        keep, at = refs[6], 0
        for family in statics:
            for member in family:
                keep[level(at), :] = member
                at += 1
    else:
        statics, at = [], 0
        for count in COUNTS:
            statics.append([kept[level(at + m), :] for m in range(count)])
            at += count
    w_low, p_high = interface(position, by_group, statics)
    above = p_high
    sum_a = jnp.zeros((NI, NL), F32)
    sum_t = jnp.zeros((NI, NL), F32)
    for k in range(NK - 1, -1, -1):
        wn = y0[level(k), :] + y1[level(k), :] * w_low - inv[level(k), :] * above
        above = t0[level(k), :] + t1[level(k), :] * w_low + eta[level(k), :] * above
        w[level(k), :] = wn
        if last:
            p[level(k), :] = above
        else:
            p[level_ik(k), :] = above
            sum_a = sum_a - a_w[level(k), :] * wn
            sum_t = sum_t + top_w[level(k), :] * wn
    if not last:
        sums[level(0), :] = sum_a
        sums[level(1), :] = sum_t
        to_up[...] = p[pl.ds(14 * NK, 2 * NK), :]
        to_down[...] = p[pl.ds(0, 2 * NK), :]
        pack_edges(p, edges, 0)


def ring(block, axis, distance):
    size = lax.axis_size(axis)
    return lax.ppermute(block, axis, [(i, (i + distance) % size) for i in range(size)])


def partner(block, mask):
    return lax.ppermute(block, "lev", [(i, i ^ mask) for i in range(4)])


def shards(u_wind, v_wind, w_wind, pressure, buoyancy, stiffness):
    u_in, v_in, w, p_in, b_in, s_in = (
        x.reshape(BLOCK) for x in (u_wind, v_wind, w_wind, pressure, buoyancy, stiffness)
    )
    p, u, v, b, to_up, to_down, edges = call(
        prologue,
        [BLOCK] * 4 + [(4 * NK, NL), (4 * NK, NL), (96, NL)],
        [p_in, u_in, v_in, b_in],
        "prologue",
    )
    (s, theta, rest, g, eta, inv, t1, y1, a_p, top_p, a_w, top_w, statics, sums) = call(
        factor, [BLOCK] * 12 + [(3 * NI, NL), (2 * NI, NL)], [b_in, s_in, w], "factor"
    )
    halos0 = kept = u_halo = v_halo = None
    for step in range(SUBSTEPS):
        first, last = step == 0, step == SUBSTEPS - 1
        low, high = ring(to_up, "gx", 1), ring(to_down, "gx", -1)
        left, right = ring(edges, "gy", 1), ring(edges, "gy", -1)
        if first:
            halos0 = [low, high, left, right]
        args = [p, u, v, b, s, a_p, top_p, sums, edges, low, high, left, right] + halos0
        args += [statics] if first else [u_halo, v_halo]
        outs = [BLOCK] * 3 + [((5 if first else 2) * NI, NL)]
        outs += [] if last else [(2 * NK, NL), PACK]
        u, v, p_star, message, *halos = call(
            functools.partial(explicit, first, last), outs, args, f"explicit{step}"
        )
        if not last:
            u_halo, v_halo = halos
        others = [partner(message, mask) for mask in (1, 2, 3)]
        t0, y0 = call(upward, [BLOCK] * 2, [p_star, w, theta, rest, g, eta, inv], f"upward{step}")
        args = [t0, y0, t1, y1, eta, inv, message] + others
        args += [] if first else [kept]
        args += [] if last else [a_w, top_w]
        outs = [BLOCK] * 2
        if not last:
            outs += [(2 * NI, NL), (2 * NK, NL), (2 * NK, NL), PACK]
        if first:
            outs += [(sum(COUNTS) * NI, NL)]
        w, p, *more = call(functools.partial(implicit, first, last), outs, args, f"implicit{step}")
        if not last:
            sums, to_up, to_down, edges, *more = more
        if first:
            kept = more[0]
    return tuple(x.reshape(NK, NI, NL) for x in (u, v, w, p))


def solution(mesh):
    return jax.shard_map(
        shards,
        mesh=mesh,
        in_specs=(P("lev", "gx", "gy"),) * 6,
        out_specs=(P("lev", "gx", "gy"),) * 4,
        check_vma=False,
    )
```

profile of v0, /device:TPU:0, one launch (start us, length us, event | category | flops | bytes accessed | tf_op | source)
XLA Modules:
  0.0 64.2 jit_solution(2252644326246103299)
XLA Ops:
  1.7 1.0 %copy-done.4 = f32[64,16,128]{2,1,0:T(8,128)S(1)} copy-done((f32[64,16,128]{2,1,0:T(8,128)S(1)}, f32[64,16,128]{2,1,0:T(8,128)}, u32[]{:S(2)}) %copy-start.4) | copy-done | bytes 524312
  5.5 3.6 %collective-permute-start.1 = (f32[256,128]{1,0:T(8,128)S(1)}, f32[256,128]{1,0:T(8,128)S(1)}, u32[]{:S(2)}, u32[]{:S(2)}) collective-permute-start(f32[256,128]{1,0:T(8,128)S(1)} %get-tuple-element.72), channel_id=1, source_target_pairs={{0,112},{16,0},{32,16},{48,32},{64,48},{80,64},{96,80},{112,96},{1... | collective-permute-start | bytes 393224 | tf_op jit(solution)/shard_map/ppermute | solution.py:316
  9.1 2.8 %collective-permute-start.3 = (f32[96,128]{1,0:T(8,128)S(1)}, f32[96,128]{1,0:T(8,128)S(1)}, u32[]{:S(2)}, u32[]{:S(2)}) collective-permute-start(f32[96,128]{1,0:T(8,128)S(1)} %get-tuple-element.70.refs_8_), channel_id=1, source_target_pairs={{0,12},{4,0},{8,4},{12,8},{1,13},{5,1},{9,5},{13,9},{2,14},{6,2},{... | collective-permute-start | bytes 147464 | tf_op jit(solution)/shard_map/ppermute | solution.py:316
  11.9 1.8 %factor.1 = (f32[1024,128]{1,0:T(8,128)S(1)}, f32[1024,128]{1,0:T(8,128)S(1)}, f32[1024,128]{1,0:T(8,128)S(1)}, f32[1024,128]{1,0:T(8,128)S(1)}, f32[1024,128]{1...) custom-call(f32[1024,128]{1,0:T(8,128)S(1)} %bitcast.17, ...), custom_call_target="tpu_custom_call" | custom-call | tf_op jit(solution)/shard_map/factor/pallas_call | solution.py:47
  13.7 3.5 %collective-permute-done.2.refs_11_.refs_15_ = f32[96,128]{1,0:T(8,128)S(1)} collective-permute-done((f32[96,128]{1,0:T(8,128)S(1)}, f32[96,128]{1,0:T(8,128)S(1)}, u32[]{:S(2)}, u32[]{:S(2)}) %collective-permute-start.2) | collective-permute-done | bytes 49184 | tf_op jit(solution)/shard_map/ppermute | solution.py:316
  17.2 1.8 %explicit0.1 = (f32[1024,128]{1,0:T(8,128)S(1)}, f32[1024,128]{1,0:T(8,128)S(1)}, f32[1024,128]{1,0:T(8,128)S(1)}, f32[80,128]{1,0:T(8,128)S(1)}, f32[128,128]{1,0:T(8,128)S(1)}, /*index=5*/f32[32,128]{1,0:T(8,128)S(1)}) custom-call(f32[1024,128]{1,0:T(8,128)S(1)} %get-tuple-element.62.refs_0_, f32[1024,128]{1,0:T(8,128)S(1)} %get-tuple-element.63.refs_1_, ...), custom_call_target="tpu_custom_call" | custom-call | tf_op jit(solution)/shard_map/explicit0/pallas_call | solution.py:47
  18.9 3.1 %collective-permute-start.6 = (f32[80,128]{1,0:T(8,128)S(1)}, f32[80,128]{1,0:T(8,128)S(1)}, u32[]{:S(2)}, u32[]{:S(2)}) collective-permute-start(f32[80,128]{1,0:T(8,128)S(1)} %get-tuple-element.84.refs_6_), channel_id=1, source_target_pairs={{0,3},{1,2},{2,1},{3,0},{4,7},{5,6},{6,5},{7,4},{8,11},{9,10},{10,... | collective-permute-start | bytes 122888 | tf_op jit(solution)/shard_map/ppermute | solution.py:320
  24.2 3.3 %collective-permute-done.5.refs_8_ = f32[80,128]{1,0:T(8,128)S(1)} collective-permute-done((f32[80,128]{1,0:T(8,128)S(1)}, f32[80,128]{1,0:T(8,128)S(1)}, u32[]{:S(2)}, u32[]{:S(2)}) %collective-permute-start.5) | collective-permute-done | bytes 40992 | tf_op jit(solution)/shard_map/ppermute | solution.py:320
  28.3 2.9 %collective-permute-start.8 = (f32[128,128]{1,0:T(8,128)S(1)}, f32[128,128]{1,0:T(8,128)S(1)}, u32[]{:S(2)}, u32[]{:S(2)}) collective-permute-start(f32[128,128]{1,0:T(8,128)S(1)} %get-tuple-element.93), channel_id=1, source_target_pairs={{0,112},{16,0},{32,16},{48,32},{64,48},{80,64},{96,80},{112,96},{1... | collective-permute-start | bytes 196616 | tf_op jit(solution)/shard_map/ppermute | solution.py:316
  31.2 2.0 %collective-permute-start.9 = (f32[32,128]{1,0:T(8,128)S(1)}, f32[32,128]{1,0:T(8,128)S(1)}, u32[]{:S(2)}, u32[]{:S(2)}) collective-permute-start(f32[32,128]{1,0:T(8,128)S(1)} %get-tuple-element.91.refs_8_), channel_id=1, source_target_pairs={{0,4},{4,8},{8,12},{12,0},{1,5},{5,9},{9,13},{13,1},{2,6},{6,10},{... | collective-permute-start | bytes 49160 | tf_op jit(solution)/shard_map/ppermute | solution.py:316
  33.2 1.7 %collective-permute-done.10.refs_12_ = f32[32,128]{1,0:T(8,128)S(1)} collective-permute-done((f32[32,128]{1,0:T(8,128)S(1)}, f32[32,128]{1,0:T(8,128)S(1)}, u32[]{:S(2)}, u32[]{:S(2)}) %collective-permute-start.10) | collective-permute-done | bytes 16416 | tf_op jit(solution)/shard_map/ppermute | solution.py:316
  35.0 1.2 %collective-permute-done.9.refs_11_ = f32[32,128]{1,0:T(8,128)S(1)} collective-permute-done((f32[32,128]{1,0:T(8,128)S(1)}, f32[32,128]{1,0:T(8,128)S(1)}, u32[]{:S(2)}, u32[]{:S(2)}) %collective-permute-start.9) | collective-permute-done | bytes 16416 | tf_op jit(solution)/shard_map/ppermute | solution.py:316
  36.2 1.8 %explicit1.1 = (f32[1024,128]{1,0:T(8,128)S(1)}, f32[1024,128]{1,0:T(8,128)S(1)}, f32[1024,128]{1,0:T(8,128)S(1)}, f32[32,128]{1,0:T(8,128)S(1)}, f32[128,128]{1,0:T(8,128)S(1)}, /*index=5*/f32[32,128]{1,0:T(8,128)S(1)}) custom-call(f32[1024,128]{1,0:T(8,128)S(1)} %get-tuple-element.87.refs_0_, f32[1024,128]{1,0:T(8,128)S(1)} %get-tuple-element.88.refs_1_, ...), custom_call_target="tpu_custom_call" | custom-call | tf_op jit(solution)/shard_map/explicit1/pallas_call | solution.py:47
  38.0 1.4 %collective-permute-start.13 = (f32[32,128]{1,0:T(8,128)S(1)}, f32[32,128]{1,0:T(8,128)S(1)}, u32[]{:S(2)}, u32[]{:S(2)}) collective-permute-start(f32[32,128]{1,0:T(8,128)S(1)} %get-tuple-element.100.refs_6_), channel_id=1, source_target_pairs={{0,3},{1,2},{2,1},{3,0},{4,7},{5,6},{6,5},{7,4},{8,11},{9,10},{10,... | collective-permute-start | bytes 49160 | tf_op jit(solution)/shard_map/ppermute | solution.py:320
  40.2 1.9 %collective-permute-start.11 = (f32[32,128]{1,0:T(8,128)S(1)}, f32[32,128]{1,0:T(8,128)S(1)}, u32[]{:S(2)}, u32[]{:S(2)}) collective-permute-start(f32[32,128]{1,0:T(8,128)S(1)} %get-tuple-element.100.refs_6_), channel_id=1, source_target_pairs={{0,1},{1,0},{2,3},{3,2},{4,5},{5,4},{6,7},{7,6},{8,9},{9,8},{10,11... | collective-permute-start | bytes 49160 | tf_op jit(solution)/shard_map/ppermute | solution.py:320
  43.0 1.6 %collective-permute-done.12.refs_8_ = f32[32,128]{1,0:T(8,128)S(1)} collective-permute-done((f32[32,128]{1,0:T(8,128)S(1)}, f32[32,128]{1,0:T(8,128)S(1)}, u32[]{:S(2)}, u32[]{:S(2)}) %collective-permute-start.12) | collective-permute-done | bytes 16416 | tf_op jit(solution)/shard_map/ppermute | solution.py:320
  45.3 2.9 %collective-permute-start.15 = (f32[128,128]{1,0:T(8,128)S(1)}, f32[128,128]{1,0:T(8,128)S(1)}, u32[]{:S(2)}, u32[]{:S(2)}) collective-permute-start(f32[128,128]{1,0:T(8,128)S(1)} %get-tuple-element.108), channel_id=1, source_target_pairs={{0,112},{16,0},{32,16},{48,32},{64,48},{80,64},{96,80},{112,96},{1... | collective-permute-start | bytes 196616 | tf_op jit(solution)/shard_map/ppermute | solution.py:316
  48.2 2.0 %collective-permute-start.16 = (f32[32,128]{1,0:T(8,128)S(1)}, f32[32,128]{1,0:T(8,128)S(1)}, u32[]{:S(2)}, u32[]{:S(2)}) collective-permute-start(f32[32,128]{1,0:T(8,128)S(1)} %get-tuple-element.106.refs_8_), channel_id=1, source_target_pairs={{0,4},{4,8},{8,12},{12,0},{1,5},{5,9},{9,13},{13,1},{2,6},{6,10},{... | collective-permute-start | bytes 49160 | tf_op jit(solution)/shard_map/ppermute | solution.py:316
  50.3 1.7 %collective-permute-done.17.refs_12_ = f32[32,128]{1,0:T(8,128)S(1)} collective-permute-done((f32[32,128]{1,0:T(8,128)S(1)}, f32[32,128]{1,0:T(8,128)S(1)}, u32[]{:S(2)}, u32[]{:S(2)}) %collective-permute-start.17) | collective-permute-done | bytes 16416 | tf_op jit(solution)/shard_map/ppermute | solution.py:316
  52.0 1.2 %collective-permute-done.16.refs_11_ = f32[32,128]{1,0:T(8,128)S(1)} collective-permute-done((f32[32,128]{1,0:T(8,128)S(1)}, f32[32,128]{1,0:T(8,128)S(1)}, u32[]{:S(2)}, u32[]{:S(2)}) %collective-permute-start.16) | collective-permute-done | bytes 16416 | tf_op jit(solution)/shard_map/ppermute | solution.py:316
  53.2 1.9 %explicit2.1 = (f32[1024,128]{1,0:T(8,128)S(1)}, f32[1024,128]{1,0:T(8,128)S(1)}, f32[1024,128]{1,0:T(8,128)S(1)}, f32[32,128]{1,0:T(8,128)S(1)}) custom-call(f32[1024,128]{1,0:T(8,128)S(1)} %get-tuple-element.102.refs_0_, f32[1024,128]{1,0:T(8,128)S(1)} %get-tuple-element.103.refs_1_, f32[1024,128]{1,0:T(8,128)S(1)} %get-tuple-element.104.refs_2_, ...), custom_call_target="tpu_custom_call" | custom-call | tf_op jit(solution)/shard_map/explicit2/pallas_call | solution.py:47
  55.1 2.0 %collective-permute-start.20 = (f32[32,128]{1,0:T(8,128)S(1)}, f32[32,128]{1,0:T(8,128)S(1)}, u32[]{:S(2)}, u32[]{:S(2)}) collective-permute-start(f32[32,128]{1,0:T(8,128)S(1)} %get-tuple-element.117.refs_6_), channel_id=1, source_target_pairs={{0,3},{1,2},{2,1},{3,0},{4,7},{5,6},{6,5},{7,4},{8,11},{9,10},{10,... | collective-permute-start | bytes 49160 | tf_op jit(solution)/shard_map/ppermute | solution.py:320
  57.1 1.4 %collective-permute-start.19 = (f32[32,128]{1,0:T(8,128)S(1)}, f32[32,128]{1,0:T(8,128)S(1)}, u32[]{:S(2)}, u32[]{:S(2)}) collective-permute-start(f32[32,128]{1,0:T(8,128)S(1)} %get-tuple-element.117.refs_6_), channel_id=1, source_target_pairs={{0,2},{1,3},{2,0},{3,1},{4,6},{5,7},{6,4},{7,5},{8,10},{9,11},{10,... | collective-permute-start | bytes 49160 | tf_op jit(solution)/shard_map/ppermute | solution.py:320
  61.1 1.3 %collective-permute-done.19.refs_8_ = f32[32,128]{1,0:T(8,128)S(1)} collective-permute-done((f32[32,128]{1,0:T(8,128)S(1)}, f32[32,128]{1,0:T(8,128)S(1)}, u32[]{:S(2)}, u32[]{:S(2)}) %collective-permute-start.19) | collective-permute-done | bytes 16416 | tf_op jit(solution)/shard_map/ppermute | solution.py:320
  (47 shorter events, 13.6 us)
Async XLA Ops:
  4.8 7.1 %copy-start = (f32[64,16,128]{2,1,0:T(8,128)S(1)}, f32[64,16,128]{2,1,0:T(8,128)}, u32[]{:S(2)}) copy-start(f32[64,16,128]{2,1,0:T(8,128)} %param.8) | copy-start | bytes 1572868
  4.8 7.1 %copy-start.2 = (f32[64,16,128]{2,1,0:T(8,128)S(1)}, f32[64,16,128]{2,1,0:T(8,128)}, u32[]{:S(2)}) copy-start(f32[64,16,128]{2,1,0:T(8,128)} %param.10) | copy-start | bytes 1572868
  4.8 7.1 %copy-start.3 = (f32[64,16,128]{2,1,0:T(8,128)S(1)}, f32[64,16,128]{2,1,0:T(8,128)}, u32[]{:S(2)}) copy-start(f32[64,16,128]{2,1,0:T(8,128)} %param.11) | copy-start | bytes 1572868
  5.5 11.7 %collective-permute-start = (f32[256,128]{1,0:T(8,128)S(1)}, f32[256,128]{1,0:T(8,128)S(1)}, u32[]{:S(2)}, u32[]{:S(2)}) collective-permute-start(f32[256,128]{1,0:T(8,128)S(1)} %get-tuple-element.71), channel_id=1, source_target_pairs={{0,16},{16,32},{32,48},{48,64},{64,80},{80,96},{96,112},{112,0},{1... | collective-permute-start | bytes 393224 | tf_op jit(solution)/shard_map/ppermute | solution.py:316
  5.5 11.7 %collective-permute-start.1 = (f32[256,128]{1,0:T(8,128)S(1)}, f32[256,128]{1,0:T(8,128)S(1)}, u32[]{:S(2)}, u32[]{:S(2)}) collective-permute-start(f32[256,128]{1,0:T(8,128)S(1)} %get-tuple-element.72), channel_id=1, source_target_pairs={{0,112},{16,0},{32,16},{48,32},{64,48},{80,64},{96,80},{112,96},{1... | collective-permute-start | bytes 393224 | tf_op jit(solution)/shard_map/ppermute | solution.py:316
  9.1 4.6 %collective-permute-start.3 = (f32[96,128]{1,0:T(8,128)S(1)}, f32[96,128]{1,0:T(8,128)S(1)}, u32[]{:S(2)}, u32[]{:S(2)}) collective-permute-start(f32[96,128]{1,0:T(8,128)S(1)} %get-tuple-element.70.refs_8_), channel_id=1, source_target_pairs={{0,12},{4,0},{8,4},{12,8},{1,13},{5,1},{9,5},{13,9},{2,14},{6,2},{... | collective-permute-start | bytes 147464 | tf_op jit(solution)/shard_map/ppermute | solution.py:316
  11.9 5.3 %collective-permute-start.2 = (f32[96,128]{1,0:T(8,128)S(1)}, f32[96,128]{1,0:T(8,128)S(1)}, u32[]{:S(2)}, u32[]{:S(2)}) collective-permute-start(f32[96,128]{1,0:T(8,128)S(1)} %get-tuple-element.70.refs_8_), channel_id=1, source_target_pairs={{0,4},{4,8},{8,12},{12,0},{1,5},{5,9},{9,13},{13,1},{2,6},{6,10},{... | collective-permute-start | bytes 147464 | tf_op jit(solution)/shard_map/ppermute | solution.py:316
  18.9 5.3 %collective-permute-start.6 = (f32[80,128]{1,0:T(8,128)S(1)}, f32[80,128]{1,0:T(8,128)S(1)}, u32[]{:S(2)}, u32[]{:S(2)}) collective-permute-start(f32[80,128]{1,0:T(8,128)S(1)} %get-tuple-element.84.refs_6_), channel_id=1, source_target_pairs={{0,3},{1,2},{2,1},{3,0},{4,7},{5,6},{6,5},{7,4},{8,11},{9,10},{10,... | collective-permute-start | bytes 122888 | tf_op jit(solution)/shard_map/ppermute | solution.py:320
  22.0 5.5 %collective-permute-start.5 = (f32[80,128]{1,0:T(8,128)S(1)}, f32[80,128]{1,0:T(8,128)S(1)}, u32[]{:S(2)}, u32[]{:S(2)}) collective-permute-start(f32[80,128]{1,0:T(8,128)S(1)} %get-tuple-element.84.refs_6_), channel_id=1, source_target_pairs={{0,2},{1,3},{2,0},{3,1},{4,6},{5,7},{6,4},{7,5},{8,10},{9,11},{10,... | collective-permute-start | bytes 122888 | tf_op jit(solution)/shard_map/ppermute | solution.py:320
  22.7 4.9 %collective-permute-start.4 = (f32[80,128]{1,0:T(8,128)S(1)}, f32[80,128]{1,0:T(8,128)S(1)}, u32[]{:S(2)}, u32[]{:S(2)}) collective-permute-start(f32[80,128]{1,0:T(8,128)S(1)} %get-tuple-element.84.refs_6_), channel_id=1, source_target_pairs={{0,1},{1,0},{2,3},{3,2},{4,5},{5,4},{6,7},{7,6},{8,9},{9,8},{10,11... | collective-permute-start | bytes 122888 | tf_op jit(solution)/shard_map/ppermute | solution.py:320
  28.2 7.9 %collective-permute-start.7 = (f32[128,128]{1,0:T(8,128)S(1)}, f32[128,128]{1,0:T(8,128)S(1)}, u32[]{:S(2)}, u32[]{:S(2)}) collective-permute-start(f32[128,128]{1,0:T(8,128)S(1)} %get-tuple-element.92), channel_id=1, source_target_pairs={{0,16},{16,32},{32,48},{48,64},{64,80},{80,96},{96,112},{112,0},{1... | collective-permute-start | bytes 196616 | tf_op jit(solution)/shard_map/ppermute | solution.py:316
  28.3 7.9 %collective-permute-start.8 = (f32[128,128]{1,0:T(8,128)S(1)}, f32[128,128]{1,0:T(8,128)S(1)}, u32[]{:S(2)}, u32[]{:S(2)}) collective-permute-start(f32[128,128]{1,0:T(8,128)S(1)} %get-tuple-element.93), channel_id=1, source_target_pairs={{0,112},{16,0},{32,16},{48,32},{64,48},{80,64},{96,80},{112,96},{1... | collective-permute-start | bytes 196616 | tf_op jit(solution)/shard_map/ppermute | solution.py:316
  31.2 3.7 %collective-permute-start.10 = (f32[32,128]{1,0:T(8,128)S(1)}, f32[32,128]{1,0:T(8,128)S(1)}, u32[]{:S(2)}, u32[]{:S(2)}) collective-permute-start(f32[32,128]{1,0:T(8,128)S(1)} %get-tuple-element.91.refs_8_), channel_id=1, source_target_pairs={{0,12},{4,0},{8,4},{12,8},{1,13},{5,1},{9,5},{13,9},{2,14},{6,2},{... | collective-permute-start | bytes 49160 | tf_op jit(solution)/shard_map/ppermute | solution.py:316
  31.2 4.9 %collective-permute-start.9 = (f32[32,128]{1,0:T(8,128)S(1)}, f32[32,128]{1,0:T(8,128)S(1)}, u32[]{:S(2)}, u32[]{:S(2)}) collective-permute-start(f32[32,128]{1,0:T(8,128)S(1)} %get-tuple-element.91.refs_8_), channel_id=1, source_target_pairs={{0,4},{4,8},{8,12},{12,0},{1,5},{5,9},{9,13},{13,1},{2,6},{6,10},{... | collective-permute-start | bytes 49160 | tf_op jit(solution)/shard_map/ppermute | solution.py:316
  38.0 5.0 %collective-permute-start.13 = (f32[32,128]{1,0:T(8,128)S(1)}, f32[32,128]{1,0:T(8,128)S(1)}, u32[]{:S(2)}, u32[]{:S(2)}) collective-permute-start(f32[32,128]{1,0:T(8,128)S(1)} %get-tuple-element.100.refs_6_), channel_id=1, source_target_pairs={{0,3},{1,2},{2,1},{3,0},{4,7},{5,6},{6,5},{7,4},{8,11},{9,10},{10,... | collective-permute-start | bytes 49160 | tf_op jit(solution)/shard_map/ppermute | solution.py:320
  39.3 5.2 %collective-permute-start.12 = (f32[32,128]{1,0:T(8,128)S(1)}, f32[32,128]{1,0:T(8,128)S(1)}, u32[]{:S(2)}, u32[]{:S(2)}) collective-permute-start(f32[32,128]{1,0:T(8,128)S(1)} %get-tuple-element.100.refs_6_), channel_id=1, source_target_pairs={{0,2},{1,3},{2,0},{3,1},{4,6},{5,7},{6,4},{7,5},{8,10},{9,11},{10,... | collective-permute-start | bytes 49160 | tf_op jit(solution)/shard_map/ppermute | solution.py:320
  40.2 4.3 %collective-permute-start.11 = (f32[32,128]{1,0:T(8,128)S(1)}, f32[32,128]{1,0:T(8,128)S(1)}, u32[]{:S(2)}, u32[]{:S(2)}) collective-permute-start(f32[32,128]{1,0:T(8,128)S(1)} %get-tuple-element.100.refs_6_), channel_id=1, source_target_pairs={{0,1},{1,0},{2,3},{3,2},{4,5},{5,4},{6,7},{7,6},{8,9},{9,8},{10,11... | collective-permute-start | bytes 49160 | tf_op jit(solution)/shard_map/ppermute | solution.py:320
  45.3 7.9 %collective-permute-start.14 = (f32[128,128]{1,0:T(8,128)S(1)}, f32[128,128]{1,0:T(8,128)S(1)}, u32[]{:S(2)}, u32[]{:S(2)}) collective-permute-start(f32[128,128]{1,0:T(8,128)S(1)} %get-tuple-element.107), channel_id=1, source_target_pairs={{0,16},{16,32},{32,48},{48,64},{64,80},{80,96},{96,112},{112,0},{1... | collective-permute-start | bytes 196616 | tf_op jit(solution)/shard_map/ppermute | solution.py:316
  45.3 7.9 %collective-permute-start.15 = (f32[128,128]{1,0:T(8,128)S(1)}, f32[128,128]{1,0:T(8,128)S(1)}, u32[]{:S(2)}, u32[]{:S(2)}) collective-permute-start(f32[128,128]{1,0:T(8,128)S(1)} %get-tuple-element.108), channel_id=1, source_target_pairs={{0,112},{16,0},{32,16},{48,32},{64,48},{80,64},{96,80},{112,96},{1... | collective-permute-start | bytes 196616 | tf_op jit(solution)/shard_map/ppermute | solution.py:316
  48.2 3.7 %collective-permute-start.17 = (f32[32,128]{1,0:T(8,128)S(1)}, f32[32,128]{1,0:T(8,128)S(1)}, u32[]{:S(2)}, u32[]{:S(2)}) collective-permute-start(f32[32,128]{1,0:T(8,128)S(1)} %get-tuple-element.106.refs_8_), channel_id=1, source_target_pairs={{0,12},{4,0},{8,4},{12,8},{1,13},{5,1},{9,5},{13,9},{2,14},{6,2},{... | collective-permute-start | bytes 49160 | tf_op jit(solution)/shard_map/ppermute | solution.py:316
  48.2 4.9 %collective-permute-start.16 = (f32[32,128]{1,0:T(8,128)S(1)}, f32[32,128]{1,0:T(8,128)S(1)}, u32[]{:S(2)}, u32[]{:S(2)}) collective-permute-start(f32[32,128]{1,0:T(8,128)S(1)} %get-tuple-element.106.refs_8_), channel_id=1, source_target_pairs={{0,4},{4,8},{8,12},{12,0},{1,5},{5,9},{9,13},{13,1},{2,6},{6,10},{... | collective-permute-start | bytes 49160 | tf_op jit(solution)/shard_map/ppermute | solution.py:316
  55.1 6.0 %collective-permute-start.20 = (f32[32,128]{1,0:T(8,128)S(1)}, f32[32,128]{1,0:T(8,128)S(1)}, u32[]{:S(2)}, u32[]{:S(2)}) collective-permute-start(f32[32,128]{1,0:T(8,128)S(1)} %get-tuple-element.117.refs_6_), channel_id=1, source_target_pairs={{0,3},{1,2},{2,1},{3,0},{4,7},{5,6},{6,5},{7,4},{8,11},{9,10},{10,... | collective-permute-start | bytes 49160 | tf_op jit(solution)/shard_map/ppermute | solution.py:320
  57.1 5.2 %collective-permute-start.19 = (f32[32,128]{1,0:T(8,128)S(1)}, f32[32,128]{1,0:T(8,128)S(1)}, u32[]{:S(2)}, u32[]{:S(2)}) collective-permute-start(f32[32,128]{1,0:T(8,128)S(1)} %get-tuple-element.117.refs_6_), channel_id=1, source_target_pairs={{0,2},{1,3},{2,0},{3,1},{4,6},{5,7},{6,4},{7,5},{8,10},{9,11},{10,... | collective-permute-start | bytes 49160 | tf_op jit(solution)/shard_map/ppermute | solution.py:320
  58.5 3.8 %collective-permute-start.18 = (f32[32,128]{1,0:T(8,128)S(1)}, f32[32,128]{1,0:T(8,128)S(1)}, u32[]{:S(2)}, u32[]{:S(2)}) collective-permute-start(f32[32,128]{1,0:T(8,128)S(1)} %get-tuple-element.117.refs_6_), channel_id=1, source_target_pairs={{0,1},{1,0},{2,3},{3,2},{4,5},{5,4},{6,7},{7,6},{8,9},{9,8},{10,11... | collective-permute-start | bytes 49160 | tf_op jit(solution)/shard_map/ppermute | solution.py:320
  (4 other events, 4.2 us)
where the time goes:
time: 64.5 us; the launch traced here: 64.2 us
  starting transfers between devices  28.9 us (45%)
  waiting for transfers between devices  16.8 us (26%)
  Pallas kernels  10.3 us (16%)
  local copies, waits for them, and re-layouts  7.34 us (11%)
  between operations  0.76 us (1%)
    ppermute x12, starting transfers between devices, ring(): lax.ppermute(block, axis, [(i, (i + distance) % size) for i in range(size)])  16.4 us
    ppermute x9, starting transfers between devices, partner(): return lax.ppermute(block, 'lev', [(i, i ^ mask) for i in range(4)])  12.5 us
    pallas_call x11, Pallas kernels, call(): pl.pallas_call(body, out_shape=tuple((vmem(*shape) for shape in outs)), i...  10.3 us
    ppermute x12, waiting for transfers between devices, ring(): lax.ppermute(block, axis, [(i, (i + distance) % size) for i in range(size)])  9.34 us
    ppermute x9, waiting for transfers between devices, partner(): return lax.ppermute(block, 'lev', [(i, i ^ mask) for i in range(4)])  7.5 us
    unnamed x18, local copies, waits for them, and re-layouts  7.34 us
  transfers between devices with their start and end apart: 21, of which 10 were waited for; matrix products, arithmetic and copies ran while one was open for 2% of the time, Pallas kernels for 4%

commit v1 on v0

v1 whole, which is shorter than its diff:
```python
import functools

import jax
import jax.numpy as jnp
from jax import lax
from jax.experimental import pallas as pl
from jax.experimental.pallas import tpu as pltpu
from jax.sharding import PartitionSpec as P

SUBSTEPS = 3

courant_h = 0.3
vertical_gain = 4096.0

F32 = jnp.float32
NI, NK, NL = 16, 64, 128

STEP = 24
PADDED = ((NK + 1) * STEP, NL)
BLOCK = (NI * NK, NL)
PACK = (4 * 8, NL)


def level(k):
    return pl.ds(NI * k, NI)


def row(i):
    return pl.ds(NK * i, NK)


def padded_row(i):
    return pl.ds(8 + i, NK, stride=STEP)


def vmem(*shape):
    return pltpu.VMEM(shape, F32)


def hbm(*shape):
    return pltpu.HBM(shape, F32)


def call(body, outs, args, name, scratch=(), aliases=None, far_in=0, far_out=0, limit=2):
    near, far = pl.BlockSpec(memory_space=pltpu.VMEM), pl.BlockSpec(memory_space=pltpu.HBM)
    args = [
        pltpu.with_memory_space_constraint(x, pltpu.HBM if at < far_in else pltpu.VMEM) for at, x in enumerate(args)
    ]
    return pl.pallas_call(
        body,
        out_shape=tuple((hbm if at < far_out else vmem)(*shape) for at, shape in enumerate(outs)),
        in_specs=[far] * far_in + [near] * (len(args) - far_in),
        out_specs=(far,) * far_out + (near,) * (len(outs) - far_out),
        scratch_shapes=list(scratch),
        input_output_aliases=aliases or {},
        name=name,
        compiler_params=pltpu.CompilerParams(vmem_limit_bytes=limit << 20),
    )(*args)


def tiles():
    for group in range(4):
        for tile in range(32):
            yield group, tile, group * 16 + tile // 2, 8 * (tile % 2)


def pack_edges(load):
    lane = lax.broadcasted_iota(jnp.int32, (8, NL), 1) // 4
    packs = [jnp.zeros((8, NL), F32)] * 4
    for group, tile, k, i in tiles():
        rolled = pltpu.roll(load(k, i), 4 * tile + 2, 1)
        packs[group] = jnp.where(lane == tile, rolled, packs[group])
    return jnp.concatenate(packs, 0)


def slots(shape=PACK):
    return lax.broadcasted_iota(jnp.int32, shape, 1) % 4


def turn(x, by):
    return pltpu.roll(x, by % NL, 1)


def block_row(i):
    return pl.ds(i, NK, stride=NI)


def prologue(p_in, v_in, b_in, u_in, p, v, b, u, to_up, to_down, to_right, to_left, sems):
    copies = []
    for at, (source, target) in enumerate(((p_in, p), (v_in, v), (b_in, b), (u_in, u))):
        copies.append(pltpu.make_async_copy(source, target, sems.at[at]))
    for copy in copies:
        copy.start()
    packs = []
    for copy, field in zip(copies, (p, v, b)):
        copy.wait()
        packs.append(pack_edges(lambda k, i: field[pl.ds(NI * k + i, 8), :]))
    edge_p, edge_v, edge_b = packs
    slot = slots()
    to_right[...] = jnp.where(slot < 2, edge_p, jnp.where(slot == 2, turn(edge_v, 1), turn(edge_b, 2)))
    to_left[...] = jnp.where(slot < 2, turn(edge_p, -2), jnp.where(slot == 2, edge_v, turn(edge_b, 1)))
    copies[3].wait()
    for at, (field, i) in enumerate(((p, 14), (p, 15), (u, 15), (b, 15))):
        to_up[row(at), :] = field[block_row(i), :]
    for at, (field, i) in enumerate(((p, 0), (p, 1), (u, 0), (b, 0))):
        to_down[row(at), :] = field[block_row(i), :]


def factor(
    s_in, w_in, b_in, v_in,
    theta, rest, g_out, eta, inv, t1, y1, a_p, top_p, a_w, top_w, v, b_v, statics, sums,
):
    first = s_in[level(0), :]
    passed = first
    held = None
    for k in range(NK):
        v[level(k), :] = turn(v_in[level(k), :], -1)
        b_v[level(k), :] = turn(b_in[level(k), :], -1)
        g = 1.0 / (vertical_gain * b_in[level(k), :])
        g_out[level(k), :] = g
        stiff = s_in[level(k), :]
        if k == 0:
            c = first
        else:
            ratio = 1.0 / (held + stiff)
            th = held * ratio
            rs = stiff * ratio
            theta[level(k), :] = th
            rest[level(k), :] = rs
            c = stiff * th
            passed = passed * rs
        held = g + c
        ic = 1.0 / held
        inv[level(k), :] = ic
        eta[level(k), :] = c * ic
        t1[level(k), :] = (g * ic) * passed
        y1[level(k), :] = passed * ic
    theta[level(0), :] = jnp.ones((NI, NL), F32)
    rest[level(0), :] = jnp.zeros((NI, NL), F32)
    statics[level(1), :] = passed
    statics[level(2), :] = held
    weight = jnp.ones((NI, NL), F32)
    above = jnp.zeros((NI, NL), F32)
    reply_above = None
    sum_a = jnp.zeros((NI, NL), F32)
    sum_t = jnp.zeros((NI, NL), F32)
    for k in range(NK - 1, -1, -1):
        g = g_out[level(k), :]
        w = w_in[level(k), :]
        top_p[level(k), :] = theta[level(k), :] * weight
        gw = g * weight
        top_w[level(k), :] = gw
        sum_t = sum_t + gw * w
        weight = weight * rest[level(k), :]
        reply = y1[level(k), :] - inv[level(k), :] * above
        above = t1[level(k), :] + eta[level(k), :] * above
        gr = g * reply
        a_w[level(k), :] = gr
        sum_a = sum_a - gr * w
        if reply_above is not None:
            a_p[level(k + 1), :] = reply - reply_above
        reply_above = reply
    a_p[level(0), :] = 1.0 - reply_above
    statics[level(0), :] = above
    sums[level(0), :] = sum_a
    sums[level(1), :] = sum_t


BATCH = 8


def explicit(first, last, *refs):
    (p, u, v, b_u, b_v, s, a_p, top_p, sums, own, low, high, left, right, low0, high0, extra), refs = refs[:17], refs[17:]
    if not first:
        u_sides, refs = refs[0], refs[1:]
    (u_out, v_out, p_star, message), refs = refs[:4], refs[4:]
    if first:
        b_patched, refs = refs[0], refs[1:]
    if not last:
        (side, u_side), refs = refs[:2], refs[2:]
    p_pad, u_pad = refs
    for k in range(NK):
        p_pad[pl.ds(STEP * k + 8, NI), :] = p[level(k), :]
    for i, (source, at) in ((-2, (low, 0)), (-1, (low, 1)), (NI, (high, 0)), (NI + 1, (high, 1))):
        p_pad[padded_row(i), :] = source[row(at), :]
    for n, (i, source, old) in enumerate(((-1, low, low0), (NI, high, high0))):
        held = old[row(2), :] if first else u_sides[row(n), :]
        away = 1 if n == 0 else -1
        gap = away * (p[block_row(0 if n == 0 else NI - 1), :] - source[row(0 if n == 0 else 1), :])
        held = held - courant_h * old[row(3), :] * gap
        u_pad[padded_row(i), :] = held
        if not last:
            u_side[row(n), :] = held
    slot = slots()
    from_left = turn(left[...], 2)
    if first:
        mine = own[...]
        edge = turn(mine, 2)
        v_side = jnp.where(slot == 2, left[...], turn(mine, 1))
        b_side = jnp.where(slot == 2, turn(left[...], -1), mine)
        from_right = right[...]
    else:
        edge = own[...]
        v_side, b_side = extra[pl.ds(0, 32), :], extra[pl.ds(32, 32), :]
        from_right = turn(right[...], -2)
    v_side = v_side - courant_h * b_side * (edge - from_left)
    packed = jnp.where(slot < 2, from_right, v_side)
    if not last:
        side[pl.ds(0, 32), :] = v_side
        side[pl.ds(32, 32), :] = b_side
    for k in range(NK):
        at = STEP * k + 8
        fresh = u[level(k), :] - courant_h * b_u[level(k), :] * (p_pad[pl.ds(at + 1, NI), :] - p_pad[pl.ds(at - 1, NI), :])
        u_pad[pl.ds(at, NI), :] = fresh
        u_out[level(k), :] = fresh
    size = NI * BATCH
    lane = lax.broadcasted_iota(jnp.int32, (size, NL), 1)

    def spread(source, by):
        return jnp.concatenate([turn(source, by - 4 * tile) for tile in spots], 0)

    total_a, total_t = sums[level(0), :], sums[level(1), :]
    for start in range(0, NK, BATCH):
        rows = pl.ds(NI * start, size)
        spots = range(2 * (start % 16), 2 * (start % 16) + 2 * BATCH)
        group = slice(8 * (start // 16), 8 * (start // 16) + 8)
        halo = spread(packed[group], -2)
        pressure, vs, bs = p[rows, :], v[rows, :], b_v[rows, :]
        if first:
            theirs = right[group, :]
            vs = jnp.where(lane == NL - 1, spread(theirs, NL - 3), vs)
            bs = jnp.where(lane == NL - 1, spread(theirs, NL - 4), bs)
            b_patched[rows, :] = bs
        p_next = jnp.where(lane >= NL - 2, halo, turn(pressure, -2))
        vn = vs - courant_h * bs * (p_next - pressure)
        dv = vn - jnp.where(lane < 2, halo, turn(vn, 2))
        if last:
            ahead = spread(packed[group], -4)
            v_out[rows, :] = turn(jnp.where(lane == NL - 1, ahead, vn), 1)
        else:
            v_out[rows, :] = vn
        du = jnp.concatenate(
            [
                u_pad[pl.ds(STEP * k + 9, NI), :] - u_pad[pl.ds(STEP * k + 7, NI), :]
                for k in range(start, start + BATCH)
            ],
            0,
        )
        star = pressure - courant_h * s[rows, :] * (du + dv)
        p_star[rows, :] = star
        part_a, part_t = a_p[rows, :] * star, top_p[rows, :] * star
        for k in range(BATCH):
            total_a = total_a + part_a[NI * k : NI * k + NI]
            total_t = total_t + part_t[NI * k : NI * k + NI]
    message[level(0), :] = total_a
    message[level(1), :] = total_t
    if first:
        message[pl.ds(2 * NI, 3 * NI), :] = extra[...]


def upward(last, *refs):
    if last:
        (p_star, w, theta, rest, g_in, eta, inv, u_in, v_in), (u_far, v_far, t0, y0, sems) = refs[:9], refs[9:]
        copies = [pltpu.make_async_copy(*pair, sems.at[at]) for at, pair in enumerate(((u_in, u_far), (v_in, v_far)))]
        for copy in copies:
            copy.start()
    else:
        p_star, w, theta, rest, g_in, eta, inv, t0, y0 = refs
    carried = held_gw = None
    for k in range(NK):
        star = p_star[level(k), :]
        gw = g_in[level(k), :] * w[level(k), :]
        if k == 0:
            carried = star
        else:
            carried = theta[level(k), :] * star + rest[level(k), :] * (carried + held_gw)
        held_gw = gw
        e = eta[level(k), :]
        t0[level(k), :] = carried - e * (carried + gw)
        y0[level(k), :] = (carried + gw) * inv[level(k), :]
    if last:
        for copy in copies:
            copy.wait()


def interface(position, by_group, statics):
    a = [x[0:NI] for x in by_group]
    top = [x[NI : 2 * NI] for x in by_group]
    kappa, scale, shifted, reach, conduct = statics
    tops = [top[0]]
    for m in range(2):
        tops.append(scale[m] * top[m + 1] + shifted[m] * (tops[m] - a[m + 1]))
    y_above = jnp.zeros((NI, NL), F32)
    xs, ys = [None] * 3, [None] * 3
    for m in (2, 1, 0):
        xs[m] = kappa[m] * (tops[m] - a[m + 1] - (reach[m] * y_above if m < 2 else 0.0))
        ys[m] = tops[m] - conduct[m] * xs[m]
        y_above = ys[m]
    zero = jnp.zeros((NI, NL), F32)
    w_low = jnp.where(position == 0, zero, jnp.where(position == 1, xs[0], jnp.where(position == 2, xs[1], xs[2])))
    p_high = jnp.where(position == 3, zero, jnp.where(position == 2, ys[2], jnp.where(position == 1, ys[1], ys[0])))
    return w_low, p_high


def reduced_statics(by_group):
    beta = [x[2 * NI : 3 * NI] for x in by_group]
    phi = [x[3 * NI : 4 * NI] for x in by_group]
    grounded = [x[4 * NI : 5 * NI] for x in by_group]
    conduct = [grounded[0]]
    kappa, scale, shifted, reach = [], [], [], []
    for m in range(3):
        kappa.append(1.0 / (conduct[m] + beta[m + 1]))
        reach.append(phi[m + 1] / grounded[m + 1])
        if m < 2:
            coupled = phi[m + 1] * kappa[m]
            scale.append(1.0 / (1.0 + coupled * reach[m]))
            shifted.append(coupled * scale[m])
            conduct.append(grounded[m + 1] * scale[m])
    return kappa, scale, shifted, reach, conduct


COUNTS = (3, 2, 2, 3, 3)


def implicit(first, last, *refs):
    (t0, y0, t1, y1, eta, inv, own, by1, by2, by3), refs = refs[:10], refs[10:]
    if not first:
        kept, refs = refs[0], refs[1:]
    if last:
        w_far, p_far, w, p, sems = refs
    else:
        (a_w, top_w), (w, p, sums, to_up, to_down, edges), refs = refs[:2], refs[2:8], refs[8:]
    position = lax.axis_index("lev")
    others = [ref[...] for ref in (own, by1, by2, by3)]
    by_group = []
    for group in range(4):
        mask = position ^ group
        by_group.append(
            jnp.where(mask == 0, others[0], jnp.where(mask == 1, others[1], jnp.where(mask == 2, others[2], others[3])))
        )
    if first:
        statics = reduced_statics(by_group)
        keep, at = refs[0], 0
        for family in statics:
            for member in family:
                keep[level(at), :] = member
                at += 1
    else:
        statics, at = [], 0
        for count in COUNTS:
            statics.append([kept[level(at + m), :] for m in range(count)])
            at += count
    w_low, p_high = interface(position, by_group, statics)
    above = p_high
    sum_a = jnp.zeros((NI, NL), F32)
    sum_t = jnp.zeros((NI, NL), F32)
    copies = []
    for k in range(NK - 1, -1, -1):
        wn = y0[level(k), :] + y1[level(k), :] * w_low - inv[level(k), :] * above
        above = t0[level(k), :] + t1[level(k), :] * w_low + eta[level(k), :] * above
        w[level(k), :] = wn
        p[level(k), :] = above
        if last:
            if k % 16 == 0:
                part = pl.ds(NI * k, NI * 16)
                for source, target in ((w, w_far), (p, p_far)):
                    copy = pltpu.make_async_copy(source.at[part, :], target.at[part, :], sems.at[len(copies)])
                    copy.start()
                    copies.append(copy)
        else:
            sum_a = sum_a - a_w[level(k), :] * wn
            sum_t = sum_t + top_w[level(k), :] * wn
    for copy in copies:
        copy.wait()
    if not last:
        sums[level(0), :] = sum_a
        sums[level(1), :] = sum_t
        for at, i in enumerate((14, 15)):
            to_up[row(at), :] = p[block_row(i), :]
        for at, i in enumerate((0, 1)):
            to_down[row(at), :] = p[block_row(i), :]
        edges[...] = pack_edges(lambda k, i: p[pl.ds(NI * k + i, 8), :])


def ring(block, axis, distance):
    size = lax.axis_size(axis)
    return lax.ppermute(block, axis, [(i, (i + distance) % size) for i in range(size)])


def partner(block, mask):
    return lax.ppermute(block, "lev", [(i, i ^ mask) for i in range(4)])


def shards(u_wind, v_wind, w_wind, pressure, buoyancy, stiffness):
    w, s = w_wind.reshape(BLOCK), stiffness.reshape(BLOCK)
    p, v, b, u, to_up, to_down, to_right, own = call(
        prologue,
        [BLOCK] * 4 + [(4 * NK, NL), (4 * NK, NL), PACK, PACK],
        [x.reshape(BLOCK) for x in (pressure, v_wind, buoyancy, u_wind)],
        "prologue",
        scratch=[pltpu.SemaphoreType.DMA((4,))],
        far_in=4,
    )
    to_left = own
    (theta, rest, g, eta, inv, t1, y1, a_p, top_p, a_w, top_w, v, b_v, statics, sums) = call(
        factor, [BLOCK] * 13 + [(3 * NI, NL), (2 * NI, NL)], [s, w, b, v], "factor"
    )
    extra, u_side = [statics], []
    for step in range(SUBSTEPS):
        first, last = step == 0, step == SUBSTEPS - 1
        low, high = ring(to_up, "gx", 1), ring(to_down, "gx", -1)
        left, right = ring(to_right, "gy", 1), ring(to_left, "gy", -1)
        if first:
            gx_first = [low, high]
        outs = [BLOCK] * 3 + [((5 if first else 2) * NI, NL)]
        outs += [BLOCK] if first else []
        outs += [] if last else [(2 * PACK[0], NL), (2 * NK, NL)]
        u, v, p_star, message, *more = call(
            functools.partial(explicit, first, last),
            outs,
            [p, u, v, b, b_v, s, a_p, top_p, sums, own, low, high, left, right] + gx_first + extra + u_side,
            f"explicit{step}",
            scratch=[vmem(*PADDED), vmem(*PADDED)],
            limit=3,
        )
        if first:
            b_v, *more = more
        if not last:
            extra, u_side = more[:1], more[1:]
        others = [partner(message, mask) for mask in (1, 2, 3)]
        args = [p_star, w, theta, rest, g, eta, inv]
        if last:
            u_far, v_far, t0, y0 = call(
                functools.partial(upward, True),
                [BLOCK] * 4,
                args + [u, v],
                f"upward{step}",
                scratch=[pltpu.SemaphoreType.DMA((2,))],
                far_out=2,
            )
        else:
            t0, y0 = call(functools.partial(upward, False), [BLOCK] * 2, args, f"upward{step}")
        args = [t0, y0, t1, y1, eta, inv, message] + others
        args += [] if first else [kept]
        body = functools.partial(implicit, first, last)
        if last:
            w_far, p_far = call(
                body,
                [BLOCK] * 2,
                args,
                f"implicit{step}",
                scratch=[vmem(*BLOCK), vmem(*BLOCK), pltpu.SemaphoreType.DMA((8,))],
                far_out=2,
                limit=3,
            )
        else:
            outs = [BLOCK, BLOCK, (2 * NI, NL), (2 * NK, NL), (2 * NK, NL), PACK]
            outs += [(sum(COUNTS) * NI, NL)] if first else []
            w, p, sums, to_up, to_down, own, *more = call(body, outs, args + [a_w, top_w], f"implicit{step}")
            to_right = to_left = own
            if first:
                kept = more[0]
    return tuple(x.reshape(NK, NI, NL) for x in (u_far, v_far, w_far, p_far))


def solution(mesh):
    return jax.shard_map(
        shards,
        mesh=mesh,
        in_specs=(P("lev", "gx", "gy"),) * 6,
        out_specs=(P("lev", "gx", "gy"),) * 4,
        check_vma=False,
    )
```

time: 64.5 us -> 58.8 us (0.912)
  local copies, waits for them, and re-layouts: 7.34 us -> 0.01 us
  starting transfers between devices: 28.9 us -> 30.3 us
    unnamed x18 -> x4, local copies, waits for them, and re-layouts: 7.34 us -> 0.01 us
    ppermute x12, starting transfers between devices: 16.4 us -> 17.8 us  [ring(): lax.ppermute(block, axis, [(i, (i + distance) % size) for i in range(size)])]
    ppermute x9, waiting for transfers between devices: 7.5 us -> 8.54 us  [partner(): return lax.ppermute(block, 'lev', [(i, i ^ mask) for i in range(4)])]
  transfers between devices with their start and end apart: 21 -> 21, of which waited for: 10 -> 11; matrix products, arithmetic and copies ran while one was open for 2% -> 0% of each run, Pallas kernels for 4% -> 4%
where the time goes in v1:
time: 58.8 us; the launch traced here: 58.6 us
  starting transfers between devices  30.3 us (52%)
  waiting for transfers between devices  17.4 us (30%)
  Pallas kernels  10.2 us (17%)
  between operations  0.77 us (1%)
    ppermute x12, starting transfers between devices, ring(): lax.ppermute(block, axis, [(i, (i + distance) % size) for i in range(size)])  17.8 us
    ppermute x9, starting transfers between devices, partner(): return lax.ppermute(block, 'lev', [(i, i ^ mask) for i in range(4)])  12.5 us
    pallas_call x11, Pallas kernels, call(): pl.pallas_call(body, out_shape=tuple(((hbm if at < far_out else vmem)(*sh...  10.2 us
    ppermute x12, waiting for transfers between devices, ring(): lax.ppermute(block, axis, [(i, (i + distance) % size) for i in range(size)])  8.86 us
    ppermute x9, waiting for transfers between devices, partner(): return lax.ppermute(block, 'lev', [(i, i ^ mask) for i in range(4)])  8.54 us
  transfers between devices with their start and end apart: 21, of which 11 were waited for; matrix products, arithmetic and copies ran while one was open for 0% of the time, Pallas kernels for 4%

profile of v1, /device:TPU:0, one launch (start us, length us, event | category | flops | bytes accessed | tf_op | source)
XLA Modules:
  0.0 58.6 jit_solution(8793020843226085235)
XLA Ops:
  0.7 1.9 %prologue.1 = (f32[1024,128]{1,0:T(8,128)S(1)}, f32[1024,128]{1,0:T(8,128)S(1)}, f32[1024,128]{1,0:T(8,128)S(1)}, f32[1024,128]{1,0:T(8,128)S(1)}, f32[256,128]{...) custom-call(f32[1024,128]{1,0:T(8,128)} %bitcast.16, ...), custom_call_target="tpu_custom_call" | custom-call | tf_op jit(solution)/shard_map/prologue/pallas_call | solution.py:49
  2.6 3.6 %collective-permute-start.1 = (f32[256,128]{1,0:T(8,128)S(1)}, f32[256,128]{1,0:T(8,128)S(1)}, u32[]{:S(2)}, u32[]{:S(2)}) collective-permute-start(f32[256,128]{1,0:T(8,128)S(1)} %get-tuple-element.78), channel_id=1, source_target_pairs={{0,112},{16,0},{32,16},{48,32},{64,48},{80,64},{96,80},{112,96},{1... | collective-permute-start | bytes 393224 | tf_op jit(solution)/shard_map/ppermute | solution.py:387
  6.2 1.5 %collective-permute-start.2 = (f32[32,128]{1,0:T(8,128)S(1)}, f32[32,128]{1,0:T(8,128)S(1)}, u32[]{:S(2)}, u32[]{:S(2)}) collective-permute-start(f32[32,128]{1,0:T(8,128)S(1)} %get-tuple-element.79), channel_id=1, source_target_pairs={{0,4},{4,8},{8,12},{12,0},{1,5},{5,9},{9,13},{13,1},{2,6},{6,10},{... | collective-permute-start | bytes 49160 | tf_op jit(solution)/shard_map/ppermute | solution.py:387
  7.7 1.7 %collective-permute-start.3 = (f32[32,128]{1,0:T(8,128)S(1)}, f32[32,128]{1,0:T(8,128)S(1)}, u32[]{:S(2)}, u32[]{:S(2)}) collective-permute-start(f32[32,128]{1,0:T(8,128)S(1)} %get-tuple-element.76.refs_9_), channel_id=1, source_target_pairs={{0,12},{4,0},{8,4},{12,8},{1,13},{5,1},{9,5},{13,9},{2,14},{6,2},{... | collective-permute-start | bytes 49160 | tf_op jit(solution)/shard_map/ppermute | solution.py:387
  11.5 1.4 %explicit0.1 = (f32[1024,128]{1,0:T(8,128)S(1)}, f32[1024,128]{1,0:T(8,128)S(1)}, f32[1024,128]{1,0:T(8,128)S(1)}, f32[80,128]{1,0:T(8,128)S(1)}, f32[1024,128]{...) custom-call(f32[1024,128]{1,0:T(8,128)S(1)} %get-tuple-element.67.refs_0_, ...), custom_call_target="tpu_custom_call" | custom-call | tf_op jit(solution)/shard_map/explicit0/pallas_call | solution.py:49
  12.8 3.1 %collective-permute-start.6 = (f32[80,128]{1,0:T(8,128)S(1)}, f32[80,128]{1,0:T(8,128)S(1)}, u32[]{:S(2)}, u32[]{:S(2)}) collective-permute-start(f32[80,128]{1,0:T(8,128)S(1)} %get-tuple-element.91.refs_6_), channel_id=1, source_target_pairs={{0,3},{1,2},{2,1},{3,0},{4,7},{5,6},{6,5},{7,4},{8,11},{9,10},{10,... | collective-permute-start | bytes 122888 | tf_op jit(solution)/shard_map/ppermute | solution.py:391
  17.2 1.1 %collective-permute-done.6.refs_9_ = f32[80,128]{1,0:T(8,128)S(1)} collective-permute-done((f32[80,128]{1,0:T(8,128)S(1)}, f32[80,128]{1,0:T(8,128)S(1)}, u32[]{:S(2)}, u32[]{:S(2)}) %collective-permute-start.6) | collective-permute-done | bytes 40992 | tf_op jit(solution)/shard_map/ppermute | solution.py:391
  18.3 3.1 %collective-permute-done.5.refs_8_ = f32[80,128]{1,0:T(8,128)S(1)} collective-permute-done((f32[80,128]{1,0:T(8,128)S(1)}, f32[80,128]{1,0:T(8,128)S(1)}, u32[]{:S(2)}, u32[]{:S(2)}) %collective-permute-start.5) | collective-permute-done | bytes 40992 | tf_op jit(solution)/shard_map/ppermute | solution.py:391
  21.9 2.9 %collective-permute-start.8 = (f32[128,128]{1,0:T(8,128)S(1)}, f32[128,128]{1,0:T(8,128)S(1)}, u32[]{:S(2)}, u32[]{:S(2)}) collective-permute-start(f32[128,128]{1,0:T(8,128)S(1)} %get-tuple-element.101), channel_id=1, source_target_pairs={{0,112},{16,0},{32,16},{48,32},{64,48},{80,64},{96,80},{112,96},{1... | collective-permute-start | bytes 196616 | tf_op jit(solution)/shard_map/ppermute | solution.py:387
  24.9 3.0 %collective-permute-start.10 = (f32[32,128]{1,0:T(8,128)S(1)}, f32[32,128]{1,0:T(8,128)S(1)}, u32[]{:S(2)}, u32[]{:S(2)}) collective-permute-start(f32[32,128]{1,0:T(8,128)S(1)} %get-tuple-element.99.refs_9_), channel_id=1, source_target_pairs={{0,12},{4,0},{8,4},{12,8},{1,13},{5,1},{9,5},{13,9},{2,14},{6,2},{... | collective-permute-start | bytes 49160 | tf_op jit(solution)/shard_map/ppermute | solution.py:387
  27.8 1.4 %collective-permute-done.10.refs_13_ = f32[32,128]{1,0:T(8,128)S(1)} collective-permute-done((f32[32,128]{1,0:T(8,128)S(1)}, f32[32,128]{1,0:T(8,128)S(1)}, u32[]{:S(2)}, u32[]{:S(2)}) %collective-permute-start.10) | collective-permute-done | bytes 16416 | tf_op jit(solution)/shard_map/ppermute | solution.py:387
  29.3 3.5 %collective-permute-done.9.refs_12_ = f32[32,128]{1,0:T(8,128)S(1)} collective-permute-done((f32[32,128]{1,0:T(8,128)S(1)}, f32[32,128]{1,0:T(8,128)S(1)}, u32[]{:S(2)}, u32[]{:S(2)}) %collective-permute-start.9) | collective-permute-done | bytes 16416 | tf_op jit(solution)/shard_map/ppermute | solution.py:387
  33.7 1.4 %collective-permute-start.13 = (f32[32,128]{1,0:T(8,128)S(1)}, f32[32,128]{1,0:T(8,128)S(1)}, u32[]{:S(2)}, u32[]{:S(2)}) collective-permute-start(f32[32,128]{1,0:T(8,128)S(1)} %get-tuple-element.108.refs_6_), channel_id=1, source_target_pairs={{0,3},{1,2},{2,1},{3,0},{4,7},{5,6},{6,5},{7,4},{8,11},{9,10},{10,... | collective-permute-start | bytes 49160 | tf_op jit(solution)/shard_map/ppermute | solution.py:391
  36.0 1.9 %collective-permute-start.11 = (f32[32,128]{1,0:T(8,128)S(1)}, f32[32,128]{1,0:T(8,128)S(1)}, u32[]{:S(2)}, u32[]{:S(2)}) collective-permute-start(f32[32,128]{1,0:T(8,128)S(1)} %get-tuple-element.108.refs_6_), channel_id=1, source_target_pairs={{0,1},{1,0},{2,3},{3,2},{4,5},{5,4},{6,7},{7,6},{8,9},{9,8},{10,11... | collective-permute-start | bytes 49160 | tf_op jit(solution)/shard_map/ppermute | solution.py:391
  38.7 1.6 %collective-permute-done.12.refs_8_ = f32[32,128]{1,0:T(8,128)S(1)} collective-permute-done((f32[32,128]{1,0:T(8,128)S(1)}, f32[32,128]{1,0:T(8,128)S(1)}, u32[]{:S(2)}, u32[]{:S(2)}) %collective-permute-start.12) | collective-permute-done | bytes 16416 | tf_op jit(solution)/shard_map/ppermute | solution.py:391
  40.8 2.9 %collective-permute-start.15 = (f32[128,128]{1,0:T(8,128)S(1)}, f32[128,128]{1,0:T(8,128)S(1)}, u32[]{:S(2)}, u32[]{:S(2)}) collective-permute-start(f32[128,128]{1,0:T(8,128)S(1)} %get-tuple-element.116), channel_id=1, source_target_pairs={{0,112},{16,0},{32,16},{48,32},{64,48},{80,64},{96,80},{112,96},{1... | collective-permute-start | bytes 196616 | tf_op jit(solution)/shard_map/ppermute | solution.py:387
  43.7 2.0 %collective-permute-start.16 = (f32[32,128]{1,0:T(8,128)S(1)}, f32[32,128]{1,0:T(8,128)S(1)}, u32[]{:S(2)}, u32[]{:S(2)}) collective-permute-start(f32[32,128]{1,0:T(8,128)S(1)} %get-tuple-element.114.refs_9_), channel_id=1, source_target_pairs={{0,4},{4,8},{8,12},{12,0},{1,5},{5,9},{9,13},{13,1},{2,6},{6,10},{... | collective-permute-start | bytes 49160 | tf_op jit(solution)/shard_map/ppermute | solution.py:387
  45.8 1.7 %collective-permute-done.17.refs_13_ = f32[32,128]{1,0:T(8,128)S(1)} collective-permute-done((f32[32,128]{1,0:T(8,128)S(1)}, f32[32,128]{1,0:T(8,128)S(1)}, u32[]{:S(2)}, u32[]{:S(2)}) %collective-permute-start.17) | collective-permute-done | bytes 16416 | tf_op jit(solution)/shard_map/ppermute | solution.py:387
  47.5 1.2 %collective-permute-done.16.refs_12_ = f32[32,128]{1,0:T(8,128)S(1)} collective-permute-done((f32[32,128]{1,0:T(8,128)S(1)}, f32[32,128]{1,0:T(8,128)S(1)}, u32[]{:S(2)}, u32[]{:S(2)}) %collective-permute-start.16) | collective-permute-done | bytes 16416 | tf_op jit(solution)/shard_map/ppermute | solution.py:387
  48.7 1.6 %explicit2.1 = (f32[1024,128]{1,0:T(8,128)S(1)}, f32[1024,128]{1,0:T(8,128)S(1)}, f32[1024,128]{1,0:T(8,128)S(1)}, f32[32,128]{1,0:T(8,128)S(1)}) custom-call(f32[1024,128]{1,0:T(8,128)S(1)} %get-tuple-element.110.refs_0_, f32[1024,128]{1,0:T(8,128)S(1)} %get-tuple-element.111.refs_1_, f32[1024,128]{1,0:T(8,128)S(1)} %get-tuple-element.112.refs_2_, ...), custom_call_target="tpu_custom_call" | custom-call | tf_op jit(solution)/shard_map/explicit2/pallas_call | solution.py:49
  50.3 2.0 %collective-permute-start.20 = (f32[32,128]{1,0:T(8,128)S(1)}, f32[32,128]{1,0:T(8,128)S(1)}, u32[]{:S(2)}, u32[]{:S(2)}) collective-permute-start(f32[32,128]{1,0:T(8,128)S(1)} %get-tuple-element.127.refs_6_), channel_id=1, source_target_pairs={{0,3},{1,2},{2,1},{3,0},{4,7},{5,6},{6,5},{7,4},{8,11},{9,10},{10,... | collective-permute-start | bytes 49160 | tf_op jit(solution)/shard_map/ppermute | solution.py:391
  52.3 1.4 %collective-permute-start.19 = (f32[32,128]{1,0:T(8,128)S(1)}, f32[32,128]{1,0:T(8,128)S(1)}, u32[]{:S(2)}, u32[]{:S(2)}) collective-permute-start(f32[32,128]{1,0:T(8,128)S(1)} %get-tuple-element.127.refs_6_), channel_id=1, source_target_pairs={{0,2},{1,3},{2,0},{3,1},{4,6},{5,7},{6,4},{7,5},{8,10},{9,11},{10,... | collective-permute-start | bytes 49160 | tf_op jit(solution)/shard_map/ppermute | solution.py:391
  55.5 2.1 %collective-permute-done.19.refs_8_ = f32[32,128]{1,0:T(8,128)S(1)} collective-permute-done((f32[32,128]{1,0:T(8,128)S(1)}, f32[32,128]{1,0:T(8,128)S(1)}, u32[]{:S(2)}, u32[]{:S(2)}) %collective-permute-start.19) | collective-permute-done | bytes 16416 | tf_op jit(solution)/shard_map/ppermute | solution.py:391
  57.5 1.1 %implicit2.1 = (f32[1024,128]{1,0:T(8,128)}, f32[1024,128]{1,0:T(8,128)}) custom-call(f32[1024,128]{1,0:T(8,128)S(1)} %get-tuple-element.125.refs_0_, f32[1024,128]{1,0:T(8,128)S(1)} %get-tuple-element.126.refs_1_, f32[1024,128]{1,0:T(8,128)S(1)} %get-tuple-element.89.refs_2_, f32[1024,128]{1,0:T(8,128)S(1)} %get-tuple-element.90.refs_3_, ...), custom_call_target="tpu_custom_call" | custom-call | tf_op jit(solution)/shard_map/implicit2/pallas_call | solution.py:49
  (33 shorter events, 8.6 us)
Async XLA Ops:
  0.6 8.8 %copy-start = (f32[64,16,128]{2,1,0:T(8,128)S(1)}, f32[64,16,128]{2,1,0:T(8,128)}, u32[]{:S(2)}) copy-start(f32[64,16,128]{2,1,0:T(8,128)} %param.11) | copy-start | bytes 1572868
  0.6 8.8 %copy-start.1 = (f32[64,16,128]{2,1,0:T(8,128)S(1)}, f32[64,16,128]{2,1,0:T(8,128)}, u32[]{:S(2)}) copy-start(f32[64,16,128]{2,1,0:T(8,128)} %param.8) | copy-start | bytes 1572868
  2.6 8.9 %collective-permute-start = (f32[256,128]{1,0:T(8,128)S(1)}, f32[256,128]{1,0:T(8,128)S(1)}, u32[]{:S(2)}, u32[]{:S(2)}) collective-permute-start(f32[256,128]{1,0:T(8,128)S(1)} %get-tuple-element.77), channel_id=1, source_target_pairs={{0,16},{16,32},{32,48},{48,64},{64,80},{80,96},{96,112},{112,0},{1... | collective-permute-start | bytes 393224 | tf_op jit(solution)/shard_map/ppermute | solution.py:387
  2.6 8.8 %collective-permute-start.1 = (f32[256,128]{1,0:T(8,128)S(1)}, f32[256,128]{1,0:T(8,128)S(1)}, u32[]{:S(2)}, u32[]{:S(2)}) collective-permute-start(f32[256,128]{1,0:T(8,128)S(1)} %get-tuple-element.78), channel_id=1, source_target_pairs={{0,112},{16,0},{32,16},{48,32},{64,48},{80,64},{96,80},{112,96},{1... | collective-permute-start | bytes 393224 | tf_op jit(solution)/shard_map/ppermute | solution.py:387
  6.2 4.9 %collective-permute-start.2 = (f32[32,128]{1,0:T(8,128)S(1)}, f32[32,128]{1,0:T(8,128)S(1)}, u32[]{:S(2)}, u32[]{:S(2)}) collective-permute-start(f32[32,128]{1,0:T(8,128)S(1)} %get-tuple-element.79), channel_id=1, source_target_pairs={{0,4},{4,8},{8,12},{12,0},{1,5},{5,9},{9,13},{13,1},{2,6},{6,10},{... | collective-permute-start | bytes 49160 | tf_op jit(solution)/shard_map/ppermute | solution.py:387
  7.7 3.7 %collective-permute-start.3 = (f32[32,128]{1,0:T(8,128)S(1)}, f32[32,128]{1,0:T(8,128)S(1)}, u32[]{:S(2)}, u32[]{:S(2)}) collective-permute-start(f32[32,128]{1,0:T(8,128)S(1)} %get-tuple-element.76.refs_9_), channel_id=1, source_target_pairs={{0,12},{4,0},{8,4},{12,8},{1,13},{5,1},{9,5},{13,9},{2,14},{6,2},{... | collective-permute-start | bytes 49160 | tf_op jit(solution)/shard_map/ppermute | solution.py:387
  12.8 5.5 %collective-permute-start.6 = (f32[80,128]{1,0:T(8,128)S(1)}, f32[80,128]{1,0:T(8,128)S(1)}, u32[]{:S(2)}, u32[]{:S(2)}) collective-permute-start(f32[80,128]{1,0:T(8,128)S(1)} %get-tuple-element.91.refs_6_), channel_id=1, source_target_pairs={{0,3},{1,2},{2,1},{3,0},{4,7},{5,6},{6,5},{7,4},{8,11},{9,10},{10,... | collective-permute-start | bytes 122888 | tf_op jit(solution)/shard_map/ppermute | solution.py:391
  15.9 5.5 %collective-permute-start.5 = (f32[80,128]{1,0:T(8,128)S(1)}, f32[80,128]{1,0:T(8,128)S(1)}, u32[]{:S(2)}, u32[]{:S(2)}) collective-permute-start(f32[80,128]{1,0:T(8,128)S(1)} %get-tuple-element.91.refs_6_), channel_id=1, source_target_pairs={{0,2},{1,3},{2,0},{3,1},{4,6},{5,7},{6,4},{7,5},{8,10},{9,11},{10,... | collective-permute-start | bytes 122888 | tf_op jit(solution)/shard_map/ppermute | solution.py:391
  16.6 4.9 %collective-permute-start.4 = (f32[80,128]{1,0:T(8,128)S(1)}, f32[80,128]{1,0:T(8,128)S(1)}, u32[]{:S(2)}, u32[]{:S(2)}) collective-permute-start(f32[80,128]{1,0:T(8,128)S(1)} %get-tuple-element.91.refs_6_), channel_id=1, source_target_pairs={{0,1},{1,0},{2,3},{3,2},{4,5},{5,4},{6,7},{7,6},{8,9},{9,8},{10,11... | collective-permute-start | bytes 122888 | tf_op jit(solution)/shard_map/ppermute | solution.py:391
  21.9 10.9 %collective-permute-start.7 = (f32[128,128]{1,0:T(8,128)S(1)}, f32[128,128]{1,0:T(8,128)S(1)}, u32[]{:S(2)}, u32[]{:S(2)}) collective-permute-start(f32[128,128]{1,0:T(8,128)S(1)} %get-tuple-element.100), channel_id=1, source_target_pairs={{0,16},{16,32},{32,48},{48,64},{64,80},{80,96},{96,112},{112,0},{1... | collective-permute-start | bytes 196616 | tf_op jit(solution)/shard_map/ppermute | solution.py:387
  21.9 10.9 %collective-permute-start.8 = (f32[128,128]{1,0:T(8,128)S(1)}, f32[128,128]{1,0:T(8,128)S(1)}, u32[]{:S(2)}, u32[]{:S(2)}) collective-permute-start(f32[128,128]{1,0:T(8,128)S(1)} %get-tuple-element.101), channel_id=1, source_target_pairs={{0,112},{16,0},{32,16},{48,32},{64,48},{80,64},{96,80},{112,96},{1... | collective-permute-start | bytes 196616 | tf_op jit(solution)/shard_map/ppermute | solution.py:387
  24.9 4.4 %collective-permute-start.10 = (f32[32,128]{1,0:T(8,128)S(1)}, f32[32,128]{1,0:T(8,128)S(1)}, u32[]{:S(2)}, u32[]{:S(2)}) collective-permute-start(f32[32,128]{1,0:T(8,128)S(1)} %get-tuple-element.99.refs_9_), channel_id=1, source_target_pairs={{0,12},{4,0},{8,4},{12,8},{1,13},{5,1},{9,5},{13,9},{2,14},{6,2},{... | collective-permute-start | bytes 49160 | tf_op jit(solution)/shard_map/ppermute | solution.py:387
  27.8 4.9 %collective-permute-start.9 = (f32[32,128]{1,0:T(8,128)S(1)}, f32[32,128]{1,0:T(8,128)S(1)}, u32[]{:S(2)}, u32[]{:S(2)}) collective-permute-start(f32[32,128]{1,0:T(8,128)S(1)} %get-tuple-element.99.refs_9_), channel_id=1, source_target_pairs={{0,4},{4,8},{8,12},{12,0},{1,5},{5,9},{9,13},{13,1},{2,6},{6,10},{... | collective-permute-start | bytes 49160 | tf_op jit(solution)/shard_map/ppermute | solution.py:387
  33.7 5.0 %collective-permute-start.13 = (f32[32,128]{1,0:T(8,128)S(1)}, f32[32,128]{1,0:T(8,128)S(1)}, u32[]{:S(2)}, u32[]{:S(2)}) collective-permute-start(f32[32,128]{1,0:T(8,128)S(1)} %get-tuple-element.108.refs_6_), channel_id=1, source_target_pairs={{0,3},{1,2},{2,1},{3,0},{4,7},{5,6},{6,5},{7,4},{8,11},{9,10},{10,... | collective-permute-start | bytes 49160 | tf_op jit(solution)/shard_map/ppermute | solution.py:391
  35.1 5.2 %collective-permute-start.12 = (f32[32,128]{1,0:T(8,128)S(1)}, f32[32,128]{1,0:T(8,128)S(1)}, u32[]{:S(2)}, u32[]{:S(2)}) collective-permute-start(f32[32,128]{1,0:T(8,128)S(1)} %get-tuple-element.108.refs_6_), channel_id=1, source_target_pairs={{0,2},{1,3},{2,0},{3,1},{4,6},{5,7},{6,4},{7,5},{8,10},{9,11},{10,... | collective-permute-start | bytes 49160 | tf_op jit(solution)/shard_map/ppermute | solution.py:391
  36.0 4.3 %collective-permute-start.11 = (f32[32,128]{1,0:T(8,128)S(1)}, f32[32,128]{1,0:T(8,128)S(1)}, u32[]{:S(2)}, u32[]{:S(2)}) collective-permute-start(f32[32,128]{1,0:T(8,128)S(1)} %get-tuple-element.108.refs_6_), channel_id=1, source_target_pairs={{0,1},{1,0},{2,3},{3,2},{4,5},{5,4},{6,7},{7,6},{8,9},{9,8},{10,11... | collective-permute-start | bytes 49160 | tf_op jit(solution)/shard_map/ppermute | solution.py:391
  40.8 7.9 %collective-permute-start.14 = (f32[128,128]{1,0:T(8,128)S(1)}, f32[128,128]{1,0:T(8,128)S(1)}, u32[]{:S(2)}, u32[]{:S(2)}) collective-permute-start(f32[128,128]{1,0:T(8,128)S(1)} %get-tuple-element.115), channel_id=1, source_target_pairs={{0,16},{16,32},{32,48},{48,64},{64,80},{80,96},{96,112},{112,0},{1... | collective-permute-start | bytes 196616 | tf_op jit(solution)/shard_map/ppermute | solution.py:387
  40.8 7.9 %collective-permute-start.15 = (f32[128,128]{1,0:T(8,128)S(1)}, f32[128,128]{1,0:T(8,128)S(1)}, u32[]{:S(2)}, u32[]{:S(2)}) collective-permute-start(f32[128,128]{1,0:T(8,128)S(1)} %get-tuple-element.116), channel_id=1, source_target_pairs={{0,112},{16,0},{32,16},{48,32},{64,48},{80,64},{96,80},{112,96},{1... | collective-permute-start | bytes 196616 | tf_op jit(solution)/shard_map/ppermute | solution.py:387
  43.7 3.7 %collective-permute-start.17 = (f32[32,128]{1,0:T(8,128)S(1)}, f32[32,128]{1,0:T(8,128)S(1)}, u32[]{:S(2)}, u32[]{:S(2)}) collective-permute-start(f32[32,128]{1,0:T(8,128)S(1)} %get-tuple-element.114.refs_9_), channel_id=1, source_target_pairs={{0,12},{4,0},{8,4},{12,8},{1,13},{5,1},{9,5},{13,9},{2,14},{6,2},{... | collective-permute-start | bytes 49160 | tf_op jit(solution)/shard_map/ppermute | solution.py:387
  43.7 4.9 %collective-permute-start.16 = (f32[32,128]{1,0:T(8,128)S(1)}, f32[32,128]{1,0:T(8,128)S(1)}, u32[]{:S(2)}, u32[]{:S(2)}) collective-permute-start(f32[32,128]{1,0:T(8,128)S(1)} %get-tuple-element.114.refs_9_), channel_id=1, source_target_pairs={{0,4},{4,8},{8,12},{12,0},{1,5},{5,9},{9,13},{13,1},{2,6},{6,10},{... | collective-permute-start | bytes 49160 | tf_op jit(solution)/shard_map/ppermute | solution.py:387
  50.3 5.2 %collective-permute-start.20 = (f32[32,128]{1,0:T(8,128)S(1)}, f32[32,128]{1,0:T(8,128)S(1)}, u32[]{:S(2)}, u32[]{:S(2)}) collective-permute-start(f32[32,128]{1,0:T(8,128)S(1)} %get-tuple-element.127.refs_6_), channel_id=1, source_target_pairs={{0,3},{1,2},{2,1},{3,0},{4,7},{5,6},{6,5},{7,4},{8,11},{9,10},{10,... | collective-permute-start | bytes 49160 | tf_op jit(solution)/shard_map/ppermute | solution.py:391
  52.3 5.2 %collective-permute-start.19 = (f32[32,128]{1,0:T(8,128)S(1)}, f32[32,128]{1,0:T(8,128)S(1)}, u32[]{:S(2)}, u32[]{:S(2)}) collective-permute-start(f32[32,128]{1,0:T(8,128)S(1)} %get-tuple-element.127.refs_6_), channel_id=1, source_target_pairs={{0,2},{1,3},{2,0},{3,1},{4,6},{5,7},{6,4},{7,5},{8,10},{9,11},{10,... | collective-permute-start | bytes 49160 | tf_op jit(solution)/shard_map/ppermute | solution.py:391
  53.7 3.8 %collective-permute-start.18 = (f32[32,128]{1,0:T(8,128)S(1)}, f32[32,128]{1,0:T(8,128)S(1)}, u32[]{:S(2)}, u32[]{:S(2)}) collective-permute-start(f32[32,128]{1,0:T(8,128)S(1)} %get-tuple-element.127.refs_6_), channel_id=1, source_target_pairs={{0,1},{1,0},{2,3},{3,2},{4,5},{5,4},{6,7},{7,6},{8,9},{9,8},{10,11... | collective-permute-start | bytes 49160 | tf_op jit(solution)/shard_map/ppermute | solution.py:391

commit v2 on v1

--- a/solution.py
+++ b/solution.py
@@ -31,6 +31,10 @@
 
 def padded_row(i):
     return pl.ds(8 + i, NK, stride=STEP)
+
+
+def main_rows(padded):
+    return padded.reshape(NK + 1, STEP, NL).at[pl.ds(0, NK), pl.ds(8, NI), :]
 
 
 def vmem(*shape):
@@ -88,6 +92,8 @@
 def prologue(p_in, v_in, b_in, u_in, p, v, b, u, to_up, to_down, to_right, to_left, sems):
     copies = []
     for at, (source, target) in enumerate(((p_in, p), (v_in, v), (b_in, b), (u_in, u))):
+        if at == 3:
+            target = main_rows(target)
         copies.append(pltpu.make_async_copy(source, target, sems.at[at]))
     for copy in copies:
         copy.start()
@@ -101,9 +107,9 @@
     to_left[...] = jnp.where(slot < 2, turn(edge_p, -2), jnp.where(slot == 2, edge_v, turn(edge_b, 1)))
     copies[3].wait()
     for at, (field, i) in enumerate(((p, 14), (p, 15), (u, 15), (b, 15))):
-        to_up[row(at), :] = field[block_row(i), :]
+        to_up[row(at), :] = field[padded_row(i) if field is u else block_row(i), :]
     for at, (field, i) in enumerate(((p, 0), (p, 1), (u, 0), (b, 0))):
-        to_down[row(at), :] = field[block_row(i), :]
+        to_down[row(at), :] = field[padded_row(i) if field is u else block_row(i), :]
 
 
 def factor(
@@ -167,86 +173,95 @@
 
 
 BATCH = 8
+CHUNK = 8
+
+
+def batches():
+    for start in range(0, NK, BATCH):
+        spots = range(2 * (start % 16), 2 * (start % 16) + 2 * BATCH)
+
+        def spread(pack, by, spots=spots, group=slice(8 * (start // 16), 8 * (start // 16) + 8)):
+            return jnp.concatenate([turn(pack[group, :], by - 4 * tile) for tile in spots], 0)
+
+        yield start, pl.ds(NI * start, NI * BATCH), spread
+
+
+def inner(first, p, u, v, b_u, b_v, s, u_new, v_part, star_part):
+    for k in range(NK):
+        rows = pl.ds(STEP * k + 8, NI)
+        if k == 0:
+            below = jnp.concatenate([p[pl.ds(0, 1), :], p[pl.ds(0, NI - 1), :]], 0)
+        else:
+            below = p[pl.ds(NI * k - 1, NI), :]
+        if k == NK - 1:
+            above = jnp.concatenate([p[pl.ds(NI * k + 1, NI - 1), :], p[pl.ds(NI * k, 1), :]], 0)
+        else:
+            above = p[pl.ds(NI * k + 1, NI), :]
+        u_new[rows, :] = u[rows, :] - courant_h * b_u[level(k), :] * (above - below)
+    lane = lax.broadcasted_iota(jnp.int32, (NI * BATCH, NL), 1)
+    for _, rows, _ in batches():
+        pressure = p[rows, :]
+        p_next = jnp.where(lane >= NL - 2, 0.0, turn(pressure, -2))
+        vn = v[rows, :] - courant_h * b_v[rows, :] * (p_next - pressure)
+        if first:
+            vn = jnp.where(lane == NL - 1, 0.0, vn)
+        v_part[rows, :] = vn
+        star_part[rows, :] = pressure - courant_h * s[rows, :] * (vn - jnp.where(lane < 2, 0.0, turn(vn, 2)))
 
 
 def explicit(first, last, *refs):
-    (p, u, v, b_u, b_v, s, a_p, top_p, sums, own, low, high, left, right, low0, high0, extra), refs = refs[:17], refs[17:]
-    if not first:
+    (p, u_old, b_u, star_part, s, a_p, top_p, sums, own, low, high, left, right, low0, high0, extra), refs = (
+        refs[:16],
+        refs[17:],
+    )
+    if first:
+        own_right, refs = refs[0], refs[1:]
+    else:
         u_sides, refs = refs[0], refs[1:]
-    (u_out, v_out, p_star, message), refs = refs[:4], refs[4:]
-    if first:
-        b_patched, refs = refs[0], refs[1:]
-    if not last:
-        (side, u_side), refs = refs[:2], refs[2:]
-    p_pad, u_pad = refs
-    for k in range(NK):
-        p_pad[pl.ds(STEP * k + 8, NI), :] = p[level(k), :]
-    for i, (source, at) in ((-2, (low, 0)), (-1, (low, 1)), (NI, (high, 0)), (NI + 1, (high, 1))):
-        p_pad[padded_row(i), :] = source[row(at), :]
-    for n, (i, source, old) in enumerate(((-1, low, low0), (NI, high, high0))):
+    u, p_star, message, side = refs[:4]
+    for n, (source, old) in enumerate(((low, low0), (high, high0))):
+        away, edge, second = (1, 0, 1) if n == 0 else (-1, NI - 1, NI - 2)
+        far, near = (0, 1) if n == 0 else (1, 0)
         held = old[row(2), :] if first else u_sides[row(n), :]
-        away = 1 if n == 0 else -1
-        gap = away * (p[block_row(0 if n == 0 else NI - 1), :] - source[row(0 if n == 0 else 1), :])
-        held = held - courant_h * old[row(3), :] * gap
-        u_pad[padded_row(i), :] = held
+        held = held - courant_h * old[row(3), :] * (away * (p[block_row(edge), :] - source[row(far), :]))
+        u[padded_row(edge - away), :] = held
         if not last:
-            u_side[row(n), :] = held
+            refs[4][row(n), :] = held
+        u[padded_row(edge), :] = u_old[padded_row(edge), :] - courant_h * b_u[block_row(edge), :] * (
+            away * (p[block_row(second), :] - source[row(near), :])
+        )
     slot = slots()
     from_left = turn(left[...], 2)
     if first:
-        mine = own[...]
+        mine, from_right = own[...], right[...]
         edge = turn(mine, 2)
         v_side = jnp.where(slot == 2, left[...], turn(mine, 1))
-        b_side = jnp.where(slot == 2, turn(left[...], -1), mine)
-        from_right = right[...]
+        b_pack = jnp.where(slot == 2, turn(left[...], -1), mine)
+        b_edge = jnp.where(slot == 0, turn(own_right[...], -3), turn(from_right, -2))
+        b_pack = jnp.where(slot < 2, b_edge, b_pack)
+        ahead = turn(from_right, -1) - courant_h * b_edge * (from_right - own_right[...])
+        taken = jnp.where(slot == 0, courant_h * b_edge * from_right, -ahead)
     else:
         edge = own[...]
-        v_side, b_side = extra[pl.ds(0, 32), :], extra[pl.ds(32, 32), :]
-        from_right = turn(right[...], -2)
-    v_side = v_side - courant_h * b_side * (edge - from_left)
-    packed = jnp.where(slot < 2, from_right, v_side)
+        v_side, b_pack = extra[pl.ds(0, 32), :], extra[pl.ds(32, 32), :]
+        taken = courant_h * b_pack * turn(right[...], -2)
+    v_side = v_side - courant_h * b_pack * (edge - from_left)
+    packed = jnp.where(slot < 2, taken, v_side)
+    side[pl.ds(0, 32), :] = packed
     if not last:
-        side[pl.ds(0, 32), :] = v_side
-        side[pl.ds(32, 32), :] = b_side
-    for k in range(NK):
-        at = STEP * k + 8
-        fresh = u[level(k), :] - courant_h * b_u[level(k), :] * (p_pad[pl.ds(at + 1, NI), :] - p_pad[pl.ds(at - 1, NI), :])
-        u_pad[pl.ds(at, NI), :] = fresh
-        u_out[level(k), :] = fresh
-    size = NI * BATCH
-    lane = lax.broadcasted_iota(jnp.int32, (size, NL), 1)
-
-    def spread(source, by):
-        return jnp.concatenate([turn(source, by - 4 * tile) for tile in spots], 0)
-
+        side[pl.ds(32, 32), :] = b_pack
+    lane = lax.broadcasted_iota(jnp.int32, (NI * BATCH, NL), 1)
+    at_edge = (lane < 2) | (lane >= NL - 2)
     total_a, total_t = sums[level(0), :], sums[level(1), :]
-    for start in range(0, NK, BATCH):
-        rows = pl.ds(NI * start, size)
-        spots = range(2 * (start % 16), 2 * (start % 16) + 2 * BATCH)
-        group = slice(8 * (start // 16), 8 * (start // 16) + 8)
-        halo = spread(packed[group], -2)
-        pressure, vs, bs = p[rows, :], v[rows, :], b_v[rows, :]
-        if first:
-            theirs = right[group, :]
-            vs = jnp.where(lane == NL - 1, spread(theirs, NL - 3), vs)
-            bs = jnp.where(lane == NL - 1, spread(theirs, NL - 4), bs)
-            b_patched[rows, :] = bs
-        p_next = jnp.where(lane >= NL - 2, halo, turn(pressure, -2))
-        vn = vs - courant_h * bs * (p_next - pressure)
-        dv = vn - jnp.where(lane < 2, halo, turn(vn, 2))
-        if last:
-            ahead = spread(packed[group], -4)
-            v_out[rows, :] = turn(jnp.where(lane == NL - 1, ahead, vn), 1)
-        else:
-            v_out[rows, :] = vn
+    for start, rows, spread in batches():
         du = jnp.concatenate(
             [
-                u_pad[pl.ds(STEP * k + 9, NI), :] - u_pad[pl.ds(STEP * k + 7, NI), :]
+                u[pl.ds(STEP * k + 9, NI), :] - u[pl.ds(STEP * k + 7, NI), :]
                 for k in range(start, start + BATCH)
             ],
             0,
         )
-        star = pressure - courant_h * s[rows, :] * (du + dv)
+        star = star_part[rows, :] - courant_h * s[rows, :] * (du - jnp.where(at_edge, spread(packed, -2), 0.0))
         p_star[rows, :] = star
         part_a, part_t = a_p[rows, :] * star, top_p[rows, :] * star
         for k in range(BATCH):
@@ -258,14 +273,31 @@
         message[pl.ds(2 * NI, 3 * NI), :] = extra[...]
 
 
-def upward(last, *refs):
+def upward(first, last, *refs):
+    (p_star, w, theta, rest, g_in, eta, inv, v_part, side), refs = refs[:9], refs[9:]
+    copies = []
     if last:
-        (p_star, w, theta, rest, g_in, eta, inv, u_in, v_in), (u_far, v_far, t0, y0, sems) = refs[:9], refs[9:]
-        copies = [pltpu.make_async_copy(*pair, sems.at[at]) for at, pair in enumerate(((u_in, u_far), (v_in, v_far)))]
-        for copy in copies:
-            copy.start()
+        u, u_far, v_far, t0, y0, v_out, sems = refs
+
+        def send(source, target):
+            copies.append(pltpu.make_async_copy(source, target, sems.at[len(copies)]))
+            copies[-1].start()
+
+        send(main_rows(u), u_far)
+    elif first:
+        b_v, right, t0, y0, v_out, b_patched = refs
     else:
-        p_star, w, theta, rest, g_in, eta, inv, t0, y0 = refs
+        t0, y0, v_out = refs
+    lane = lax.broadcasted_iota(jnp.int32, (NI * BATCH, NL), 1)
+    for _, rows, spread in batches():
+        vn = v_part[rows, :] - jnp.where(lane >= NL - 2, spread(side, -2), 0.0)
+        if last:
+            vn = turn(jnp.where(lane == NL - 1, spread(side, -4), vn), 1)
+        v_out[rows, :] = vn
+        if last:
+            send(v_out.at[rows, :], v_far.at[rows, :])
+        if first:
+            b_patched[rows, :] = jnp.where(lane == NL - 1, spread(right, NL - 4), b_v[rows, :])
     carried = held_gw = None
     for k in range(NK):
         star = p_star[level(k), :]
@@ -278,9 +310,8 @@
         e = eta[level(k), :]
         t0[level(k), :] = carried - e * (carried + gw)
         y0[level(k), :] = (carried + gw) * inv[level(k), :]
-    if last:
-        for copy in copies:
-            copy.wait()
+    for copy in copies:
+        copy.wait()
 
 
 def interface(position, by_group, statics):
@@ -361,8 +392,8 @@
         w[level(k), :] = wn
         p[level(k), :] = above
         if last:
-            if k % 16 == 0:
-                part = pl.ds(NI * k, NI * 16)
+            if k % CHUNK == 0:
+                part = pl.ds(NI * k, NI * CHUNK)
                 for source, target in ((w, w_far), (p, p_far)):
                     copy = pltpu.make_async_copy(source.at[part, :], target.at[part, :], sems.at[len(copies)])
                     copy.start()
@@ -395,8 +426,8 @@
     w, s = w_wind.reshape(BLOCK), stiffness.reshape(BLOCK)
     p, v, b, u, to_up, to_down, to_right, own = call(
         prologue,
-        [BLOCK] * 4 + [(4 * NK, NL), (4 * NK, NL), PACK, PACK],
-        [x.reshape(BLOCK) for x in (pressure, v_wind, buoyancy, u_wind)],
+        [BLOCK] * 3 + [PADDED, (4 * NK, NL), (4 * NK, NL), PACK, PACK],
+        [x.reshape(BLOCK) for x in (pressure, v_wind, buoyancy)] + [u_wind],
         "prologue",
         scratch=[pltpu.SemaphoreType.DMA((4,))],
         far_in=4,
@@ -405,41 +436,40 @@
     (theta, rest, g, eta, inv, t1, y1, a_p, top_p, a_w, top_w, v, b_v, statics, sums) = call(
         factor, [BLOCK] * 13 + [(3 * NI, NL), (2 * NI, NL)], [s, w, b, v], "factor"
     )
-    extra, u_side = [statics], []
+    side, more = statics, [to_right]
     for step in range(SUBSTEPS):
         first, last = step == 0, step == SUBSTEPS - 1
         low, high = ring(to_up, "gx", 1), ring(to_down, "gx", -1)
         left, right = ring(to_right, "gy", 1), ring(to_left, "gy", -1)
         if first:
             gx_first = [low, high]
-        outs = [BLOCK] * 3 + [((5 if first else 2) * NI, NL)]
-        outs += [BLOCK] if first else []
-        outs += [] if last else [(2 * PACK[0], NL), (2 * NK, NL)]
-        u, v, p_star, message, *more = call(
-            functools.partial(explicit, first, last),
-            outs,
-            [p, u, v, b, b_v, s, a_p, top_p, sums, own, low, high, left, right] + gx_first + extra + u_side,
-            f"explicit{step}",
-            scratch=[vmem(*PADDED), vmem(*PADDED)],
-            limit=3,
+        u_part, v_part, star_part = call(
+            functools.partial(inner, first), [PADDED, BLOCK, BLOCK], [p, u, v, b, b_v, s], f"inner{step}"
         )
-        if first:
-            b_v, *more = more
-        if not last:
-            extra, u_side = more[:1], more[1:]
+        args = [p, u, b, star_part, s, a_p, top_p, sums, own, low, high, left, right] + gx_first + [side, u_part] + more
+        outs = [PADDED, BLOCK, ((5 if first else 2) * NI, NL)]
+        outs += [PACK] if last else [(2 * PACK[0], NL), (2 * NK, NL)]
+        u, p_star, message, side, *more = call(
+            functools.partial(explicit, first, last), outs, args, f"explicit{step}", aliases={16: 0}
+        )
         others = [partner(message, mask) for mask in (1, 2, 3)]
-        args = [p_star, w, theta, rest, g, eta, inv]
+        args = [p_star, w, theta, rest, g, eta, inv, v_part, side]
+        outs = [BLOCK] * 3
         if last:
             u_far, v_far, t0, y0 = call(
-                functools.partial(upward, True),
-                [BLOCK] * 4,
-                args + [u, v],
+                functools.partial(upward, False, True),
+                [(NK, NI, NL)] + outs,
+                args + [u],
                 f"upward{step}",
-                scratch=[pltpu.SemaphoreType.DMA((2,))],
+                scratch=[vmem(*BLOCK), pltpu.SemaphoreType.DMA((1 + NK // BATCH,))],
                 far_out=2,
             )
-        else:
-            t0, y0 = call(functools.partial(upward, False), [BLOCK] * 2, args, f"upward{step}")
+        elif first:
+            t0, y0, v, b_v = call(
+                functools.partial(upward, True, False), outs + [BLOCK], args + [b_v, right], f"upward{step}"
+            )
+        else:
+            t0, y0, v = call(functools.partial(upward, False, False), outs, args, f"upward{step}")
         args = [t0, y0, t1, y1, eta, inv, message] + others
         args += [] if first else [kept]
         body = functools.partial(implicit, first, last)
@@ -449,17 +479,17 @@
                 [BLOCK] * 2,
                 args,
                 f"implicit{step}",
-                scratch=[vmem(*BLOCK), vmem(*BLOCK), pltpu.SemaphoreType.DMA((8,))],
+                scratch=[vmem(*BLOCK), vmem(*BLOCK), pltpu.SemaphoreType.DMA((2 * NK // CHUNK,))],
                 far_out=2,
                 limit=3,
             )
         else:
             outs = [BLOCK, BLOCK, (2 * NI, NL), (2 * NK, NL), (2 * NK, NL), PACK]
             outs += [(sum(COUNTS) * NI, NL)] if first else []
-            w, p, sums, to_up, to_down, own, *more = call(body, outs, args + [a_w, top_w], f"implicit{step}")
+            w, p, sums, to_up, to_down, own, *fixed = call(body, outs, args + [a_w, top_w], f"implicit{step}")
             to_right = to_left = own
             if first:
-                kept = more[0]
+                kept = fixed[0]
     return tuple(x.reshape(NK, NI, NL) for x in (u_far, v_far, w_far, p_far))
 
 

time: 58.8 us -> 56 us (0.952)
  waiting for transfers between devices: 17.4 us -> 15.1 us
  starting transfers between devices: 30.3 us -> 28.9 us
  Pallas kernels: 10.2 us -> 11.1 us
    ppermute x12, starting transfers between devices: 17.8 us -> 16.4 us  [ring(): lax.ppermute(block, axis, [(i, (i + distance) % size) for i in range(size)])]
    ppermute x12, waiting for transfers between devices: 8.86 us -> 7.64 us  [ring(): lax.ppermute(block, axis, [(i, (i + distance) % size) for i in range(size)])]
    ppermute x9, waiting for transfers between devices: 8.54 us -> 7.5 us  [partner(): return lax.ppermute(block, 'lev', [(i, i ^ mask) for i in range(4)])]
    pallas_call x11 -> x14, Pallas kernels: 10.2 us -> 11.1 us  [call(): pl.pallas_call(body, out_shape=tuple(((hbm if at < far_out else vmem)(*sh...]
  transfers between devices with their start and end apart: 21 -> 21, of which waited for: 11 -> 10; matrix products, arithmetic and copies ran while one was open for 0% -> 0% of each run, Pallas kernels for 4% -> 10%
where the time goes in v2:
time: 56 us; the launch traced here: 55.9 us
  starting transfers between devices  28.9 us (52%)
  waiting for transfers between devices  15.1 us (27%)
  Pallas kernels  11.1 us (20%)
  between operations  0.8 us (1%)
    ppermute x12, starting transfers between devices, ring(): lax.ppermute(block, axis, [(i, (i + distance) % size) for i in range(size)])  16.4 us
    ppermute x9, starting transfers between devices, partner(): return lax.ppermute(block, 'lev', [(i, i ^ mask) for i in range(4)])  12.5 us
    pallas_call x14, Pallas kernels, call(): pl.pallas_call(body, out_shape=tuple(((hbm if at < far_out else vmem)(*sh...  11.1 us
    ppermute x12, waiting for transfers between devices, ring(): lax.ppermute(block, axis, [(i, (i + distance) % size) for i in range(size)])  7.64 us
    ppermute x9, waiting for transfers between devices, partner(): return lax.ppermute(block, 'lev', [(i, i ^ mask) for i in range(4)])  7.5 us
  transfers between devices with their start and end apart: 21, of which 10 were waited for; matrix products, arithmetic and copies ran while one was open for 0% of the time, Pallas kernels for 10%

profile of v2, /device:TPU:0, one launch (start us, length us, event | category | flops | bytes accessed | tf_op | source)
XLA Modules:
  0.0 55.9 jit_solution(7065162895197126590)
XLA Ops:
  0.7 1.9 %prologue.1 = (f32[1024,128]{1,0:T(8,128)S(1)}, f32[1024,128]{1,0:T(8,128)S(1)}, f32[1024,128]{1,0:T(8,128)S(1)}, f32[1560,128]{1,0:T(8,128)S(1)}, f32[256,128]{...) custom-call(f32[1024,128]{1,0:T(8,128)} %bitcast.17, ...), custom_call_target="tpu_custom_call" | custom-call | tf_op jit(solution)/shard_map/prologue/pallas_call | solution.py:53
  2.6 3.6 %collective-permute-start.1 = (f32[256,128]{1,0:T(8,128)S(1)}, f32[256,128]{1,0:T(8,128)S(1)}, u32[]{:S(2)}, u32[]{:S(2)}) collective-permute-start(f32[256,128]{1,0:T(8,128)S(1)} %get-tuple-element.88), channel_id=1, source_target_pairs={{0,112},{16,0},{32,16},{48,32},{64,48},{80,64},{96,80},{112,96},{1... | collective-permute-start | bytes 393224 | tf_op jit(solution)/shard_map/ppermute | solution.py:418
  6.2 2.8 %collective-permute-start.3 = (f32[32,128]{1,0:T(8,128)S(1)}, f32[32,128]{1,0:T(8,128)S(1)}, u32[]{:S(2)}, u32[]{:S(2)}) collective-permute-start(f32[32,128]{1,0:T(8,128)S(1)} %get-tuple-element.86.refs_8_), channel_id=1, source_target_pairs={{0,12},{4,0},{8,4},{12,8},{1,13},{5,1},{9,5},{13,9},{2,14},{6,2},{... | collective-permute-start | bytes 49160 | tf_op jit(solution)/shard_map/ppermute | solution.py:418
  9.0 1.0 %factor.1 = (f32[1024,128]{1,0:T(8,128)S(1)}, f32[1024,128]{1,0:T(8,128)S(1)}, f32[1024,128]{1,0:T(8,128)S(1)}, f32[1024,128]{1,0:T(8,128)S(1)}, f32[1024,128]{1...) custom-call(f32[1024,128]{1,0:T(8,128)S(1)} %bitcast.8, ...), custom_call_target="tpu_custom_call" | custom-call | tf_op jit(solution)/shard_map/factor/pallas_call | solution.py:53
  10.8 3.2 %collective-permute-done.2.refs_11_ = f32[32,128]{1,0:T(8,128)S(1)} collective-permute-done((f32[32,128]{1,0:T(8,128)S(1)}, f32[32,128]{1,0:T(8,128)S(1)}, u32[]{:S(2)}, u32[]{:S(2)}) %collective-permute-start.2) | collective-permute-done | bytes 16416 | tf_op jit(solution)/shard_map/ppermute | solution.py:418
  14.4 3.1 %collective-permute-start.6 = (f32[80,128]{1,0:T(8,128)S(1)}, f32[80,128]{1,0:T(8,128)S(1)}, u32[]{:S(2)}, u32[]{:S(2)}) collective-permute-start(f32[80,128]{1,0:T(8,128)S(1)} %get-tuple-element.104.refs_6_), channel_id=1, source_target_pairs={{0,3},{1,2},{2,1},{3,0},{4,7},{5,6},{6,5},{7,4},{8,11},{9,10},{10,... | collective-permute-start | bytes 122888 | tf_op jit(solution)/shard_map/ppermute | solution.py:422
  19.7 3.3 %collective-permute-done.5.refs_8_ = f32[80,128]{1,0:T(8,128)S(1)} collective-permute-done((f32[80,128]{1,0:T(8,128)S(1)}, f32[80,128]{1,0:T(8,128)S(1)}, u32[]{:S(2)}, u32[]{:S(2)}) %collective-permute-start.5) | collective-permute-done | bytes 40992 | tf_op jit(solution)/shard_map/ppermute | solution.py:422
  23.5 2.9 %collective-permute-start.8 = (f32[128,128]{1,0:T(8,128)S(1)}, f32[128,128]{1,0:T(8,128)S(1)}, u32[]{:S(2)}, u32[]{:S(2)}) collective-permute-start(f32[128,128]{1,0:T(8,128)S(1)} %get-tuple-element.115), channel_id=1, source_target_pairs={{0,112},{16,0},{32,16},{48,32},{64,48},{80,64},{96,80},{112,96},{1... | collective-permute-start | bytes 196616 | tf_op jit(solution)/shard_map/ppermute | solution.py:418
  26.6 1.9 %collective-permute-start.9 = (f32[32,128]{1,0:T(8,128)S(1)}, f32[32,128]{1,0:T(8,128)S(1)}, u32[]{:S(2)}, u32[]{:S(2)}) collective-permute-start(f32[32,128]{1,0:T(8,128)S(1)} %get-tuple-element.113.refs_8_), channel_id=1, source_target_pairs={{0,4},{4,8},{8,12},{12,0},{1,5},{5,9},{9,13},{13,1},{2,6},{6,10},{... | collective-permute-start | bytes 49160 | tf_op jit(solution)/shard_map/ppermute | solution.py:418
  29.3 1.0 %collective-permute-done.10.refs_12_ = f32[32,128]{1,0:T(8,128)S(1)} collective-permute-done((f32[32,128]{1,0:T(8,128)S(1)}, f32[32,128]{1,0:T(8,128)S(1)}, u32[]{:S(2)}, u32[]{:S(2)}) %collective-permute-start.10) | collective-permute-done | bytes 16416 | tf_op jit(solution)/shard_map/ppermute | solution.py:418
  30.2 1.3 %collective-permute-done.9.refs_11_ = f32[32,128]{1,0:T(8,128)S(1)} collective-permute-done((f32[32,128]{1,0:T(8,128)S(1)}, f32[32,128]{1,0:T(8,128)S(1)}, u32[]{:S(2)}, u32[]{:S(2)}) %collective-permute-start.9) | collective-permute-done | bytes 16416 | tf_op jit(solution)/shard_map/ppermute | solution.py:418
  32.0 1.4 %collective-permute-start.13 = (f32[32,128]{1,0:T(8,128)S(1)}, f32[32,128]{1,0:T(8,128)S(1)}, u32[]{:S(2)}, u32[]{:S(2)}) collective-permute-start(f32[32,128]{1,0:T(8,128)S(1)} %get-tuple-element.124.refs_6_), channel_id=1, source_target_pairs={{0,3},{1,2},{2,1},{3,0},{4,7},{5,6},{6,5},{7,4},{8,11},{9,10},{10,... | collective-permute-start | bytes 49160 | tf_op jit(solution)/shard_map/ppermute | solution.py:422
  33.4 0.9 %collective-permute-start.12 = (f32[32,128]{1,0:T(8,128)S(1)}, f32[32,128]{1,0:T(8,128)S(1)}, u32[]{:S(2)}, u32[]{:S(2)}) collective-permute-start(f32[32,128]{1,0:T(8,128)S(1)} %get-tuple-element.124.refs_6_), channel_id=1, source_target_pairs={{0,2},{1,3},{2,0},{3,1},{4,6},{5,7},{6,4},{7,5},{8,10},{9,11},{10,... | collective-permute-start | bytes 49160 | tf_op jit(solution)/shard_map/ppermute | solution.py:422
  34.3 1.9 %collective-permute-start.11 = (f32[32,128]{1,0:T(8,128)S(1)}, f32[32,128]{1,0:T(8,128)S(1)}, u32[]{:S(2)}, u32[]{:S(2)}) collective-permute-start(f32[32,128]{1,0:T(8,128)S(1)} %get-tuple-element.124.refs_6_), channel_id=1, source_target_pairs={{0,1},{1,0},{2,3},{3,2},{4,5},{5,4},{6,7},{7,6},{8,9},{9,8},{10,11... | collective-permute-start | bytes 49160 | tf_op jit(solution)/shard_map/ppermute | solution.py:422
  37.0 1.6 %collective-permute-done.12.refs_8_ = f32[32,128]{1,0:T(8,128)S(1)} collective-permute-done((f32[32,128]{1,0:T(8,128)S(1)}, f32[32,128]{1,0:T(8,128)S(1)}, u32[]{:S(2)}, u32[]{:S(2)}) %collective-permute-start.12) | collective-permute-done | bytes 16416 | tf_op jit(solution)/shard_map/ppermute | solution.py:422
  39.1 2.9 %collective-permute-start.15 = (f32[128,128]{1,0:T(8,128)S(1)}, f32[128,128]{1,0:T(8,128)S(1)}, u32[]{:S(2)}, u32[]{:S(2)}) collective-permute-start(f32[128,128]{1,0:T(8,128)S(1)} %get-tuple-element.133), channel_id=1, source_target_pairs={{0,112},{16,0},{32,16},{48,32},{64,48},{80,64},{96,80},{112,96},{1... | collective-permute-start | bytes 196616 | tf_op jit(solution)/shard_map/ppermute | solution.py:418
  42.1 2.0 %collective-permute-start.16 = (f32[32,128]{1,0:T(8,128)S(1)}, f32[32,128]{1,0:T(8,128)S(1)}, u32[]{:S(2)}, u32[]{:S(2)}) collective-permute-start(f32[32,128]{1,0:T(8,128)S(1)} %get-tuple-element.131.refs_8_), channel_id=1, source_target_pairs={{0,4},{4,8},{8,12},{12,0},{1,5},{5,9},{9,13},{13,1},{2,6},{6,10},{... | collective-permute-start | bytes 49160 | tf_op jit(solution)/shard_map/ppermute | solution.py:418
  44.8 1.0 %collective-permute-done.17.refs_12_ = f32[32,128]{1,0:T(8,128)S(1)} collective-permute-done((f32[32,128]{1,0:T(8,128)S(1)}, f32[32,128]{1,0:T(8,128)S(1)}, u32[]{:S(2)}, u32[]{:S(2)}) %collective-permute-start.17) | collective-permute-done | bytes 16416 | tf_op jit(solution)/shard_map/ppermute | solution.py:418
  45.8 1.2 %collective-permute-done.16.refs_11_ = f32[32,128]{1,0:T(8,128)S(1)} collective-permute-done((f32[32,128]{1,0:T(8,128)S(1)}, f32[32,128]{1,0:T(8,128)S(1)}, u32[]{:S(2)}, u32[]{:S(2)}) %collective-permute-start.16) | collective-permute-done | bytes 16416 | tf_op jit(solution)/shard_map/ppermute | solution.py:418
  47.5 2.0 %collective-permute-start.20 = (f32[32,128]{1,0:T(8,128)S(1)}, f32[32,128]{1,0:T(8,128)S(1)}, u32[]{:S(2)}, u32[]{:S(2)}) collective-permute-start(f32[32,128]{1,0:T(8,128)S(1)} %get-tuple-element.145.refs_6_), channel_id=1, source_target_pairs={{0,3},{1,2},{2,1},{3,0},{4,7},{5,6},{6,5},{7,4},{8,11},{9,10},{10,... | collective-permute-start | bytes 49160 | tf_op jit(solution)/shard_map/ppermute | solution.py:422
  49.5 1.4 %collective-permute-start.19 = (f32[32,128]{1,0:T(8,128)S(1)}, f32[32,128]{1,0:T(8,128)S(1)}, u32[]{:S(2)}, u32[]{:S(2)}) collective-permute-start(f32[32,128]{1,0:T(8,128)S(1)} %get-tuple-element.145.refs_6_), channel_id=1, source_target_pairs={{0,2},{1,3},{2,0},{3,1},{4,6},{5,7},{6,4},{7,5},{8,10},{9,11},{10,... | collective-permute-start | bytes 49160 | tf_op jit(solution)/shard_map/ppermute | solution.py:422
  51.7 1.6 %upward2.1 = (f32[64,16,128]{2,1,0:T(8,128)}, f32[1024,128]{1,0:T(8,128)}, f32[1024,128]{1,0:T(8,128)S(1)}, f32[1024,128]{1,0:T(8,128)S(1)}) custom-call(f32[1024,128]{1,0:T(8,128)S(1)} %get-tuple-element.136.refs_0_, f32[1024,128]{1,0:T(8,128)S(1)} %get-tuple-element.137.refs_1_, f32[1024,128]{1,0:T(8,128)S(1)} %get-tuple-element.93.refs_2_, ...), custom_call_target="tpu_custom_call" | custom-call | tf_op jit(solution)/shard_map/upward2/pallas_call | solution.py:53
  53.3 1.4 %collective-permute-done.19.refs_8_ = f32[32,128]{1,0:T(8,128)S(1)} collective-permute-done((f32[32,128]{1,0:T(8,128)S(1)}, f32[32,128]{1,0:T(8,128)S(1)}, u32[]{:S(2)}, u32[]{:S(2)}) %collective-permute-start.19) | collective-permute-done | bytes 16416 | tf_op jit(solution)/shard_map/ppermute | solution.py:422
  54.7 1.2 %implicit2.1 = (f32[1024,128]{1,0:T(8,128)}, f32[1024,128]{1,0:T(8,128)}) custom-call(f32[1024,128]{1,0:T(8,128)S(1)} %get-tuple-element.143.refs_0_, f32[1024,128]{1,0:T(8,128)S(1)} %get-tuple-element.144.refs_1_, f32[1024,128]{1,0:T(8,128)S(1)} %get-tuple-element.102.refs_2_, f32[1024,128]{1,0:T(8,128)S(1)} %get-tuple-element.103.refs_3_, ...), custom_call_target="tpu_custom_call" | custom-call | tf_op jit(solution)/shard_map/implicit2/pallas_call | solution.py:53
  (36 shorter events, 8.5 us)
Async XLA Ops:
  0.6 8.4 %copy-start = (f32[64,16,128]{2,1,0:T(8,128)S(1)}, f32[64,16,128]{2,1,0:T(8,128)}, u32[]{:S(2)}) copy-start(f32[64,16,128]{2,1,0:T(8,128)} %param.11) | copy-start | bytes 1572868
  0.6 8.3 %copy-start.1 = (f32[64,16,128]{2,1,0:T(8,128)S(1)}, f32[64,16,128]{2,1,0:T(8,128)}, u32[]{:S(2)}) copy-start(f32[64,16,128]{2,1,0:T(8,128)} %param.8) | copy-start | bytes 1572868
  2.6 11.3 %collective-permute-start = (f32[256,128]{1,0:T(8,128)S(1)}, f32[256,128]{1,0:T(8,128)S(1)}, u32[]{:S(2)}, u32[]{:S(2)}) collective-permute-start(f32[256,128]{1,0:T(8,128)S(1)} %get-tuple-element.87), channel_id=1, source_target_pairs={{0,16},{16,32},{32,48},{48,64},{64,80},{80,96},{96,112},{112,0},{1... | collective-permute-start | bytes 393224 | tf_op jit(solution)/shard_map/ppermute | solution.py:418
  2.6 11.3 %collective-permute-start.1 = (f32[256,128]{1,0:T(8,128)S(1)}, f32[256,128]{1,0:T(8,128)S(1)}, u32[]{:S(2)}, u32[]{:S(2)}) collective-permute-start(f32[256,128]{1,0:T(8,128)S(1)} %get-tuple-element.88), channel_id=1, source_target_pairs={{0,112},{16,0},{32,16},{48,32},{64,48},{80,64},{96,80},{112,96},{1... | collective-permute-start | bytes 393224 | tf_op jit(solution)/shard_map/ppermute | solution.py:418
  6.2 4.5 %collective-permute-start.3 = (f32[32,128]{1,0:T(8,128)S(1)}, f32[32,128]{1,0:T(8,128)S(1)}, u32[]{:S(2)}, u32[]{:S(2)}) collective-permute-start(f32[32,128]{1,0:T(8,128)S(1)} %get-tuple-element.86.refs_8_), channel_id=1, source_target_pairs={{0,12},{4,0},{8,4},{12,8},{1,13},{5,1},{9,5},{13,9},{2,14},{6,2},{... | collective-permute-start | bytes 49160 | tf_op jit(solution)/shard_map/ppermute | solution.py:418
  9.0 4.9 %collective-permute-start.2 = (f32[32,128]{1,0:T(8,128)S(1)}, f32[32,128]{1,0:T(8,128)S(1)}, u32[]{:S(2)}, u32[]{:S(2)}) collective-permute-start(f32[32,128]{1,0:T(8,128)S(1)} %get-tuple-element.89.refs_17_), channel_id=1, source_target_pairs={{0,4},{4,8},{8,12},{12,0},{1,5},{5,9},{9,13},{13,1},{2,6},{6,10},{... | collective-permute-start | bytes 49160 | tf_op jit(solution)/shard_map/ppermute | solution.py:418
  14.4 5.3 %collective-permute-start.6 = (f32[80,128]{1,0:T(8,128)S(1)}, f32[80,128]{1,0:T(8,128)S(1)}, u32[]{:S(2)}, u32[]{:S(2)}) collective-permute-start(f32[80,128]{1,0:T(8,128)S(1)} %get-tuple-element.104.refs_6_), channel_id=1, source_target_pairs={{0,3},{1,2},{2,1},{3,0},{4,7},{5,6},{6,5},{7,4},{8,11},{9,10},{10,... | collective-permute-start | bytes 122888 | tf_op jit(solution)/shard_map/ppermute | solution.py:422
  17.5 5.5 %collective-permute-start.5 = (f32[80,128]{1,0:T(8,128)S(1)}, f32[80,128]{1,0:T(8,128)S(1)}, u32[]{:S(2)}, u32[]{:S(2)}) collective-permute-start(f32[80,128]{1,0:T(8,128)S(1)} %get-tuple-element.104.refs_6_), channel_id=1, source_target_pairs={{0,2},{1,3},{2,0},{3,1},{4,6},{5,7},{6,4},{7,5},{8,10},{9,11},{10,... | collective-permute-start | bytes 122888 | tf_op jit(solution)/shard_map/ppermute | solution.py:422
  18.2 4.9 %collective-permute-start.4 = (f32[80,128]{1,0:T(8,128)S(1)}, f32[80,128]{1,0:T(8,128)S(1)}, u32[]{:S(2)}, u32[]{:S(2)}) collective-permute-start(f32[80,128]{1,0:T(8,128)S(1)} %get-tuple-element.104.refs_6_), channel_id=1, source_target_pairs={{0,1},{1,0},{2,3},{3,2},{4,5},{5,4},{6,7},{7,6},{8,9},{9,8},{10,11... | collective-permute-start | bytes 122888 | tf_op jit(solution)/shard_map/ppermute | solution.py:422
  23.5 8.0 %collective-permute-start.7 = (f32[128,128]{1,0:T(8,128)S(1)}, f32[128,128]{1,0:T(8,128)S(1)}, u32[]{:S(2)}, u32[]{:S(2)}) collective-permute-start(f32[128,128]{1,0:T(8,128)S(1)} %get-tuple-element.114), channel_id=1, source_target_pairs={{0,16},{16,32},{32,48},{48,64},{64,80},{80,96},{96,112},{112,0},{1... | collective-permute-start | bytes 196616 | tf_op jit(solution)/shard_map/ppermute | solution.py:418
  23.5 8.0 %collective-permute-start.8 = (f32[128,128]{1,0:T(8,128)S(1)}, f32[128,128]{1,0:T(8,128)S(1)}, u32[]{:S(2)}, u32[]{:S(2)}) collective-permute-start(f32[128,128]{1,0:T(8,128)S(1)} %get-tuple-element.115), channel_id=1, source_target_pairs={{0,112},{16,0},{32,16},{48,32},{64,48},{80,64},{96,80},{112,96},{1... | collective-permute-start | bytes 196616 | tf_op jit(solution)/shard_map/ppermute | solution.py:418
  26.5 3.7 %collective-permute-start.10 = (f32[32,128]{1,0:T(8,128)S(1)}, f32[32,128]{1,0:T(8,128)S(1)}, u32[]{:S(2)}, u32[]{:S(2)}) collective-permute-start(f32[32,128]{1,0:T(8,128)S(1)} %get-tuple-element.113.refs_8_), channel_id=1, source_target_pairs={{0,12},{4,0},{8,4},{12,8},{1,13},{5,1},{9,5},{13,9},{2,14},{6,2},{... | collective-permute-start | bytes 49160 | tf_op jit(solution)/shard_map/ppermute | solution.py:418
  26.6 4.9 %collective-permute-start.9 = (f32[32,128]{1,0:T(8,128)S(1)}, f32[32,128]{1,0:T(8,128)S(1)}, u32[]{:S(2)}, u32[]{:S(2)}) collective-permute-start(f32[32,128]{1,0:T(8,128)S(1)} %get-tuple-element.113.refs_8_), channel_id=1, source_target_pairs={{0,4},{4,8},{8,12},{12,0},{1,5},{5,9},{9,13},{13,1},{2,6},{6,10},{... | collective-permute-start | bytes 49160 | tf_op jit(solution)/shard_map/ppermute | solution.py:418
  32.0 5.0 %collective-permute-start.13 = (f32[32,128]{1,0:T(8,128)S(1)}, f32[32,128]{1,0:T(8,128)S(1)}, u32[]{:S(2)}, u32[]{:S(2)}) collective-permute-start(f32[32,128]{1,0:T(8,128)S(1)} %get-tuple-element.124.refs_6_), channel_id=1, source_target_pairs={{0,3},{1,2},{2,1},{3,0},{4,7},{5,6},{6,5},{7,4},{8,11},{9,10},{10,... | collective-permute-start | bytes 49160 | tf_op jit(solution)/shard_map/ppermute | solution.py:422
  33.4 5.2 %collective-permute-start.12 = (f32[32,128]{1,0:T(8,128)S(1)}, f32[32,128]{1,0:T(8,128)S(1)}, u32[]{:S(2)}, u32[]{:S(2)}) collective-permute-start(f32[32,128]{1,0:T(8,128)S(1)} %get-tuple-element.124.refs_6_), channel_id=1, source_target_pairs={{0,2},{1,3},{2,0},{3,1},{4,6},{5,7},{6,4},{7,5},{8,10},{9,11},{10,... | collective-permute-start | bytes 49160 | tf_op jit(solution)/shard_map/ppermute | solution.py:422
  34.3 4.3 %collective-permute-start.11 = (f32[32,128]{1,0:T(8,128)S(1)}, f32[32,128]{1,0:T(8,128)S(1)}, u32[]{:S(2)}, u32[]{:S(2)}) collective-permute-start(f32[32,128]{1,0:T(8,128)S(1)} %get-tuple-element.124.refs_6_), channel_id=1, source_target_pairs={{0,1},{1,0},{2,3},{3,2},{4,5},{5,4},{6,7},{7,6},{8,9},{9,8},{10,11... | collective-permute-start | bytes 49160 | tf_op jit(solution)/shard_map/ppermute | solution.py:422
  39.1 7.9 %collective-permute-start.14 = (f32[128,128]{1,0:T(8,128)S(1)}, f32[128,128]{1,0:T(8,128)S(1)}, u32[]{:S(2)}, u32[]{:S(2)}) collective-permute-start(f32[128,128]{1,0:T(8,128)S(1)} %get-tuple-element.132), channel_id=1, source_target_pairs={{0,16},{16,32},{32,48},{48,64},{64,80},{80,96},{96,112},{112,0},{1... | collective-permute-start | bytes 196616 | tf_op jit(solution)/shard_map/ppermute | solution.py:418
  39.1 7.9 %collective-permute-start.15 = (f32[128,128]{1,0:T(8,128)S(1)}, f32[128,128]{1,0:T(8,128)S(1)}, u32[]{:S(2)}, u32[]{:S(2)}) collective-permute-start(f32[128,128]{1,0:T(8,128)S(1)} %get-tuple-element.133), channel_id=1, source_target_pairs={{0,112},{16,0},{32,16},{48,32},{64,48},{80,64},{96,80},{112,96},{1... | collective-permute-start | bytes 196616 | tf_op jit(solution)/shard_map/ppermute | solution.py:418
  42.0 3.7 %collective-permute-start.17 = (f32[32,128]{1,0:T(8,128)S(1)}, f32[32,128]{1,0:T(8,128)S(1)}, u32[]{:S(2)}, u32[]{:S(2)}) collective-permute-start(f32[32,128]{1,0:T(8,128)S(1)} %get-tuple-element.131.refs_8_), channel_id=1, source_target_pairs={{0,12},{4,0},{8,4},{12,8},{1,13},{5,1},{9,5},{13,9},{2,14},{6,2},{... | collective-permute-start | bytes 49160 | tf_op jit(solution)/shard_map/ppermute | solution.py:418
  42.1 4.9 %collective-permute-start.16 = (f32[32,128]{1,0:T(8,128)S(1)}, f32[32,128]{1,0:T(8,128)S(1)}, u32[]{:S(2)}, u32[]{:S(2)}) collective-permute-start(f32[32,128]{1,0:T(8,128)S(1)} %get-tuple-element.131.refs_8_), channel_id=1, source_target_pairs={{0,4},{4,8},{8,12},{12,0},{1,5},{5,9},{9,13},{13,1},{2,6},{6,10},{... | collective-permute-start | bytes 49160 | tf_op jit(solution)/shard_map/ppermute | solution.py:418
  47.5 5.8 %collective-permute-start.20 = (f32[32,128]{1,0:T(8,128)S(1)}, f32[32,128]{1,0:T(8,128)S(1)}, u32[]{:S(2)}, u32[]{:S(2)}) collective-permute-start(f32[32,128]{1,0:T(8,128)S(1)} %get-tuple-element.145.refs_6_), channel_id=1, source_target_pairs={{0,3},{1,2},{2,1},{3,0},{4,7},{5,6},{6,5},{7,4},{8,11},{9,10},{10,... | collective-permute-start | bytes 49160 | tf_op jit(solution)/shard_map/ppermute | solution.py:422
  49.5 5.2 %collective-permute-start.19 = (f32[32,128]{1,0:T(8,128)S(1)}, f32[32,128]{1,0:T(8,128)S(1)}, u32[]{:S(2)}, u32[]{:S(2)}) collective-permute-start(f32[32,128]{1,0:T(8,128)S(1)} %get-tuple-element.145.refs_6_), channel_id=1, source_target_pairs={{0,2},{1,3},{2,0},{3,1},{4,6},{5,7},{6,4},{7,5},{8,10},{9,11},{10,... | collective-permute-start | bytes 49160 | tf_op jit(solution)/shard_map/ppermute | solution.py:422
  50.9 3.8 %collective-permute-start.18 = (f32[32,128]{1,0:T(8,128)S(1)}, f32[32,128]{1,0:T(8,128)S(1)}, u32[]{:S(2)}, u32[]{:S(2)}) collective-permute-start(f32[32,128]{1,0:T(8,128)S(1)} %get-tuple-element.145.refs_6_), channel_id=1, source_target_pairs={{0,1},{1,0},{2,3},{3,2},{4,5},{5,4},{6,7},{7,6},{8,9},{9,8},{10,11... | collective-permute-start | bytes 49160 | tf_op jit(solution)/shard_map/ppermute | solution.py:422

commit v3 on v2

--- a/solution.py
+++ b/solution.py
@@ -89,7 +89,11 @@
     return pl.ds(i, NK, stride=NI)
 
 
-def prologue(p_in, v_in, b_in, u_in, p, v, b, u, to_up, to_down, to_right, to_left, sems):
+def is_even():
+    return (lax.axis_index("gx") & 1) == 0
+
+
+def prologue(p_in, v_in, b_in, u_in, p, v, b, u, to_chip, to_far, to_right, to_left, sems):
     copies = []
     for at, (source, target) in enumerate(((p_in, p), (v_in, v), (b_in, b), (u_in, u))):
         if at == 3:
@@ -106,10 +110,15 @@
     to_right[...] = jnp.where(slot < 2, edge_p, jnp.where(slot == 2, turn(edge_v, 1), turn(edge_b, 2)))
     to_left[...] = jnp.where(slot < 2, turn(edge_p, -2), jnp.where(slot == 2, edge_v, turn(edge_b, 1)))
     copies[3].wait()
-    for at, (field, i) in enumerate(((p, 14), (p, 15), (u, 15), (b, 15))):
-        to_up[row(at), :] = field[padded_row(i) if field is u else block_row(i), :]
-    for at, (field, i) in enumerate(((p, 0), (p, 1), (u, 0), (b, 0))):
-        to_down[row(at), :] = field[padded_row(i) if field is u else block_row(i), :]
+    even = is_even()
+    up, down = (
+        [p[block_row(edge), :], u[padded_row(edge), :] + away * courant_h * b[block_row(edge), :] * p[block_row(next_to), :]]
+        + [b[block_row(edge), :]]
+        for edge, next_to, away in ((NI - 1, NI - 2, 1), (0, 1, -1))
+    )
+    for at in range(3):
+        to_chip[row(at), :] = jnp.where(even, up[at], down[at])
+        to_far[row(at), :] = jnp.where(even, down[at], up[at])
 
 
 def factor(
@@ -210,25 +219,29 @@
 
 
 def explicit(first, last, *refs):
-    (p, u_old, b_u, star_part, s, a_p, top_p, sums, own, low, high, left, right, low0, high0, extra), refs = (
-        refs[:16],
-        refs[17:],
-    )
+    (p, u_old, b_u, star_part, s, a_p, top_p, sums, own, chip, far, left, right, extra), refs = refs[:14], refs[15:]
     if first:
         own_right, refs = refs[0], refs[1:]
     else:
         u_sides, refs = refs[0], refs[1:]
     u, p_star, message, side = refs[:4]
-    for n, (source, old) in enumerate(((low, low0), (high, high0))):
+    even = is_even()
+    for n in (0, 1):
         away, edge, second = (1, 0, 1) if n == 0 else (-1, NI - 1, NI - 2)
-        far, near = (0, 1) if n == 0 else (1, 0)
-        held = old[row(2), :] if first else u_sides[row(n), :]
-        held = held - courant_h * old[row(3), :] * (away * (p[block_row(edge), :] - source[row(far), :]))
+        mine, other = (far, chip) if n == 0 else (chip, far)
+        theirs = lambda at: jnp.where(even, mine[row(at), :], other[row(at), :])
+        if first:
+            near, held, b_side = theirs(0), theirs(1), theirs(2)
+            held = held - away * courant_h * b_side * p[block_row(edge), :]
+        else:
+            near, b_side = theirs(0), u_sides[row(2 + n), :]
+            held = u_sides[row(n), :] - away * courant_h * b_side * (p[block_row(edge), :] - theirs(1))
         u[padded_row(edge - away), :] = held
         if not last:
             refs[4][row(n), :] = held
-        u[padded_row(edge), :] = u_old[padded_row(edge), :] - courant_h * b_u[block_row(edge), :] * (
-            away * (p[block_row(second), :] - source[row(near), :])
+            refs[4][row(2 + n), :] = b_side
+        u[padded_row(edge), :] = u_old[padded_row(edge), :] - away * courant_h * b_u[block_row(edge), :] * (
+            p[block_row(second), :] - near
         )
     slot = slots()
     from_left = turn(left[...], 2)
@@ -360,7 +373,7 @@
     if last:
         w_far, p_far, w, p, sems = refs
     else:
-        (a_w, top_w), (w, p, sums, to_up, to_down, edges), refs = refs[:2], refs[2:8], refs[8:]
+        (a_w, top_w), (w, p, sums, to_chip, to_far, edges), refs = refs[:2], refs[2:8], refs[8:]
     position = lax.axis_index("lev")
     others = [ref[...] for ref in (own, by1, by2, by3)]
     by_group = []
@@ -406,10 +419,11 @@
     if not last:
         sums[level(0), :] = sum_a
         sums[level(1), :] = sum_t
-        for at, i in enumerate((14, 15)):
-            to_up[row(at), :] = p[block_row(i), :]
-        for at, i in enumerate((0, 1)):
-            to_down[row(at), :] = p[block_row(i), :]
+        even = is_even()
+        for at, (i, j) in enumerate(((NI - 1, 0), (NI - 2, 1))):
+            up, down = p[block_row(i), :], p[block_row(j), :]
+            to_chip[row(at), :] = jnp.where(even, up, down)
+            to_far[row(at), :] = jnp.where(even, down, up)
         edges[...] = pack_edges(lambda k, i: p[pl.ds(NI * k + i, 8), :])
 
 
@@ -418,15 +432,21 @@
     return lax.ppermute(block, axis, [(i, (i + distance) % size) for i in range(size)])
 
 
+def swap(block, first):
+    size = lax.axis_size("gx")
+    pairs = [(i, (i + 1) % size) for i in range(first, size, 2)]
+    return lax.ppermute(block, "gx", pairs + [(j, i) for i, j in pairs])
+
+
 def partner(block, mask):
     return lax.ppermute(block, "lev", [(i, i ^ mask) for i in range(4)])
 
 
 def shards(u_wind, v_wind, w_wind, pressure, buoyancy, stiffness):
     w, s = w_wind.reshape(BLOCK), stiffness.reshape(BLOCK)
-    p, v, b, u, to_up, to_down, to_right, own = call(
+    p, v, b, u, to_chip, to_far, to_right, own = call(
         prologue,
-        [BLOCK] * 3 + [PADDED, (4 * NK, NL), (4 * NK, NL), PACK, PACK],
+        [BLOCK] * 3 + [PADDED, (3 * NK, NL), (3 * NK, NL), PACK, PACK],
         [x.reshape(BLOCK) for x in (pressure, v_wind, buoyancy)] + [u_wind],
         "prologue",
         scratch=[pltpu.SemaphoreType.DMA((4,))],
@@ -439,20 +459,18 @@
     side, more = statics, [to_right]
     for step in range(SUBSTEPS):
         first, last = step == 0, step == SUBSTEPS - 1
-        low, high = ring(to_up, "gx", 1), ring(to_down, "gx", -1)
+        chip, far = swap(to_chip, 0), swap(to_far, 1)
         left, right = ring(to_right, "gy", 1), ring(to_left, "gy", -1)
-        if first:
-            gx_first = [low, high]
         u_part, v_part, star_part = call(
             functools.partial(inner, first), [PADDED, BLOCK, BLOCK], [p, u, v, b, b_v, s], f"inner{step}"
         )
-        args = [p, u, b, star_part, s, a_p, top_p, sums, own, low, high, left, right] + gx_first + [side, u_part] + more
+        args = [p, u, b, star_part, s, a_p, top_p, sums, own, chip, far, left, right, side, u_part] + more
         outs = [PADDED, BLOCK, ((5 if first else 2) * NI, NL)]
-        outs += [PACK] if last else [(2 * PACK[0], NL), (2 * NK, NL)]
+        outs += [PACK] if last else [(2 * PACK[0], NL), (4 * NK, NL)]
         u, p_star, message, side, *more = call(
-            functools.partial(explicit, first, last), outs, args, f"explicit{step}", aliases={16: 0}
+            functools.partial(explicit, first, last), outs, args, f"explicit{step}", aliases={14: 0}
         )
-        others = [partner(message, mask) for mask in (1, 2, 3)]
+        by1, by3, by2 = (partner(message, mask) for mask in (1, 3, 2))
         args = [p_star, w, theta, rest, g, eta, inv, v_part, side]
         outs = [BLOCK] * 3
         if last:
@@ -470,7 +488,7 @@
             )
         else:
             t0, y0, v = call(functools.partial(upward, False, False), outs, args, f"upward{step}")
-        args = [t0, y0, t1, y1, eta, inv, message] + others
+        args = [t0, y0, t1, y1, eta, inv, message, by1, by2, by3]
         args += [] if first else [kept]
         body = functools.partial(implicit, first, last)
         if last:
@@ -486,7 +504,7 @@
         else:
             outs = [BLOCK, BLOCK, (2 * NI, NL), (2 * NK, NL), (2 * NK, NL), PACK]
             outs += [(sum(COUNTS) * NI, NL)] if first else []
-            w, p, sums, to_up, to_down, own, *fixed = call(body, outs, args + [a_w, top_w], f"implicit{step}")
+            w, p, sums, to_chip, to_far, own, *fixed = call(body, outs, args + [a_w, top_w], f"implicit{step}")
             to_right = to_left = own
             if first:
                 kept = fixed[0]

time: 56 us -> 52.4 us (0.936)
  starting transfers between devices: 28.9 us -> 25 us
    ppermute x12 -> x6, starting transfers between devices: 16.4 us -> 6.81 us  [ring(): lax.ppermute(block, axis, [(i, (i + distance) % size) for i in range(size)])]
    ppermute x0 -> x6, starting transfers between devices: none -> 5.72 us  [swap(): return lax.ppermute(block, 'gx', pairs + [(j, i) for i, j in pairs])]
    ppermute x12 -> x6, waiting for transfers between devices: 7.64 us -> 7.65 us  [ring(): lax.ppermute(block, axis, [(i, (i + distance) % size) for i in range(size)])]
  transfers between devices with their start and end apart: 21 -> 21, of which waited for: 10 -> 10; matrix products, arithmetic and copies ran while one was open for 0% -> 0% of each run, Pallas kernels for 10% -> 11%
where the time goes in v3:
time: 52.4 us; the launch traced here: 52.3 us
  starting transfers between devices  25 us (48%)
  waiting for transfers between devices  15.4 us (29%)
  Pallas kernels  11.1 us (21%)
  between operations  0.79 us (2%)
    ppermute x9, starting transfers between devices, partner(): return lax.ppermute(block, 'lev', [(i, i ^ mask) for i in range(4)])  12.5 us
    pallas_call x14, Pallas kernels, call(): pl.pallas_call(body, out_shape=tuple(((hbm if at < far_out else vmem)(*sh...  11.1 us
    ppermute x9, waiting for transfers between devices, partner(): return lax.ppermute(block, 'lev', [(i, i ^ mask) for i in range(4)])  7.72 us
    ppermute x6, waiting for transfers between devices, ring(): lax.ppermute(block, axis, [(i, (i + distance) % size) for i in range(size)])  7.65 us
    ppermute x6, starting transfers between devices, ring(): lax.ppermute(block, axis, [(i, (i + distance) % size) for i in range(size)])  6.81 us
    ppermute x6, starting transfers between devices, swap(): return lax.ppermute(block, 'gx', pairs + [(j, i) for i, j in pairs])  5.72 us
  transfers between devices with their start and end apart: 21, of which 10 were waited for; matrix products, arithmetic and copies ran while one was open for 0% of the time, Pallas kernels for 11%

profile of v3, /device:TPU:0, one launch (start us, length us, event | category | flops | bytes accessed | tf_op | source)
XLA Modules:
  0.0 52.3 jit_solution(17893663299075395608)
XLA Ops:
  0.7 1.9 %prologue.1 = (f32[1024,128]{1,0:T(8,128)S(1)}, f32[1024,128]{1,0:T(8,128)S(1)}, f32[1024,128]{1,0:T(8,128)S(1)}, f32[1560,128]{1,0:T(8,128)S(1)}, f32[192,128]{...) custom-call(f32[1024,128]{1,0:T(8,128)} %bitcast.17, ...), custom_call_target="tpu_custom_call" | custom-call | tf_op jit(solution)/shard_map/prologue/pallas_call | solution.py:53
  2.7 4.3 %collective-permute-start.1 = (f32[192,128]{1,0:T(8,128)S(1)}, f32[192,128]{1,0:T(8,128)S(1)}, u32[]{:S(2)}, u32[]{:S(2)}) collective-permute-start(f32[192,128]{1,0:T(8,128)S(1)} %get-tuple-element.88), channel_id=1, source_target_pairs={{16,32},{48,64},{80,96},{112,0},{32,16},{64,48},{96,80},{0,112},{1... | collective-permute-start | bytes 294920 | tf_op jit(solution)/shard_map/ppermute | solution.py:438
  6.9 2.8 %collective-permute-start.3 = (f32[32,128]{1,0:T(8,128)S(1)}, f32[32,128]{1,0:T(8,128)S(1)}, u32[]{:S(2)}, u32[]{:S(2)}) collective-permute-start(f32[32,128]{1,0:T(8,128)S(1)} %get-tuple-element.86.refs_8_), channel_id=1, source_target_pairs={{0,12},{4,0},{8,4},{12,8},{1,13},{5,1},{9,5},{13,9},{2,14},{6,2},{... | collective-permute-start | bytes 49160 | tf_op jit(solution)/shard_map/ppermute | solution.py:432
  9.7 1.0 %factor.1 = (f32[1024,128]{1,0:T(8,128)S(1)}, f32[1024,128]{1,0:T(8,128)S(1)}, f32[1024,128]{1,0:T(8,128)S(1)}, f32[1024,128]{1,0:T(8,128)S(1)}, f32[1024,128]{1...) custom-call(f32[1024,128]{1,0:T(8,128)S(1)} %bitcast.8, ...), custom_call_target="tpu_custom_call" | custom-call | tf_op jit(solution)/shard_map/factor/pallas_call | solution.py:53
  10.7 0.7 %inner0.1 = (f32[1560,128]{1,0:T(8,128)S(1)}, f32[1024,128]{1,0:T(8,128)S(1)}, f32[1024,128]{1,0:T(8,128)S(1)}) custom-call(f32[1024,128]{1,0:T(8,128)S(1)} %get-tuple-element.76.p.refs_0_, f32[1560,128]{1,0:T(8,128)S(1)} %get-tuple-element.77.u.refs_1_, f32[1024,128]{1,0:T(8,128)S(1)} %get-tuple-element.80.v, ...), custom_call_target="tpu_custom_call" | custom-call | tf_op jit(solution)/shard_map/inner0/pallas_call | solution.py:53
  11.5 3.1 %collective-permute-done.2.refs_11_ = f32[32,128]{1,0:T(8,128)S(1)} collective-permute-done((f32[32,128]{1,0:T(8,128)S(1)}, f32[32,128]{1,0:T(8,128)S(1)}, u32[]{:S(2)}, u32[]{:S(2)}) %collective-permute-start.2) | collective-permute-done | bytes 16416 | tf_op jit(solution)/shard_map/ppermute | solution.py:432
  15.2 3.1 %collective-permute-start.6 = (f32[80,128]{1,0:T(8,128)S(1)}, f32[80,128]{1,0:T(8,128)S(1)}, u32[]{:S(2)}, u32[]{:S(2)}) collective-permute-start(f32[80,128]{1,0:T(8,128)S(1)} %get-tuple-element.104.refs_6_), channel_id=1, source_target_pairs={{0,3},{1,2},{2,1},{3,0},{4,7},{5,6},{6,5},{7,4},{8,11},{9,10},{10,... | collective-permute-start | bytes 122888 | tf_op jit(solution)/shard_map/ppermute | solution.py:442
  20.4 3.3 %collective-permute-done.5.refs_8_ = f32[80,128]{1,0:T(8,128)S(1)} collective-permute-done((f32[80,128]{1,0:T(8,128)S(1)}, f32[80,128]{1,0:T(8,128)S(1)}, u32[]{:S(2)}, u32[]{:S(2)}) %collective-permute-start.5) | collective-permute-done | bytes 40992 | tf_op jit(solution)/shard_map/ppermute | solution.py:442
  24.9 1.9 %collective-permute-start.9 = (f32[32,128]{1,0:T(8,128)S(1)}, f32[32,128]{1,0:T(8,128)S(1)}, u32[]{:S(2)}, u32[]{:S(2)}) collective-permute-start(f32[32,128]{1,0:T(8,128)S(1)} %get-tuple-element.113.refs_8_), channel_id=1, source_target_pairs={{0,4},{4,8},{8,12},{12,0},{1,5},{5,9},{9,13},{13,1},{2,6},{6,10},{... | collective-permute-start | bytes 49160 | tf_op jit(solution)/shard_map/ppermute | solution.py:432
  27.6 1.0 %collective-permute-done.10.refs_12_ = f32[32,128]{1,0:T(8,128)S(1)} collective-permute-done((f32[32,128]{1,0:T(8,128)S(1)}, f32[32,128]{1,0:T(8,128)S(1)}, u32[]{:S(2)}, u32[]{:S(2)}) %collective-permute-start.10) | collective-permute-done | bytes 16416 | tf_op jit(solution)/shard_map/ppermute | solution.py:432
  28.6 1.3 %collective-permute-done.9.refs_11_ = f32[32,128]{1,0:T(8,128)S(1)} collective-permute-done((f32[32,128]{1,0:T(8,128)S(1)}, f32[32,128]{1,0:T(8,128)S(1)}, u32[]{:S(2)}, u32[]{:S(2)}) %collective-permute-start.9) | collective-permute-done | bytes 16416 | tf_op jit(solution)/shard_map/ppermute | solution.py:432
  30.3 1.4 %collective-permute-start.13 = (f32[32,128]{1,0:T(8,128)S(1)}, f32[32,128]{1,0:T(8,128)S(1)}, u32[]{:S(2)}, u32[]{:S(2)}) collective-permute-start(f32[32,128]{1,0:T(8,128)S(1)} %get-tuple-element.124.refs_6_), channel_id=1, source_target_pairs={{0,3},{1,2},{2,1},{3,0},{4,7},{5,6},{6,5},{7,4},{8,11},{9,10},{10,... | collective-permute-start | bytes 49160 | tf_op jit(solution)/shard_map/ppermute | solution.py:442
  31.7 1.3 %collective-permute-start.12 = (f32[32,128]{1,0:T(8,128)S(1)}, f32[32,128]{1,0:T(8,128)S(1)}, u32[]{:S(2)}, u32[]{:S(2)}) collective-permute-start(f32[32,128]{1,0:T(8,128)S(1)} %get-tuple-element.124.refs_6_), channel_id=1, source_target_pairs={{0,2},{1,3},{2,0},{3,1},{4,6},{5,7},{6,4},{7,5},{8,10},{9,11},{10,... | collective-permute-start | bytes 49160 | tf_op jit(solution)/shard_map/ppermute | solution.py:442
  33.0 1.5 %collective-permute-start.11 = (f32[32,128]{1,0:T(8,128)S(1)}, f32[32,128]{1,0:T(8,128)S(1)}, u32[]{:S(2)}, u32[]{:S(2)}) collective-permute-start(f32[32,128]{1,0:T(8,128)S(1)} %get-tuple-element.124.refs_6_), channel_id=1, source_target_pairs={{0,1},{1,0},{2,3},{3,2},{4,5},{5,4},{6,7},{7,6},{8,9},{9,8},{10,11... | collective-permute-start | bytes 49160 | tf_op jit(solution)/shard_map/ppermute | solution.py:442
  35.4 1.6 %collective-permute-done.12.refs_8_ = f32[32,128]{1,0:T(8,128)S(1)} collective-permute-done((f32[32,128]{1,0:T(8,128)S(1)}, f32[32,128]{1,0:T(8,128)S(1)}, u32[]{:S(2)}, u32[]{:S(2)}) %collective-permute-start.12) | collective-permute-done | bytes 16416 | tf_op jit(solution)/shard_map/ppermute | solution.py:442
  38.2 2.0 %collective-permute-start.16 = (f32[32,128]{1,0:T(8,128)S(1)}, f32[32,128]{1,0:T(8,128)S(1)}, u32[]{:S(2)}, u32[]{:S(2)}) collective-permute-start(f32[32,128]{1,0:T(8,128)S(1)} %get-tuple-element.131.refs_8_), channel_id=1, source_target_pairs={{0,4},{4,8},{8,12},{12,0},{1,5},{5,9},{9,13},{13,1},{2,6},{6,10},{... | collective-permute-start | bytes 49160 | tf_op jit(solution)/shard_map/ppermute | solution.py:432
  40.3 0.7 %inner2.1 = (f32[1560,128]{1,0:T(8,128)S(1)}, f32[1024,128]{1,0:T(8,128)S(1)}, f32[1024,128]{1,0:T(8,128)S(1)}) custom-call(f32[1024,128]{1,0:T(8,128)S(1)} %get-tuple-element.126.p.refs_0_, f32[1560,128]{1,0:T(8,128)S(1)} %get-tuple-element.127.u.refs_1_, f32[1024,128]{1,0:T(8,128)S(1)} %get-tuple-element.128.v, ...), custom_call_target="tpu_custom_call" | custom-call | tf_op jit(solution)/shard_map/inner2/pallas_call | solution.py:53
  41.0 1.0 %collective-permute-done.17.refs_12_ = f32[32,128]{1,0:T(8,128)S(1)} collective-permute-done((f32[32,128]{1,0:T(8,128)S(1)}, f32[32,128]{1,0:T(8,128)S(1)}, u32[]{:S(2)}, u32[]{:S(2)}) %collective-permute-start.17) | collective-permute-done | bytes 16416 | tf_op jit(solution)/shard_map/ppermute | solution.py:432
  42.0 1.2 %collective-permute-done.16.refs_11_ = f32[32,128]{1,0:T(8,128)S(1)} collective-permute-done((f32[32,128]{1,0:T(8,128)S(1)}, f32[32,128]{1,0:T(8,128)S(1)}, u32[]{:S(2)}, u32[]{:S(2)}) %collective-permute-start.16) | collective-permute-done | bytes 16416 | tf_op jit(solution)/shard_map/ppermute | solution.py:432
  43.7 2.2 %collective-permute-start.20 = (f32[32,128]{1,0:T(8,128)S(1)}, f32[32,128]{1,0:T(8,128)S(1)}, u32[]{:S(2)}, u32[]{:S(2)}) collective-permute-start(f32[32,128]{1,0:T(8,128)S(1)} %get-tuple-element.145.refs_6_), channel_id=1, source_target_pairs={{0,3},{1,2},{2,1},{3,0},{4,7},{5,6},{6,5},{7,4},{8,11},{9,10},{10,... | collective-permute-start | bytes 49160 | tf_op jit(solution)/shard_map/ppermute | solution.py:442
  45.9 1.2 %collective-permute-start.19 = (f32[32,128]{1,0:T(8,128)S(1)}, f32[32,128]{1,0:T(8,128)S(1)}, u32[]{:S(2)}, u32[]{:S(2)}) collective-permute-start(f32[32,128]{1,0:T(8,128)S(1)} %get-tuple-element.145.refs_6_), channel_id=1, source_target_pairs={{0,2},{1,3},{2,0},{3,1},{4,6},{5,7},{6,4},{7,5},{8,10},{9,11},{10,... | collective-permute-start | bytes 49160 | tf_op jit(solution)/shard_map/ppermute | solution.py:442
  47.9 1.6 %upward2.1 = (f32[64,16,128]{2,1,0:T(8,128)}, f32[1024,128]{1,0:T(8,128)}, f32[1024,128]{1,0:T(8,128)S(1)}, f32[1024,128]{1,0:T(8,128)S(1)}) custom-call(f32[1024,128]{1,0:T(8,128)S(1)} %get-tuple-element.136.refs_0_, f32[1024,128]{1,0:T(8,128)S(1)} %get-tuple-element.137.refs_1_, f32[1024,128]{1,0:T(8,128)S(1)} %get-tuple-element.93.refs_2_, ...), custom_call_target="tpu_custom_call" | custom-call | tf_op jit(solution)/shard_map/upward2/pallas_call | solution.py:53
  49.5 1.7 %collective-permute-done.19.refs_8_ = f32[32,128]{1,0:T(8,128)S(1)} collective-permute-done((f32[32,128]{1,0:T(8,128)S(1)}, f32[32,128]{1,0:T(8,128)S(1)}, u32[]{:S(2)}, u32[]{:S(2)}) %collective-permute-start.19) | collective-permute-done | bytes 16416 | tf_op jit(solution)/shard_map/ppermute | solution.py:442
  51.2 1.2 %implicit2.1 = (f32[1024,128]{1,0:T(8,128)}, f32[1024,128]{1,0:T(8,128)}) custom-call(f32[1024,128]{1,0:T(8,128)S(1)} %get-tuple-element.143.refs_0_, f32[1024,128]{1,0:T(8,128)S(1)} %get-tuple-element.144.refs_1_, f32[1024,128]{1,0:T(8,128)S(1)} %get-tuple-element.102.refs_2_, f32[1024,128]{1,0:T(8,128)S(1)} %get-tuple-element.103.refs_3_, ...), custom_call_target="tpu_custom_call" | custom-call | tf_op jit(solution)/shard_map/implicit2/pallas_call | solution.py:53
  (36 shorter events, 8.4 us)
Async XLA Ops:
  0.6 9.1 %copy-start = (f32[64,16,128]{2,1,0:T(8,128)S(1)}, f32[64,16,128]{2,1,0:T(8,128)}, u32[]{:S(2)}) copy-start(f32[64,16,128]{2,1,0:T(8,128)} %param.11) | copy-start | bytes 1572868
  0.6 9.1 %copy-start.1 = (f32[64,16,128]{2,1,0:T(8,128)S(1)}, f32[64,16,128]{2,1,0:T(8,128)}, u32[]{:S(2)}) copy-start(f32[64,16,128]{2,1,0:T(8,128)} %param.8) | copy-start | bytes 1572868
  2.6 12.1 %collective-permute-start = (f32[192,128]{1,0:T(8,128)S(1)}, f32[192,128]{1,0:T(8,128)S(1)}, u32[]{:S(2)}, u32[]{:S(2)}) collective-permute-start(f32[192,128]{1,0:T(8,128)S(1)} %get-tuple-element.87), channel_id=1, source_target_pairs={{0,16},{32,48},{64,80},{96,112},{16,0},{48,32},{80,64},{112,96},{1... | collective-permute-start | bytes 294920 | tf_op jit(solution)/shard_map/ppermute | solution.py:438
  2.7 12.0 %collective-permute-start.1 = (f32[192,128]{1,0:T(8,128)S(1)}, f32[192,128]{1,0:T(8,128)S(1)}, u32[]{:S(2)}, u32[]{:S(2)}) collective-permute-start(f32[192,128]{1,0:T(8,128)S(1)} %get-tuple-element.88), channel_id=1, source_target_pairs={{16,32},{48,64},{80,96},{112,0},{32,16},{64,48},{96,80},{0,112},{1... | collective-permute-start | bytes 294920 | tf_op jit(solution)/shard_map/ppermute | solution.py:438
  6.9 4.6 %collective-permute-start.3 = (f32[32,128]{1,0:T(8,128)S(1)}, f32[32,128]{1,0:T(8,128)S(1)}, u32[]{:S(2)}, u32[]{:S(2)}) collective-permute-start(f32[32,128]{1,0:T(8,128)S(1)} %get-tuple-element.86.refs_8_), channel_id=1, source_target_pairs={{0,12},{4,0},{8,4},{12,8},{1,13},{5,1},{9,5},{13,9},{2,14},{6,2},{... | collective-permute-start | bytes 49160 | tf_op jit(solution)/shard_map/ppermute | solution.py:432
  9.7 4.9 %collective-permute-start.2 = (f32[32,128]{1,0:T(8,128)S(1)}, f32[32,128]{1,0:T(8,128)S(1)}, u32[]{:S(2)}, u32[]{:S(2)}) collective-permute-start(f32[32,128]{1,0:T(8,128)S(1)} %get-tuple-element.89.refs_15_), channel_id=1, source_target_pairs={{0,4},{4,8},{8,12},{12,0},{1,5},{5,9},{9,13},{13,1},{2,6},{6,10},{... | collective-permute-start | bytes 49160 | tf_op jit(solution)/shard_map/ppermute | solution.py:432
  15.2 5.3 %collective-permute-start.6 = (f32[80,128]{1,0:T(8,128)S(1)}, f32[80,128]{1,0:T(8,128)S(1)}, u32[]{:S(2)}, u32[]{:S(2)}) collective-permute-start(f32[80,128]{1,0:T(8,128)S(1)} %get-tuple-element.104.refs_6_), channel_id=1, source_target_pairs={{0,3},{1,2},{2,1},{3,0},{4,7},{5,6},{6,5},{7,4},{8,11},{9,10},{10,... | collective-permute-start | bytes 122888 | tf_op jit(solution)/shard_map/ppermute | solution.py:442
  18.2 5.5 %collective-permute-start.5 = (f32[80,128]{1,0:T(8,128)S(1)}, f32[80,128]{1,0:T(8,128)S(1)}, u32[]{:S(2)}, u32[]{:S(2)}) collective-permute-start(f32[80,128]{1,0:T(8,128)S(1)} %get-tuple-element.104.refs_6_), channel_id=1, source_target_pairs={{0,2},{1,3},{2,0},{3,1},{4,6},{5,7},{6,4},{7,5},{8,10},{9,11},{10,... | collective-permute-start | bytes 122888 | tf_op jit(solution)/shard_map/ppermute | solution.py:442
  18.9 4.9 %collective-permute-start.4 = (f32[80,128]{1,0:T(8,128)S(1)}, f32[80,128]{1,0:T(8,128)S(1)}, u32[]{:S(2)}, u32[]{:S(2)}) collective-permute-start(f32[80,128]{1,0:T(8,128)S(1)} %get-tuple-element.104.refs_6_), channel_id=1, source_target_pairs={{0,1},{1,0},{2,3},{3,2},{4,5},{5,4},{6,7},{7,6},{8,9},{9,8},{10,11... | collective-permute-start | bytes 122888 | tf_op jit(solution)/shard_map/ppermute | solution.py:442
  24.2 5.7 %collective-permute-start.7 = (f32[128,128]{1,0:T(8,128)S(1)}, f32[128,128]{1,0:T(8,128)S(1)}, u32[]{:S(2)}, u32[]{:S(2)}) collective-permute-start(f32[128,128]{1,0:T(8,128)S(1)} %get-tuple-element.114), channel_id=1, source_target_pairs={{0,16},{32,48},{64,80},{96,112},{16,0},{48,32},{80,64},{112,96},{1... | collective-permute-start | bytes 196616 | tf_op jit(solution)/shard_map/ppermute | solution.py:438
  24.3 5.6 %collective-permute-start.8 = (f32[128,128]{1,0:T(8,128)S(1)}, f32[128,128]{1,0:T(8,128)S(1)}, u32[]{:S(2)}, u32[]{:S(2)}) collective-permute-start(f32[128,128]{1,0:T(8,128)S(1)} %get-tuple-element.115), channel_id=1, source_target_pairs={{16,32},{48,64},{80,96},{112,0},{32,16},{64,48},{96,80},{0,112},{1... | collective-permute-start | bytes 196616 | tf_op jit(solution)/shard_map/ppermute | solution.py:438
  24.8 3.7 %collective-permute-start.10 = (f32[32,128]{1,0:T(8,128)S(1)}, f32[32,128]{1,0:T(8,128)S(1)}, u32[]{:S(2)}, u32[]{:S(2)}) collective-permute-start(f32[32,128]{1,0:T(8,128)S(1)} %get-tuple-element.113.refs_8_), channel_id=1, source_target_pairs={{0,12},{4,0},{8,4},{12,8},{1,13},{5,1},{9,5},{13,9},{2,14},{6,2},{... | collective-permute-start | bytes 49160 | tf_op jit(solution)/shard_map/ppermute | solution.py:432
  24.9 4.9 %collective-permute-start.9 = (f32[32,128]{1,0:T(8,128)S(1)}, f32[32,128]{1,0:T(8,128)S(1)}, u32[]{:S(2)}, u32[]{:S(2)}) collective-permute-start(f32[32,128]{1,0:T(8,128)S(1)} %get-tuple-element.113.refs_8_), channel_id=1, source_target_pairs={{0,4},{4,8},{8,12},{12,0},{1,5},{5,9},{9,13},{13,1},{2,6},{6,10},{... | collective-permute-start | bytes 49160 | tf_op jit(solution)/shard_map/ppermute | solution.py:432
  30.3 5.0 %collective-permute-start.13 = (f32[32,128]{1,0:T(8,128)S(1)}, f32[32,128]{1,0:T(8,128)S(1)}, u32[]{:S(2)}, u32[]{:S(2)}) collective-permute-start(f32[32,128]{1,0:T(8,128)S(1)} %get-tuple-element.124.refs_6_), channel_id=1, source_target_pairs={{0,3},{1,2},{2,1},{3,0},{4,7},{5,6},{6,5},{7,4},{8,11},{9,10},{10,... | collective-permute-start | bytes 49160 | tf_op jit(solution)/shard_map/ppermute | solution.py:442
  31.7 5.2 %collective-permute-start.12 = (f32[32,128]{1,0:T(8,128)S(1)}, f32[32,128]{1,0:T(8,128)S(1)}, u32[]{:S(2)}, u32[]{:S(2)}) collective-permute-start(f32[32,128]{1,0:T(8,128)S(1)} %get-tuple-element.124.refs_6_), channel_id=1, source_target_pairs={{0,2},{1,3},{2,0},{3,1},{4,6},{5,7},{6,4},{7,5},{8,10},{9,11},{10,... | collective-permute-start | bytes 49160 | tf_op jit(solution)/shard_map/ppermute | solution.py:442
  33.0 4.0 %collective-permute-start.11 = (f32[32,128]{1,0:T(8,128)S(1)}, f32[32,128]{1,0:T(8,128)S(1)}, u32[]{:S(2)}, u32[]{:S(2)}) collective-permute-start(f32[32,128]{1,0:T(8,128)S(1)} %get-tuple-element.124.refs_6_), channel_id=1, source_target_pairs={{0,1},{1,0},{2,3},{3,2},{4,5},{5,4},{6,7},{7,6},{8,9},{9,8},{10,11... | collective-permute-start | bytes 49160 | tf_op jit(solution)/shard_map/ppermute | solution.py:442
  37.4 5.8 %collective-permute-start.14 = (f32[128,128]{1,0:T(8,128)S(1)}, f32[128,128]{1,0:T(8,128)S(1)}, u32[]{:S(2)}, u32[]{:S(2)}) collective-permute-start(f32[128,128]{1,0:T(8,128)S(1)} %get-tuple-element.132), channel_id=1, source_target_pairs={{0,16},{32,48},{64,80},{96,112},{16,0},{48,32},{80,64},{112,96},{1... | collective-permute-start | bytes 196616 | tf_op jit(solution)/shard_map/ppermute | solution.py:438
  37.5 5.7 %collective-permute-start.15 = (f32[128,128]{1,0:T(8,128)S(1)}, f32[128,128]{1,0:T(8,128)S(1)}, u32[]{:S(2)}, u32[]{:S(2)}) collective-permute-start(f32[128,128]{1,0:T(8,128)S(1)} %get-tuple-element.133), channel_id=1, source_target_pairs={{16,32},{48,64},{80,96},{112,0},{32,16},{64,48},{96,80},{0,112},{1... | collective-permute-start | bytes 196616 | tf_op jit(solution)/shard_map/ppermute | solution.py:438
  38.2 3.8 %collective-permute-start.17 = (f32[32,128]{1,0:T(8,128)S(1)}, f32[32,128]{1,0:T(8,128)S(1)}, u32[]{:S(2)}, u32[]{:S(2)}) collective-permute-start(f32[32,128]{1,0:T(8,128)S(1)} %get-tuple-element.131.refs_8_), channel_id=1, source_target_pairs={{0,12},{4,0},{8,4},{12,8},{1,13},{5,1},{9,5},{13,9},{2,14},{6,2},{... | collective-permute-start | bytes 49160 | tf_op jit(solution)/shard_map/ppermute | solution.py:432
  38.2 5.0 %collective-permute-start.16 = (f32[32,128]{1,0:T(8,128)S(1)}, f32[32,128]{1,0:T(8,128)S(1)}, u32[]{:S(2)}, u32[]{:S(2)}) collective-permute-start(f32[32,128]{1,0:T(8,128)S(1)} %get-tuple-element.131.refs_8_), channel_id=1, source_target_pairs={{0,4},{4,8},{8,12},{12,0},{1,5},{5,9},{9,13},{13,1},{2,6},{6,10},{... | collective-permute-start | bytes 49160 | tf_op jit(solution)/shard_map/ppermute | solution.py:432
  43.7 5.8 %collective-permute-start.20 = (f32[32,128]{1,0:T(8,128)S(1)}, f32[32,128]{1,0:T(8,128)S(1)}, u32[]{:S(2)}, u32[]{:S(2)}) collective-permute-start(f32[32,128]{1,0:T(8,128)S(1)} %get-tuple-element.145.refs_6_), channel_id=1, source_target_pairs={{0,3},{1,2},{2,1},{3,0},{4,7},{5,6},{6,5},{7,4},{8,11},{9,10},{10,... | collective-permute-start | bytes 49160 | tf_op jit(solution)/shard_map/ppermute | solution.py:442
  45.9 5.2 %collective-permute-start.19 = (f32[32,128]{1,0:T(8,128)S(1)}, f32[32,128]{1,0:T(8,128)S(1)}, u32[]{:S(2)}, u32[]{:S(2)}) collective-permute-start(f32[32,128]{1,0:T(8,128)S(1)} %get-tuple-element.145.refs_6_), channel_id=1, source_target_pairs={{0,2},{1,3},{2,0},{3,1},{4,6},{5,7},{6,4},{7,5},{8,10},{9,11},{10,... | collective-permute-start | bytes 49160 | tf_op jit(solution)/shard_map/ppermute | solution.py:442
  47.1 4.0 %collective-permute-start.18 = (f32[32,128]{1,0:T(8,128)S(1)}, f32[32,128]{1,0:T(8,128)S(1)}, u32[]{:S(2)}, u32[]{:S(2)}) collective-permute-start(f32[32,128]{1,0:T(8,128)S(1)} %get-tuple-element.145.refs_6_), channel_id=1, source_target_pairs={{0,1},{1,0},{2,3},{3,2},{4,5},{5,4},{6,7},{7,6},{8,9},{9,8},{10,11... | collective-permute-start | bytes 49160 | tf_op jit(solution)/shard_map/ppermute | solution.py:442

commit v4 on v3

--- a/solution.py
+++ b/solution.py
@@ -89,11 +89,11 @@
     return pl.ds(i, NK, stride=NI)
 
 
-def is_even():
-    return (lax.axis_index("gx") & 1) == 0
-
-
-def prologue(p_in, v_in, b_in, u_in, p, v, b, u, to_chip, to_far, to_right, to_left, sems):
+def is_even(axis):
+    return (lax.axis_index(axis) & 1) == 0
+
+
+def prologue(p_in, v_in, b_in, u_in, p, v, b, u, to_chip, to_far, to_right, to_left, to_first, to_second, sems):
     copies = []
     for at, (source, target) in enumerate(((p_in, p), (v_in, v), (b_in, b), (u_in, u))):
         if at == 3:
@@ -107,10 +107,15 @@
         packs.append(pack_edges(lambda k, i: field[pl.ds(NI * k + i, 8), :]))
     edge_p, edge_v, edge_b = packs
     slot = slots()
-    to_right[...] = jnp.where(slot < 2, edge_p, jnp.where(slot == 2, turn(edge_v, 1), turn(edge_b, 2)))
-    to_left[...] = jnp.where(slot < 2, turn(edge_p, -2), jnp.where(slot == 2, edge_v, turn(edge_b, 1)))
+    going_right = jnp.where(slot < 2, edge_p, jnp.where(slot == 2, turn(edge_v, 1), turn(edge_b, 2)))
+    going_left = jnp.where(slot < 2, turn(edge_p, -2), jnp.where(slot == 2, edge_v, turn(edge_b, 1)))
+    to_right[...] = going_right
+    to_left[...] = going_left
+    even = is_even("gy")
+    to_first[...] = jnp.where(even, going_right, going_left)
+    to_second[...] = jnp.where(even, going_left, going_right)
     copies[3].wait()
-    even = is_even()
+    even = is_even("gx")
     up, down = (
         [p[block_row(edge), :], u[padded_row(edge), :] + away * courant_h * b[block_row(edge), :] * p[block_row(next_to), :]]
         + [b[block_row(edge), :]]
@@ -219,13 +224,13 @@
 
 
 def explicit(first, last, *refs):
-    (p, u_old, b_u, star_part, s, a_p, top_p, sums, own, chip, far, left, right, extra), refs = refs[:14], refs[15:]
+    (p, u_old, b_u, star_part, s, a_p, top_p, sums, own, chip, far, by_first, by_second, extra), refs = refs[:14], refs[15:]
     if first:
         own_right, refs = refs[0], refs[1:]
     else:
         u_sides, refs = refs[0], refs[1:]
     u, p_star, message, side = refs[:4]
-    even = is_even()
+    even = is_even("gx")
     for n in (0, 1):
         away, edge, second = (1, 0, 1) if n == 0 else (-1, NI - 1, NI - 2)
         mine, other = (far, chip) if n == 0 else (chip, far)
@@ -244,12 +249,15 @@
             p[block_row(second), :] - near
         )
     slot = slots()
-    from_left = turn(left[...], 2)
+    even = is_even("gy")
+    left = jnp.where(even, by_second[...], by_first[...])
+    right = jnp.where(even, by_first[...], by_second[...])
+    from_left = turn(left, 2)
     if first:
-        mine, from_right = own[...], right[...]
+        mine, from_right = own[...], right
         edge = turn(mine, 2)
-        v_side = jnp.where(slot == 2, left[...], turn(mine, 1))
-        b_pack = jnp.where(slot == 2, turn(left[...], -1), mine)
+        v_side = jnp.where(slot == 2, left, turn(mine, 1))
+        b_pack = jnp.where(slot == 2, turn(left, -1), mine)
         b_edge = jnp.where(slot == 0, turn(own_right[...], -3), turn(from_right, -2))
         b_pack = jnp.where(slot < 2, b_edge, b_pack)
         ahead = turn(from_right, -1) - courant_h * b_edge * (from_right - own_right[...])
@@ -257,7 +265,7 @@
     else:
         edge = own[...]
         v_side, b_pack = extra[pl.ds(0, 32), :], extra[pl.ds(32, 32), :]
-        taken = courant_h * b_pack * turn(right[...], -2)
+        taken = courant_h * b_pack * turn(right, -2)
     v_side = v_side - courant_h * b_pack * (edge - from_left)
     packed = jnp.where(slot < 2, taken, v_side)
     side[pl.ds(0, 32), :] = packed
@@ -298,7 +306,8 @@
 
         send(main_rows(u), u_far)
     elif first:
-        b_v, right, t0, y0, v_out, b_patched = refs
+        b_v, by_first, by_second, t0, y0, v_out, b_patched = refs
+        right = jnp.where(is_even("gy"), by_first[...], by_second[...])
     else:
         t0, y0, v_out = refs
     lane = lax.broadcasted_iota(jnp.int32, (NI * BATCH, NL), 1)
@@ -419,7 +428,7 @@
     if not last:
         sums[level(0), :] = sum_a
         sums[level(1), :] = sum_t
-        even = is_even()
+        even = is_even("gx")
         for at, (i, j) in enumerate(((NI - 1, 0), (NI - 2, 1))):
             up, down = p[block_row(i), :], p[block_row(j), :]
             to_chip[row(at), :] = jnp.where(even, up, down)
@@ -427,15 +436,10 @@
         edges[...] = pack_edges(lambda k, i: p[pl.ds(NI * k + i, 8), :])
 
 
-def ring(block, axis, distance):
+def swap(block, axis, first):
     size = lax.axis_size(axis)
-    return lax.ppermute(block, axis, [(i, (i + distance) % size) for i in range(size)])
-
-
-def swap(block, first):
-    size = lax.axis_size("gx")
     pairs = [(i, (i + 1) % size) for i in range(first, size, 2)]
-    return lax.ppermute(block, "gx", pairs + [(j, i) for i, j in pairs])
+    return lax.ppermute(block, axis, pairs + [(j, i) for i, j in pairs])
 
 
 def partner(block, mask):
@@ -444,27 +448,26 @@
 
 def shards(u_wind, v_wind, w_wind, pressure, buoyancy, stiffness):
     w, s = w_wind.reshape(BLOCK), stiffness.reshape(BLOCK)
-    p, v, b, u, to_chip, to_far, to_right, own = call(
+    p, v, b, u, to_chip, to_far, to_right, own, to_first, to_second = call(
         prologue,
-        [BLOCK] * 3 + [PADDED, (3 * NK, NL), (3 * NK, NL), PACK, PACK],
+        [BLOCK] * 3 + [PADDED, (3 * NK, NL), (3 * NK, NL)] + [PACK] * 4,
         [x.reshape(BLOCK) for x in (pressure, v_wind, buoyancy)] + [u_wind],
         "prologue",
         scratch=[pltpu.SemaphoreType.DMA((4,))],
         far_in=4,
     )
-    to_left = own
     (theta, rest, g, eta, inv, t1, y1, a_p, top_p, a_w, top_w, v, b_v, statics, sums) = call(
         factor, [BLOCK] * 13 + [(3 * NI, NL), (2 * NI, NL)], [s, w, b, v], "factor"
     )
     side, more = statics, [to_right]
     for step in range(SUBSTEPS):
         first, last = step == 0, step == SUBSTEPS - 1
-        chip, far = swap(to_chip, 0), swap(to_far, 1)
-        left, right = ring(to_right, "gy", 1), ring(to_left, "gy", -1)
+        chip, far = swap(to_chip, "gx", 0), swap(to_far, "gx", 1)
+        by_first, by_second = swap(to_first, "gy", 0), swap(to_second, "gy", 1)
         u_part, v_part, star_part = call(
             functools.partial(inner, first), [PADDED, BLOCK, BLOCK], [p, u, v, b, b_v, s], f"inner{step}"
         )
-        args = [p, u, b, star_part, s, a_p, top_p, sums, own, chip, far, left, right, side, u_part] + more
+        args = [p, u, b, star_part, s, a_p, top_p, sums, own, chip, far, by_first, by_second, side, u_part] + more
         outs = [PADDED, BLOCK, ((5 if first else 2) * NI, NL)]
         outs += [PACK] if last else [(2 * PACK[0], NL), (4 * NK, NL)]
         u, p_star, message, side, *more = call(
@@ -484,7 +487,7 @@
             )
         elif first:
             t0, y0, v, b_v = call(
-                functools.partial(upward, True, False), outs + [BLOCK], args + [b_v, right], f"upward{step}"
+                functools.partial(upward, True, False), outs + [BLOCK], args + [b_v, by_first, by_second], f"upward{step}"
             )
         else:
             t0, y0, v = call(functools.partial(upward, False, False), outs, args, f"upward{step}")
@@ -505,7 +508,7 @@
             outs = [BLOCK, BLOCK, (2 * NI, NL), (2 * NK, NL), (2 * NK, NL), PACK]
             outs += [(sum(COUNTS) * NI, NL)] if first else []
             w, p, sums, to_chip, to_far, own, *fixed = call(body, outs, args + [a_w, top_w], f"implicit{step}")
-            to_right = to_left = own
+            to_first = to_second = own
             if first:
                 kept = fixed[0]
     return tuple(x.reshape(NK, NI, NL) for x in (u_far, v_far, w_far, p_far))

time: 52.4 us -> 51.3 us (0.979)
  waiting for transfers between devices: 15.4 us -> 14.6 us
    ppermute x12, waiting for transfers between devices: 7.66 us -> 7.09 us  [swap(): return lax.ppermute(block, axis, pairs + [(j, i) for i, j in pairs])]
  transfers between devices with their start and end apart: 21 -> 21, of which waited for: 10 -> 9; matrix products, arithmetic and copies ran while one was open for 0% -> 0% of each run, Pallas kernels for 11% -> 11%
where the time goes in v4:
time: 51.3 us; the launch traced here: 51.1 us
  starting transfers between devices  24.6 us (48%)
  waiting for transfers between devices  14.6 us (28%)
  Pallas kernels  11.1 us (22%)
  between operations  0.79 us (2%)
    ppermute x9, starting transfers between devices, partner(): return lax.ppermute(block, 'lev', [(i, i ^ mask) for i in range(4)])  12.5 us
    ppermute x12, starting transfers between devices, swap(): return lax.ppermute(block, axis, pairs + [(j, i) for i, j in pairs])  12.1 us
    pallas_call x14, Pallas kernels, call(): pl.pallas_call(body, out_shape=tuple(((hbm if at < far_out else vmem)(*sh...  11.1 us
    ppermute x9, waiting for transfers between devices, partner(): return lax.ppermute(block, 'lev', [(i, i ^ mask) for i in range(4)])  7.5 us
    ppermute x12, waiting for transfers between devices, swap(): return lax.ppermute(block, axis, pairs + [(j, i) for i, j in pairs])  7.09 us
  transfers between devices with their start and end apart: 21, of which 9 were waited for; matrix products, arithmetic and copies ran while one was open for 0% of the time, Pallas kernels for 11%

profile of v4, /device:TPU:0, one launch (start us, length us, event | category | flops | bytes accessed | tf_op | source)
XLA Modules:
  0.0 51.1 jit_solution(543452413331914071)
XLA Ops:
  0.7 1.9 %prologue.1 = (f32[1024,128]{1,0:T(8,128)S(1)}, f32[1024,128]{1,0:T(8,128)S(1)}, f32[1024,128]{1,0:T(8,128)S(1)}, f32[1560,128]{1,0:T(8,128)S(1)}, f32[192,128]{...) custom-call(f32[1024,128]{1,0:T(8,128)} %bitcast.17, ...), custom_call_target="tpu_custom_call" | custom-call | tf_op jit(solution)/shard_map/prologue/pallas_call | solution.py:53
  2.7 4.3 %collective-permute-start.1 = (f32[192,128]{1,0:T(8,128)S(1)}, f32[192,128]{1,0:T(8,128)S(1)}, u32[]{:S(2)}, u32[]{:S(2)}) collective-permute-start(f32[192,128]{1,0:T(8,128)S(1)} %get-tuple-element.90), channel_id=1, source_target_pairs={{16,32},{48,64},{80,96},{112,0},{32,16},{64,48},{96,80},{0,112},{1... | collective-permute-start | bytes 294920 | tf_op jit(solution)/shard_map/ppermute | solution.py:442
  6.9 1.5 %collective-permute-start.2 = (f32[32,128]{1,0:T(8,128)S(1)}, f32[32,128]{1,0:T(8,128)S(1)}, u32[]{:S(2)}, u32[]{:S(2)}) collective-permute-start(f32[32,128]{1,0:T(8,128)S(1)} %get-tuple-element.91), channel_id=1, source_target_pairs={{0,4},{8,12},{4,0},{12,8},{1,5},{9,13},{5,1},{13,9},{2,6},{10,14},... | collective-permute-start | bytes 49160 | tf_op jit(solution)/shard_map/ppermute | solution.py:442
  8.4 2.1 %collective-permute-start.3 = (f32[32,128]{1,0:T(8,128)S(1)}, f32[32,128]{1,0:T(8,128)S(1)}, u32[]{:S(2)}, u32[]{:S(2)}) collective-permute-start(f32[32,128]{1,0:T(8,128)S(1)} %get-tuple-element.92), channel_id=1, source_target_pairs={{4,8},{12,0},{8,4},{0,12},{5,9},{13,1},{9,5},{1,13},{6,10},{14,2},... | collective-permute-start | bytes 49160 | tf_op jit(solution)/shard_map/ppermute | solution.py:442
  10.5 1.0 %factor.1 = (f32[1024,128]{1,0:T(8,128)S(1)}, f32[1024,128]{1,0:T(8,128)S(1)}, f32[1024,128]{1,0:T(8,128)S(1)}, f32[1024,128]{1,0:T(8,128)S(1)}, f32[1024,128]{1...) custom-call(f32[1024,128]{1,0:T(8,128)S(1)} %bitcast.8, ...), custom_call_target="tpu_custom_call" | custom-call | tf_op jit(solution)/shard_map/factor/pallas_call | solution.py:53
  11.5 0.7 %inner0.1 = (f32[1560,128]{1,0:T(8,128)S(1)}, f32[1024,128]{1,0:T(8,128)S(1)}, f32[1024,128]{1,0:T(8,128)S(1)}) custom-call(f32[1024,128]{1,0:T(8,128)S(1)} %get-tuple-element.78.p.refs_0_, f32[1560,128]{1,0:T(8,128)S(1)} %get-tuple-element.79.u.refs_1_, f32[1024,128]{1,0:T(8,128)S(1)} %get-tuple-element.82.v, ...), custom_call_target="tpu_custom_call" | custom-call | tf_op jit(solution)/shard_map/inner0/pallas_call | solution.py:53
  12.3 1.1 %collective-permute-done.3.refs_12_.refs_11_ = f32[32,128]{1,0:T(8,128)S(1)} collective-permute-done((f32[32,128]{1,0:T(8,128)S(1)}, f32[32,128]{1,0:T(8,128)S(1)}, u32[]{:S(2)}, u32[]{:S(2)}) %collective-permute-start.3) | collective-permute-done | bytes 16416 | tf_op jit(solution)/shard_map/ppermute | solution.py:442
  13.9 3.1 %collective-permute-start.6 = (f32[80,128]{1,0:T(8,128)S(1)}, f32[80,128]{1,0:T(8,128)S(1)}, u32[]{:S(2)}, u32[]{:S(2)}) collective-permute-start(f32[80,128]{1,0:T(8,128)S(1)} %get-tuple-element.108.refs_6_), channel_id=1, source_target_pairs={{0,3},{1,2},{2,1},{3,0},{4,7},{5,6},{6,5},{7,4},{8,11},{9,10},{10,... | collective-permute-start | bytes 122888 | tf_op jit(solution)/shard_map/ppermute | solution.py:446
  19.2 3.3 %collective-permute-done.5.refs_8_ = f32[80,128]{1,0:T(8,128)S(1)} collective-permute-done((f32[80,128]{1,0:T(8,128)S(1)}, f32[80,128]{1,0:T(8,128)S(1)}, u32[]{:S(2)}, u32[]{:S(2)}) %collective-permute-start.5) | collective-permute-done | bytes 40992 | tf_op jit(solution)/shard_map/ppermute | solution.py:446
  23.6 2.1 %collective-permute-start.10 = (f32[32,128]{1,0:T(8,128)S(1)}, f32[32,128]{1,0:T(8,128)S(1)}, u32[]{:S(2)}, u32[]{:S(2)}) collective-permute-start(f32[32,128]{1,0:T(8,128)S(1)} %get-tuple-element.117.refs_8_), channel_id=1, source_target_pairs={{4,8},{12,0},{8,4},{0,12},{5,9},{13,1},{9,5},{1,13},{6,10},{14,2},... | collective-permute-start | bytes 49160 | tf_op jit(solution)/shard_map/ppermute | solution.py:442
  26.4 2.1 %collective-permute-done.10.refs_12_ = f32[32,128]{1,0:T(8,128)S(1)} collective-permute-done((f32[32,128]{1,0:T(8,128)S(1)}, f32[32,128]{1,0:T(8,128)S(1)}, u32[]{:S(2)}, u32[]{:S(2)}) %collective-permute-start.10) | collective-permute-done | bytes 16416 | tf_op jit(solution)/shard_map/ppermute | solution.py:442
  28.5 0.9 %collective-permute-done.9.refs_11_ = f32[32,128]{1,0:T(8,128)S(1)} collective-permute-done((f32[32,128]{1,0:T(8,128)S(1)}, f32[32,128]{1,0:T(8,128)S(1)}, u32[]{:S(2)}, u32[]{:S(2)}) %collective-permute-start.9) | collective-permute-done | bytes 16416 | tf_op jit(solution)/shard_map/ppermute | solution.py:442
  29.9 1.4 %collective-permute-start.13 = (f32[32,128]{1,0:T(8,128)S(1)}, f32[32,128]{1,0:T(8,128)S(1)}, u32[]{:S(2)}, u32[]{:S(2)}) collective-permute-start(f32[32,128]{1,0:T(8,128)S(1)} %get-tuple-element.128.refs_6_), channel_id=1, source_target_pairs={{0,3},{1,2},{2,1},{3,0},{4,7},{5,6},{6,5},{7,4},{8,11},{9,10},{10,... | collective-permute-start | bytes 49160 | tf_op jit(solution)/shard_map/ppermute | solution.py:446
  31.3 0.9 %collective-permute-start.12 = (f32[32,128]{1,0:T(8,128)S(1)}, f32[32,128]{1,0:T(8,128)S(1)}, u32[]{:S(2)}, u32[]{:S(2)}) collective-permute-start(f32[32,128]{1,0:T(8,128)S(1)} %get-tuple-element.128.refs_6_), channel_id=1, source_target_pairs={{0,2},{1,3},{2,0},{3,1},{4,6},{5,7},{6,4},{7,5},{8,10},{9,11},{10,... | collective-permute-start | bytes 49160 | tf_op jit(solution)/shard_map/ppermute | solution.py:446
  32.2 1.9 %collective-permute-start.11 = (f32[32,128]{1,0:T(8,128)S(1)}, f32[32,128]{1,0:T(8,128)S(1)}, u32[]{:S(2)}, u32[]{:S(2)}) collective-permute-start(f32[32,128]{1,0:T(8,128)S(1)} %get-tuple-element.128.refs_6_), channel_id=1, source_target_pairs={{0,1},{1,0},{2,3},{3,2},{4,5},{5,4},{6,7},{7,6},{8,9},{9,8},{10,11... | collective-permute-start | bytes 49160 | tf_op jit(solution)/shard_map/ppermute | solution.py:446
  34.9 1.6 %collective-permute-done.12.refs_8_ = f32[32,128]{1,0:T(8,128)S(1)} collective-permute-done((f32[32,128]{1,0:T(8,128)S(1)}, f32[32,128]{1,0:T(8,128)S(1)}, u32[]{:S(2)}, u32[]{:S(2)}) %collective-permute-start.12) | collective-permute-done | bytes 16416 | tf_op jit(solution)/shard_map/ppermute | solution.py:446
  37.3 1.2 %collective-permute-start.17 = (f32[32,128]{1,0:T(8,128)S(1)}, f32[32,128]{1,0:T(8,128)S(1)}, u32[]{:S(2)}, u32[]{:S(2)}) collective-permute-start(f32[32,128]{1,0:T(8,128)S(1)} %get-tuple-element.135.refs_8_), channel_id=1, source_target_pairs={{4,8},{12,0},{8,4},{0,12},{5,9},{13,1},{9,5},{1,13},{6,10},{14,2},... | collective-permute-start | bytes 49160 | tf_op jit(solution)/shard_map/ppermute | solution.py:442
  38.5 0.7 %inner2.1 = (f32[1560,128]{1,0:T(8,128)S(1)}, f32[1024,128]{1,0:T(8,128)S(1)}, f32[1024,128]{1,0:T(8,128)S(1)}) custom-call(f32[1024,128]{1,0:T(8,128)S(1)} %get-tuple-element.130.p.refs_0_, f32[1560,128]{1,0:T(8,128)S(1)} %get-tuple-element.131.u.refs_1_, f32[1024,128]{1,0:T(8,128)S(1)} %get-tuple-element.132.v, ...), custom_call_target="tpu_custom_call" | custom-call | tf_op jit(solution)/shard_map/inner2/pallas_call | solution.py:53
  39.2 3.0 %collective-permute-done.17.refs_12_ = f32[32,128]{1,0:T(8,128)S(1)} collective-permute-done((f32[32,128]{1,0:T(8,128)S(1)}, f32[32,128]{1,0:T(8,128)S(1)}, u32[]{:S(2)}, u32[]{:S(2)}) %collective-permute-start.17) | collective-permute-done | bytes 16416 | tf_op jit(solution)/shard_map/ppermute | solution.py:442
  42.7 2.0 %collective-permute-start.20 = (f32[32,128]{1,0:T(8,128)S(1)}, f32[32,128]{1,0:T(8,128)S(1)}, u32[]{:S(2)}, u32[]{:S(2)}) collective-permute-start(f32[32,128]{1,0:T(8,128)S(1)} %get-tuple-element.149.refs_6_), channel_id=1, source_target_pairs={{0,3},{1,2},{2,1},{3,0},{4,7},{5,6},{6,5},{7,4},{8,11},{9,10},{10,... | collective-permute-start | bytes 49160 | tf_op jit(solution)/shard_map/ppermute | solution.py:446
  44.7 1.4 %collective-permute-start.19 = (f32[32,128]{1,0:T(8,128)S(1)}, f32[32,128]{1,0:T(8,128)S(1)}, u32[]{:S(2)}, u32[]{:S(2)}) collective-permute-start(f32[32,128]{1,0:T(8,128)S(1)} %get-tuple-element.149.refs_6_), channel_id=1, source_target_pairs={{0,2},{1,3},{2,0},{3,1},{4,6},{5,7},{6,4},{7,5},{8,10},{9,11},{10,... | collective-permute-start | bytes 49160 | tf_op jit(solution)/shard_map/ppermute | solution.py:446
  46.9 1.6 %upward2.1 = (f32[64,16,128]{2,1,0:T(8,128)}, f32[1024,128]{1,0:T(8,128)}, f32[1024,128]{1,0:T(8,128)S(1)}, f32[1024,128]{1,0:T(8,128)S(1)}) custom-call(f32[1024,128]{1,0:T(8,128)S(1)} %get-tuple-element.140.refs_0_, f32[1024,128]{1,0:T(8,128)S(1)} %get-tuple-element.141.refs_1_, f32[1024,128]{1,0:T(8,128)S(1)} %get-tuple-element.97.refs_2_, ...), custom_call_target="tpu_custom_call" | custom-call | tf_op jit(solution)/shard_map/upward2/pallas_call | solution.py:53
  48.5 1.4 %collective-permute-done.19.refs_8_ = f32[32,128]{1,0:T(8,128)S(1)} collective-permute-done((f32[32,128]{1,0:T(8,128)S(1)}, f32[32,128]{1,0:T(8,128)S(1)}, u32[]{:S(2)}, u32[]{:S(2)}) %collective-permute-start.19) | collective-permute-done | bytes 16416 | tf_op jit(solution)/shard_map/ppermute | solution.py:446
  50.0 1.2 %implicit2.1 = (f32[1024,128]{1,0:T(8,128)}, f32[1024,128]{1,0:T(8,128)}) custom-call(f32[1024,128]{1,0:T(8,128)S(1)} %get-tuple-element.147.refs_0_, f32[1024,128]{1,0:T(8,128)S(1)} %get-tuple-element.148.refs_1_, f32[1024,128]{1,0:T(8,128)S(1)} %get-tuple-element.106.refs_2_, f32[1024,128]{1,0:T(8,128)S(1)} %get-tuple-element.107.refs_3_, ...), custom_call_target="tpu_custom_call" | custom-call | tf_op jit(solution)/shard_map/implicit2/pallas_call | solution.py:53
  (36 shorter events, 7.9 us)
Async XLA Ops:
  0.6 9.9 %copy-start = (f32[64,16,128]{2,1,0:T(8,128)S(1)}, f32[64,16,128]{2,1,0:T(8,128)}, u32[]{:S(2)}) copy-start(f32[64,16,128]{2,1,0:T(8,128)} %param.11) | copy-start | bytes 1572868
  0.6 9.9 %copy-start.1 = (f32[64,16,128]{2,1,0:T(8,128)S(1)}, f32[64,16,128]{2,1,0:T(8,128)}, u32[]{:S(2)}) copy-start(f32[64,16,128]{2,1,0:T(8,128)} %param.8) | copy-start | bytes 1572868
  2.6 10.8 %collective-permute-start = (f32[192,128]{1,0:T(8,128)S(1)}, f32[192,128]{1,0:T(8,128)S(1)}, u32[]{:S(2)}, u32[]{:S(2)}) collective-permute-start(f32[192,128]{1,0:T(8,128)S(1)} %get-tuple-element.89), channel_id=1, source_target_pairs={{0,16},{32,48},{64,80},{96,112},{16,0},{48,32},{80,64},{112,96},{1... | collective-permute-start | bytes 294920 | tf_op jit(solution)/shard_map/ppermute | solution.py:442
  2.7 10.7 %collective-permute-start.1 = (f32[192,128]{1,0:T(8,128)S(1)}, f32[192,128]{1,0:T(8,128)S(1)}, u32[]{:S(2)}, u32[]{:S(2)}) collective-permute-start(f32[192,128]{1,0:T(8,128)S(1)} %get-tuple-element.90), channel_id=1, source_target_pairs={{16,32},{48,64},{80,96},{112,0},{32,16},{64,48},{96,80},{0,112},{1... | collective-permute-start | bytes 294920 | tf_op jit(solution)/shard_map/ppermute | solution.py:442
  6.9 5.4 %collective-permute-start.2 = (f32[32,128]{1,0:T(8,128)S(1)}, f32[32,128]{1,0:T(8,128)S(1)}, u32[]{:S(2)}, u32[]{:S(2)}) collective-permute-start(f32[32,128]{1,0:T(8,128)S(1)} %get-tuple-element.91), channel_id=1, source_target_pairs={{0,4},{8,12},{4,0},{12,8},{1,5},{9,13},{5,1},{13,9},{2,6},{10,14},... | collective-permute-start | bytes 49160 | tf_op jit(solution)/shard_map/ppermute | solution.py:442
  8.4 4.9 %collective-permute-start.3 = (f32[32,128]{1,0:T(8,128)S(1)}, f32[32,128]{1,0:T(8,128)S(1)}, u32[]{:S(2)}, u32[]{:S(2)}) collective-permute-start(f32[32,128]{1,0:T(8,128)S(1)} %get-tuple-element.92), channel_id=1, source_target_pairs={{4,8},{12,0},{8,4},{0,12},{5,9},{13,1},{9,5},{1,13},{6,10},{14,2},... | collective-permute-start | bytes 49160 | tf_op jit(solution)/shard_map/ppermute | solution.py:442
  13.9 5.3 %collective-permute-start.6 = (f32[80,128]{1,0:T(8,128)S(1)}, f32[80,128]{1,0:T(8,128)S(1)}, u32[]{:S(2)}, u32[]{:S(2)}) collective-permute-start(f32[80,128]{1,0:T(8,128)S(1)} %get-tuple-element.108.refs_6_), channel_id=1, source_target_pairs={{0,3},{1,2},{2,1},{3,0},{4,7},{5,6},{6,5},{7,4},{8,11},{9,10},{10,... | collective-permute-start | bytes 122888 | tf_op jit(solution)/shard_map/ppermute | solution.py:446
  17.0 5.5 %collective-permute-start.5 = (f32[80,128]{1,0:T(8,128)S(1)}, f32[80,128]{1,0:T(8,128)S(1)}, u32[]{:S(2)}, u32[]{:S(2)}) collective-permute-start(f32[80,128]{1,0:T(8,128)S(1)} %get-tuple-element.108.refs_6_), channel_id=1, source_target_pairs={{0,2},{1,3},{2,0},{3,1},{4,6},{5,7},{6,4},{7,5},{8,10},{9,11},{10,... | collective-permute-start | bytes 122888 | tf_op jit(solution)/shard_map/ppermute | solution.py:446
  17.6 4.9 %collective-permute-start.4 = (f32[80,128]{1,0:T(8,128)S(1)}, f32[80,128]{1,0:T(8,128)S(1)}, u32[]{:S(2)}, u32[]{:S(2)}) collective-permute-start(f32[80,128]{1,0:T(8,128)S(1)} %get-tuple-element.108.refs_6_), channel_id=1, source_target_pairs={{0,1},{1,0},{2,3},{3,2},{4,5},{5,4},{6,7},{7,6},{8,9},{9,8},{10,11... | collective-permute-start | bytes 122888 | tf_op jit(solution)/shard_map/ppermute | solution.py:446
  23.0 6.4 %collective-permute-start.7 = (f32[128,128]{1,0:T(8,128)S(1)}, f32[128,128]{1,0:T(8,128)S(1)}, u32[]{:S(2)}, u32[]{:S(2)}) collective-permute-start(f32[128,128]{1,0:T(8,128)S(1)} %get-tuple-element.118), channel_id=1, source_target_pairs={{0,16},{32,48},{64,80},{96,112},{16,0},{48,32},{80,64},{112,96},{1... | collective-permute-start | bytes 196616 | tf_op jit(solution)/shard_map/ppermute | solution.py:442
  23.1 6.3 %collective-permute-start.8 = (f32[128,128]{1,0:T(8,128)S(1)}, f32[128,128]{1,0:T(8,128)S(1)}, u32[]{:S(2)}, u32[]{:S(2)}) collective-permute-start(f32[128,128]{1,0:T(8,128)S(1)} %get-tuple-element.119), channel_id=1, source_target_pairs={{16,32},{48,64},{80,96},{112,0},{32,16},{64,48},{96,80},{0,112},{1... | collective-permute-start | bytes 196616 | tf_op jit(solution)/shard_map/ppermute | solution.py:442
  23.6 4.9 %collective-permute-start.10 = (f32[32,128]{1,0:T(8,128)S(1)}, f32[32,128]{1,0:T(8,128)S(1)}, u32[]{:S(2)}, u32[]{:S(2)}) collective-permute-start(f32[32,128]{1,0:T(8,128)S(1)} %get-tuple-element.117.refs_8_), channel_id=1, source_target_pairs={{4,8},{12,0},{8,4},{0,12},{5,9},{13,1},{9,5},{1,13},{6,10},{14,2},... | collective-permute-start | bytes 49160 | tf_op jit(solution)/shard_map/ppermute | solution.py:442
  25.7 3.7 %collective-permute-start.9 = (f32[32,128]{1,0:T(8,128)S(1)}, f32[32,128]{1,0:T(8,128)S(1)}, u32[]{:S(2)}, u32[]{:S(2)}) collective-permute-start(f32[32,128]{1,0:T(8,128)S(1)} %get-tuple-element.117.refs_8_), channel_id=1, source_target_pairs={{0,4},{8,12},{4,0},{12,8},{1,5},{9,13},{5,1},{13,9},{2,6},{10,14},... | collective-permute-start | bytes 49160 | tf_op jit(solution)/shard_map/ppermute | solution.py:442
  29.9 5.0 %collective-permute-start.13 = (f32[32,128]{1,0:T(8,128)S(1)}, f32[32,128]{1,0:T(8,128)S(1)}, u32[]{:S(2)}, u32[]{:S(2)}) collective-permute-start(f32[32,128]{1,0:T(8,128)S(1)} %get-tuple-element.128.refs_6_), channel_id=1, source_target_pairs={{0,3},{1,2},{2,1},{3,0},{4,7},{5,6},{6,5},{7,4},{8,11},{9,10},{10,... | collective-permute-start | bytes 49160 | tf_op jit(solution)/shard_map/ppermute | solution.py:446
  31.3 5.2 %collective-permute-start.12 = (f32[32,128]{1,0:T(8,128)S(1)}, f32[32,128]{1,0:T(8,128)S(1)}, u32[]{:S(2)}, u32[]{:S(2)}) collective-permute-start(f32[32,128]{1,0:T(8,128)S(1)} %get-tuple-element.128.refs_6_), channel_id=1, source_target_pairs={{0,2},{1,3},{2,0},{3,1},{4,6},{5,7},{6,4},{7,5},{8,10},{9,11},{10,... | collective-permute-start | bytes 49160 | tf_op jit(solution)/shard_map/ppermute | solution.py:446
  32.2 4.3 %collective-permute-start.11 = (f32[32,128]{1,0:T(8,128)S(1)}, f32[32,128]{1,0:T(8,128)S(1)}, u32[]{:S(2)}, u32[]{:S(2)}) collective-permute-start(f32[32,128]{1,0:T(8,128)S(1)} %get-tuple-element.128.refs_6_), channel_id=1, source_target_pairs={{0,1},{1,0},{2,3},{3,2},{4,5},{5,4},{6,7},{7,6},{8,9},{9,8},{10,11... | collective-permute-start | bytes 49160 | tf_op jit(solution)/shard_map/ppermute | solution.py:446
  37.0 5.3 %collective-permute-start.14 = (f32[128,128]{1,0:T(8,128)S(1)}, f32[128,128]{1,0:T(8,128)S(1)}, u32[]{:S(2)}, u32[]{:S(2)}) collective-permute-start(f32[128,128]{1,0:T(8,128)S(1)} %get-tuple-element.136), channel_id=1, source_target_pairs={{0,16},{32,48},{64,80},{96,112},{16,0},{48,32},{80,64},{112,96},{1... | collective-permute-start | bytes 196616 | tf_op jit(solution)/shard_map/ppermute | solution.py:442
  37.0 5.2 %collective-permute-start.15 = (f32[128,128]{1,0:T(8,128)S(1)}, f32[128,128]{1,0:T(8,128)S(1)}, u32[]{:S(2)}, u32[]{:S(2)}) collective-permute-start(f32[128,128]{1,0:T(8,128)S(1)} %get-tuple-element.137), channel_id=1, source_target_pairs={{16,32},{48,64},{80,96},{112,0},{32,16},{64,48},{96,80},{0,112},{1... | collective-permute-start | bytes 196616 | tf_op jit(solution)/shard_map/ppermute | solution.py:442
  37.3 4.9 %collective-permute-start.17 = (f32[32,128]{1,0:T(8,128)S(1)}, f32[32,128]{1,0:T(8,128)S(1)}, u32[]{:S(2)}, u32[]{:S(2)}) collective-permute-start(f32[32,128]{1,0:T(8,128)S(1)} %get-tuple-element.135.refs_8_), channel_id=1, source_target_pairs={{4,8},{12,0},{8,4},{0,12},{5,9},{13,1},{9,5},{1,13},{6,10},{14,2},... | collective-permute-start | bytes 49160 | tf_op jit(solution)/shard_map/ppermute | solution.py:442
  38.5 3.8 %collective-permute-start.16 = (f32[32,128]{1,0:T(8,128)S(1)}, f32[32,128]{1,0:T(8,128)S(1)}, u32[]{:S(2)}, u32[]{:S(2)}) collective-permute-start(f32[32,128]{1,0:T(8,128)S(1)} %get-tuple-element.135.refs_8_), channel_id=1, source_target_pairs={{0,4},{8,12},{4,0},{12,8},{1,5},{9,13},{5,1},{13,9},{2,6},{10,14},... | collective-permute-start | bytes 49160 | tf_op jit(solution)/shard_map/ppermute | solution.py:442
  42.7 5.8 %collective-permute-start.20 = (f32[32,128]{1,0:T(8,128)S(1)}, f32[32,128]{1,0:T(8,128)S(1)}, u32[]{:S(2)}, u32[]{:S(2)}) collective-permute-start(f32[32,128]{1,0:T(8,128)S(1)} %get-tuple-element.149.refs_6_), channel_id=1, source_target_pairs={{0,3},{1,2},{2,1},{3,0},{4,7},{5,6},{6,5},{7,4},{8,11},{9,10},{10,... | collective-permute-start | bytes 49160 | tf_op jit(solution)/shard_map/ppermute | solution.py:446
  44.7 5.2 %collective-permute-start.19 = (f32[32,128]{1,0:T(8,128)S(1)}, f32[32,128]{1,0:T(8,128)S(1)}, u32[]{:S(2)}, u32[]{:S(2)}) collective-permute-start(f32[32,128]{1,0:T(8,128)S(1)} %get-tuple-element.149.refs_6_), channel_id=1, source_target_pairs={{0,2},{1,3},{2,0},{3,1},{4,6},{5,7},{6,4},{7,5},{8,10},{9,11},{10,... | collective-permute-start | bytes 49160 | tf_op jit(solution)/shard_map/ppermute | solution.py:446
  46.2 3.8 %collective-permute-start.18 = (f32[32,128]{1,0:T(8,128)S(1)}, f32[32,128]{1,0:T(8,128)S(1)}, u32[]{:S(2)}, u32[]{:S(2)}) collective-permute-start(f32[32,128]{1,0:T(8,128)S(1)} %get-tuple-element.149.refs_6_), channel_id=1, source_target_pairs={{0,1},{1,0},{2,3},{3,2},{4,5},{5,4},{6,7},{7,6},{8,9},{9,8},{10,11... | collective-permute-start | bytes 49160 | tf_op jit(solution)/shard_map/ppermute | solution.py:446

commit v5 on v4

--- a/solution.py
+++ b/solution.py
@@ -7,6 +7,7 @@
 from jax.experimental.pallas import tpu as pltpu
 from jax.sharding import PartitionSpec as P
 
+
 SUBSTEPS = 3
 
 courant_h = 0.3
@@ -45,7 +46,7 @@
     return pltpu.HBM(shape, F32)
 
 
-def call(body, outs, args, name, scratch=(), aliases=None, far_in=0, far_out=0, limit=2):
+def call(body, outs, args, scratch=(), aliases=None, far_in=0, far_out=0, limit=2):
     near, far = pl.BlockSpec(memory_space=pltpu.VMEM), pl.BlockSpec(memory_space=pltpu.HBM)
     args = [
         pltpu.with_memory_space_constraint(x, pltpu.HBM if at < far_in else pltpu.VMEM) for at, x in enumerate(args)
@@ -57,7 +58,6 @@
         out_specs=(far,) * far_out + (near,) * (len(outs) - far_out),
         scratch_shapes=list(scratch),
         input_output_aliases=aliases or {},
-        name=name,
         compiler_params=pltpu.CompilerParams(vmem_limit_bytes=limit << 20),
     )(*args)
 
@@ -452,28 +452,28 @@
         prologue,
         [BLOCK] * 3 + [PADDED, (3 * NK, NL), (3 * NK, NL)] + [PACK] * 4,
         [x.reshape(BLOCK) for x in (pressure, v_wind, buoyancy)] + [u_wind],
-        "prologue",
         scratch=[pltpu.SemaphoreType.DMA((4,))],
         far_in=4,
     )
     (theta, rest, g, eta, inv, t1, y1, a_p, top_p, a_w, top_w, v, b_v, statics, sums) = call(
-        factor, [BLOCK] * 13 + [(3 * NI, NL), (2 * NI, NL)], [s, w, b, v], "factor"
+        factor, [BLOCK] * 13 + [(3 * NI, NL), (2 * NI, NL)], [s, w, b, v]
     )
     side, more = statics, [to_right]
     for step in range(SUBSTEPS):
         first, last = step == 0, step == SUBSTEPS - 1
-        chip, far = swap(to_chip, "gx", 0), swap(to_far, "gx", 1)
-        by_first, by_second = swap(to_first, "gy", 0), swap(to_second, "gy", 1)
-        u_part, v_part, star_part = call(
-            functools.partial(inner, first), [PADDED, BLOCK, BLOCK], [p, u, v, b, b_v, s], f"inner{step}"
-        )
+        chip = swap(to_chip, "gx", 0)
+        far = swap(to_far, "gx", 1)
+        by_first = swap(to_first, "gy", 0)
+        by_second = swap(to_second, "gy", 1)
+        u_part, v_part, star_part = call(functools.partial(inner, first), [PADDED, BLOCK, BLOCK], [p, u, v, b, b_v, s])
         args = [p, u, b, star_part, s, a_p, top_p, sums, own, chip, far, by_first, by_second, side, u_part] + more
         outs = [PADDED, BLOCK, ((5 if first else 2) * NI, NL)]
         outs += [PACK] if last else [(2 * PACK[0], NL), (4 * NK, NL)]
-        u, p_star, message, side, *more = call(
-            functools.partial(explicit, first, last), outs, args, f"explicit{step}", aliases={14: 0}
-        )
-        by1, by3, by2 = (partner(message, mask) for mask in (1, 3, 2))
+        u, p_star, message, side, *more = call(functools.partial(explicit, first, last), outs, args, aliases={14: 0})
+        partners = []
+        for mask in (1, 2, 3):
+            partners.append(partner(message, mask))
+        by1, by2, by3 = partners
         args = [p_star, w, theta, rest, g, eta, inv, v_part, side]
         outs = [BLOCK] * 3
         if last:
@@ -481,16 +481,15 @@
                 functools.partial(upward, False, True),
                 [(NK, NI, NL)] + outs,
                 args + [u],
-                f"upward{step}",
                 scratch=[vmem(*BLOCK), pltpu.SemaphoreType.DMA((1 + NK // BATCH,))],
                 far_out=2,
             )
         elif first:
             t0, y0, v, b_v = call(
-                functools.partial(upward, True, False), outs + [BLOCK], args + [b_v, by_first, by_second], f"upward{step}"
+                functools.partial(upward, True, False), outs + [BLOCK], args + [b_v, by_first, by_second]
             )
         else:
-            t0, y0, v = call(functools.partial(upward, False, False), outs, args, f"upward{step}")
+            t0, y0, v = call(functools.partial(upward, False, False), outs, args)
         args = [t0, y0, t1, y1, eta, inv, message, by1, by2, by3]
         args += [] if first else [kept]
         body = functools.partial(implicit, first, last)
@@ -499,7 +498,6 @@
                 body,
                 [BLOCK] * 2,
                 args,
-                f"implicit{step}",
                 scratch=[vmem(*BLOCK), vmem(*BLOCK), pltpu.SemaphoreType.DMA((2 * NK // CHUNK,))],
                 far_out=2,
                 limit=3,
@@ -507,7 +505,7 @@
         else:
             outs = [BLOCK, BLOCK, (2 * NI, NL), (2 * NK, NL), (2 * NK, NL), PACK]
             outs += [(sum(COUNTS) * NI, NL)] if first else []
-            w, p, sums, to_chip, to_far, own, *fixed = call(body, outs, args + [a_w, top_w], f"implicit{step}")
+            w, p, sums, to_chip, to_far, own, *fixed = call(body, outs, args + [a_w, top_w])
             to_first = to_second = own
             if first:
                 kept = fixed[0]

time: 51.3 us -> 51.3 us (level)
  no operation moved by 1% of the time
where the time goes in v5:
time: 51.3 us; the launch traced here: 51.1 us
  starting transfers between devices  24.6 us (48%)
  waiting for transfers between devices  14.6 us (28%)
  Pallas kernels  11.1 us (22%)
  between operations  0.79 us (2%)
    ppermute x9, starting transfers between devices, partner(): return lax.ppermute(block, 'lev', [(i, i ^ mask) for i in range(4)])  12.5 us
    ppermute x12, starting transfers between devices, swap(): return lax.ppermute(block, axis, pairs + [(j, i) for i, j in pairs])  12.1 us
    pallas_call x14, Pallas kernels, call(): pl.pallas_call(body, out_shape=tuple(((hbm if at < far_out else vmem)(*sh...  11.1 us
    ppermute x9, waiting for transfers between devices, partner(): return lax.ppermute(block, 'lev', [(i, i ^ mask) for i in range(4)])  7.5 us
    ppermute x12, waiting for transfers between devices, swap(): return lax.ppermute(block, axis, pairs + [(j, i) for i, j in pairs])  7.09 us
  transfers between devices with their start and end apart: 21, of which 9 were waited for; matrix products, arithmetic and copies ran while one was open for 0% of the time, Pallas kernels for 11%

profile of v5, /device:TPU:0, one launch (start us, length us, event | category | flops | bytes accessed | tf_op | source)
XLA Modules:
  0.0 51.1 jit_solution(543452413331914071)
XLA Ops:
  0.7 1.9 %shard_map.93 = (f32[1024,128]{1,0:T(8,128)S(1)}, f32[1024,128]{1,0:T(8,128)S(1)}, f32[1024,128]{1,0:T(8,128)S(1)}, f32[1560,128]{1,0:T(8,128)S(1)}, f32[192,128...) custom-call(f32[1024,128]{1,0:T(8,128)} %bitcast.17, ...), custom_call_target="tpu_custom_call" | custom-call | tf_op jit(solution)/shard_map/pallas_call | solution.py:54
  2.7 4.3 %collective-permute-start.1 = (f32[192,128]{1,0:T(8,128)S(1)}, f32[192,128]{1,0:T(8,128)S(1)}, u32[]{:S(2)}, u32[]{:S(2)}) collective-permute-start(f32[192,128]{1,0:T(8,128)S(1)} %get-tuple-element.90), channel_id=1, source_target_pairs={{16,32},{48,64},{80,96},{112,0},{32,16},{64,48},{96,80},{0,112},{1... | collective-permute-start | bytes 294920 | tf_op jit(solution)/shard_map/ppermute | solution.py:442
  6.9 1.5 %collective-permute-start.2 = (f32[32,128]{1,0:T(8,128)S(1)}, f32[32,128]{1,0:T(8,128)S(1)}, u32[]{:S(2)}, u32[]{:S(2)}) collective-permute-start(f32[32,128]{1,0:T(8,128)S(1)} %get-tuple-element.91), channel_id=1, source_target_pairs={{0,4},{8,12},{4,0},{12,8},{1,5},{9,13},{5,1},{13,9},{2,6},{10,14},... | collective-permute-start | bytes 49160 | tf_op jit(solution)/shard_map/ppermute | solution.py:442
  8.4 2.1 %collective-permute-start.3 = (f32[32,128]{1,0:T(8,128)S(1)}, f32[32,128]{1,0:T(8,128)S(1)}, u32[]{:S(2)}, u32[]{:S(2)}) collective-permute-start(f32[32,128]{1,0:T(8,128)S(1)} %get-tuple-element.92), channel_id=1, source_target_pairs={{4,8},{12,0},{8,4},{0,12},{5,9},{13,1},{9,5},{1,13},{6,10},{14,2},... | collective-permute-start | bytes 49160 | tf_op jit(solution)/shard_map/ppermute | solution.py:442
  10.5 1.0 %shard_map.94 = (f32[1024,128]{1,0:T(8,128)S(1)}, f32[1024,128]{1,0:T(8,128)S(1)}, f32[1024,128]{1,0:T(8,128)S(1)}, f32[1024,128]{1,0:T(8,128)S(1)}, f32[1024,12...) custom-call(f32[1024,128]{1,0:T(8,128)S(1)} %bitcast.8, ...), custom_call_target="tpu_custom_call" | custom-call | tf_op jit(solution)/shard_map/pallas_call | solution.py:54
  11.5 0.7 %shard_map.95 = (f32[1560,128]{1,0:T(8,128)S(1)}, f32[1024,128]{1,0:T(8,128)S(1)}, f32[1024,128]{1,0:T(8,128)S(1)}) custom-call(f32[1024,128]{1,0:T(8,128)S(1)} %get-tuple-element.78.p.refs_0_, f32[1560,128]{1,0:T(8,128)S(1)} %get-tuple-element.79.u.refs_1_, f32[1024,128]{1,0:T(8,128)S(1)} %get-tuple-element.82.v, ...), custom_call_target="tpu_custom_call" | custom-call | tf_op jit(solution)/shard_map/pallas_call | solution.py:54
  12.3 1.1 %collective-permute-done.3.refs_12_.refs_11_ = f32[32,128]{1,0:T(8,128)S(1)} collective-permute-done((f32[32,128]{1,0:T(8,128)S(1)}, f32[32,128]{1,0:T(8,128)S(1)}, u32[]{:S(2)}, u32[]{:S(2)}) %collective-permute-start.3) | collective-permute-done | bytes 16416 | tf_op jit(solution)/shard_map/ppermute | solution.py:442
  13.9 3.1 %collective-permute-start.6 = (f32[80,128]{1,0:T(8,128)S(1)}, f32[80,128]{1,0:T(8,128)S(1)}, u32[]{:S(2)}, u32[]{:S(2)}) collective-permute-start(f32[80,128]{1,0:T(8,128)S(1)} %get-tuple-element.108.refs_6_), channel_id=1, source_target_pairs={{0,3},{1,2},{2,1},{3,0},{4,7},{5,6},{6,5},{7,4},{8,11},{9,10},{10,... | collective-permute-start | bytes 122888 | tf_op jit(solution)/shard_map/ppermute | solution.py:446
  19.2 3.3 %collective-permute-done.5.refs_8_ = f32[80,128]{1,0:T(8,128)S(1)} collective-permute-done((f32[80,128]{1,0:T(8,128)S(1)}, f32[80,128]{1,0:T(8,128)S(1)}, u32[]{:S(2)}, u32[]{:S(2)}) %collective-permute-start.5) | collective-permute-done | bytes 40992 | tf_op jit(solution)/shard_map/ppermute | solution.py:446
  23.6 2.1 %collective-permute-start.10 = (f32[32,128]{1,0:T(8,128)S(1)}, f32[32,128]{1,0:T(8,128)S(1)}, u32[]{:S(2)}, u32[]{:S(2)}) collective-permute-start(f32[32,128]{1,0:T(8,128)S(1)} %get-tuple-element.117.refs_8_), channel_id=1, source_target_pairs={{4,8},{12,0},{8,4},{0,12},{5,9},{13,1},{9,5},{1,13},{6,10},{14,2},... | collective-permute-start | bytes 49160 | tf_op jit(solution)/shard_map/ppermute | solution.py:442
  26.4 2.1 %collective-permute-done.10.refs_12_ = f32[32,128]{1,0:T(8,128)S(1)} collective-permute-done((f32[32,128]{1,0:T(8,128)S(1)}, f32[32,128]{1,0:T(8,128)S(1)}, u32[]{:S(2)}, u32[]{:S(2)}) %collective-permute-start.10) | collective-permute-done | bytes 16416 | tf_op jit(solution)/shard_map/ppermute | solution.py:442
  28.5 0.9 %collective-permute-done.9.refs_11_ = f32[32,128]{1,0:T(8,128)S(1)} collective-permute-done((f32[32,128]{1,0:T(8,128)S(1)}, f32[32,128]{1,0:T(8,128)S(1)}, u32[]{:S(2)}, u32[]{:S(2)}) %collective-permute-start.9) | collective-permute-done | bytes 16416 | tf_op jit(solution)/shard_map/ppermute | solution.py:442
  29.9 1.4 %collective-permute-start.13 = (f32[32,128]{1,0:T(8,128)S(1)}, f32[32,128]{1,0:T(8,128)S(1)}, u32[]{:S(2)}, u32[]{:S(2)}) collective-permute-start(f32[32,128]{1,0:T(8,128)S(1)} %get-tuple-element.128.refs_6_), channel_id=1, source_target_pairs={{0,3},{1,2},{2,1},{3,0},{4,7},{5,6},{6,5},{7,4},{8,11},{9,10},{10,... | collective-permute-start | bytes 49160 | tf_op jit(solution)/shard_map/ppermute | solution.py:446
  31.3 0.9 %collective-permute-start.12 = (f32[32,128]{1,0:T(8,128)S(1)}, f32[32,128]{1,0:T(8,128)S(1)}, u32[]{:S(2)}, u32[]{:S(2)}) collective-permute-start(f32[32,128]{1,0:T(8,128)S(1)} %get-tuple-element.128.refs_6_), channel_id=1, source_target_pairs={{0,2},{1,3},{2,0},{3,1},{4,6},{5,7},{6,4},{7,5},{8,10},{9,11},{10,... | collective-permute-start | bytes 49160 | tf_op jit(solution)/shard_map/ppermute | solution.py:446
  32.2 1.9 %collective-permute-start.11 = (f32[32,128]{1,0:T(8,128)S(1)}, f32[32,128]{1,0:T(8,128)S(1)}, u32[]{:S(2)}, u32[]{:S(2)}) collective-permute-start(f32[32,128]{1,0:T(8,128)S(1)} %get-tuple-element.128.refs_6_), channel_id=1, source_target_pairs={{0,1},{1,0},{2,3},{3,2},{4,5},{5,4},{6,7},{7,6},{8,9},{9,8},{10,11... | collective-permute-start | bytes 49160 | tf_op jit(solution)/shard_map/ppermute | solution.py:446
  34.9 1.6 %collective-permute-done.12.refs_8_ = f32[32,128]{1,0:T(8,128)S(1)} collective-permute-done((f32[32,128]{1,0:T(8,128)S(1)}, f32[32,128]{1,0:T(8,128)S(1)}, u32[]{:S(2)}, u32[]{:S(2)}) %collective-permute-start.12) | collective-permute-done | bytes 16416 | tf_op jit(solution)/shard_map/ppermute | solution.py:446
  37.3 1.2 %collective-permute-start.17 = (f32[32,128]{1,0:T(8,128)S(1)}, f32[32,128]{1,0:T(8,128)S(1)}, u32[]{:S(2)}, u32[]{:S(2)}) collective-permute-start(f32[32,128]{1,0:T(8,128)S(1)} %get-tuple-element.135.refs_8_), channel_id=1, source_target_pairs={{4,8},{12,0},{8,4},{0,12},{5,9},{13,1},{9,5},{1,13},{6,10},{14,2},... | collective-permute-start | bytes 49160 | tf_op jit(solution)/shard_map/ppermute | solution.py:442
  38.5 0.7 %shard_map.103 = (f32[1560,128]{1,0:T(8,128)S(1)}, f32[1024,128]{1,0:T(8,128)S(1)}, f32[1024,128]{1,0:T(8,128)S(1)}) custom-call(f32[1024,128]{1,0:T(8,128)S(1)} %get-tuple-element.130.p.refs_0_, f32[1560,128]{1,0:T(8,128)S(1)} %get-tuple-element.131.u.refs_1_, f32[1024,128]{1,0:T(8,128)S(1)} %get-tuple-element.132.v, ...), custom_call_target="tpu_custom_call" | custom-call | tf_op jit(solution)/shard_map/pallas_call | solution.py:54
  39.2 3.0 %collective-permute-done.17.refs_12_ = f32[32,128]{1,0:T(8,128)S(1)} collective-permute-done((f32[32,128]{1,0:T(8,128)S(1)}, f32[32,128]{1,0:T(8,128)S(1)}, u32[]{:S(2)}, u32[]{:S(2)}) %collective-permute-start.17) | collective-permute-done | bytes 16416 | tf_op jit(solution)/shard_map/ppermute | solution.py:442
  42.7 2.0 %collective-permute-start.20 = (f32[32,128]{1,0:T(8,128)S(1)}, f32[32,128]{1,0:T(8,128)S(1)}, u32[]{:S(2)}, u32[]{:S(2)}) collective-permute-start(f32[32,128]{1,0:T(8,128)S(1)} %get-tuple-element.149.refs_6_), channel_id=1, source_target_pairs={{0,3},{1,2},{2,1},{3,0},{4,7},{5,6},{6,5},{7,4},{8,11},{9,10},{10,... | collective-permute-start | bytes 49160 | tf_op jit(solution)/shard_map/ppermute | solution.py:446
  44.7 1.4 %collective-permute-start.19 = (f32[32,128]{1,0:T(8,128)S(1)}, f32[32,128]{1,0:T(8,128)S(1)}, u32[]{:S(2)}, u32[]{:S(2)}) collective-permute-start(f32[32,128]{1,0:T(8,128)S(1)} %get-tuple-element.149.refs_6_), channel_id=1, source_target_pairs={{0,2},{1,3},{2,0},{3,1},{4,6},{5,7},{6,4},{7,5},{8,10},{9,11},{10,... | collective-permute-start | bytes 49160 | tf_op jit(solution)/shard_map/ppermute | solution.py:446
  46.9 1.6 %shard_map.105 = (f32[64,16,128]{2,1,0:T(8,128)}, f32[1024,128]{1,0:T(8,128)}, f32[1024,128]{1,0:T(8,128)S(1)}, f32[1024,128]{1,0:T(8,128)S(1)}) custom-call(f32[1024,128]{1,0:T(8,128)S(1)} %get-tuple-element.140.refs_0_, f32[1024,128]{1,0:T(8,128)S(1)} %get-tuple-element.141.refs_1_, f32[1024,128]{1,0:T(8,128)S(1)} %get-tuple-element.97.refs_2_, ...), custom_call_target="tpu_custom_call" | custom-call | tf_op jit(solution)/shard_map/pallas_call | solution.py:54
  48.5 1.4 %collective-permute-done.19.refs_8_ = f32[32,128]{1,0:T(8,128)S(1)} collective-permute-done((f32[32,128]{1,0:T(8,128)S(1)}, f32[32,128]{1,0:T(8,128)S(1)}, u32[]{:S(2)}, u32[]{:S(2)}) %collective-permute-start.19) | collective-permute-done | bytes 16416 | tf_op jit(solution)/shard_map/ppermute | solution.py:446
  50.0 1.2 %shard_map.106 = (f32[1024,128]{1,0:T(8,128)}, f32[1024,128]{1,0:T(8,128)}) custom-call(f32[1024,128]{1,0:T(8,128)S(1)} %get-tuple-element.147.refs_0_, f32[1024,128]{1,0:T(8,128)S(1)} %get-tuple-element.148.refs_1_, f32[1024,128]{1,0:T(8,128)S(1)} %get-tuple-element.106.refs_2_, f32[1024,128]{1,0:T(8,128)S(1)} %get-tuple-element.107.refs_3_, ...), custom_call_target="tpu_custom_call" | custom-call | tf_op jit(solution)/shard_map/pallas_call | solution.py:54
  (36 shorter events, 7.9 us)
Async XLA Ops:
  0.6 9.9 %copy-start = (f32[64,16,128]{2,1,0:T(8,128)S(1)}, f32[64,16,128]{2,1,0:T(8,128)}, u32[]{:S(2)}) copy-start(f32[64,16,128]{2,1,0:T(8,128)} %param.11) | copy-start | bytes 1572868
  0.6 9.9 %copy-start.1 = (f32[64,16,128]{2,1,0:T(8,128)S(1)}, f32[64,16,128]{2,1,0:T(8,128)}, u32[]{:S(2)}) copy-start(f32[64,16,128]{2,1,0:T(8,128)} %param.8) | copy-start | bytes 1572868
  2.6 10.8 %collective-permute-start = (f32[192,128]{1,0:T(8,128)S(1)}, f32[192,128]{1,0:T(8,128)S(1)}, u32[]{:S(2)}, u32[]{:S(2)}) collective-permute-start(f32[192,128]{1,0:T(8,128)S(1)} %get-tuple-element.89), channel_id=1, source_target_pairs={{0,16},{32,48},{64,80},{96,112},{16,0},{48,32},{80,64},{112,96},{1... | collective-permute-start | bytes 294920 | tf_op jit(solution)/shard_map/ppermute | solution.py:442
  2.7 10.7 %collective-permute-start.1 = (f32[192,128]{1,0:T(8,128)S(1)}, f32[192,128]{1,0:T(8,128)S(1)}, u32[]{:S(2)}, u32[]{:S(2)}) collective-permute-start(f32[192,128]{1,0:T(8,128)S(1)} %get-tuple-element.90), channel_id=1, source_target_pairs={{16,32},{48,64},{80,96},{112,0},{32,16},{64,48},{96,80},{0,112},{1... | collective-permute-start | bytes 294920 | tf_op jit(solution)/shard_map/ppermute | solution.py:442
  6.9 5.4 %collective-permute-start.2 = (f32[32,128]{1,0:T(8,128)S(1)}, f32[32,128]{1,0:T(8,128)S(1)}, u32[]{:S(2)}, u32[]{:S(2)}) collective-permute-start(f32[32,128]{1,0:T(8,128)S(1)} %get-tuple-element.91), channel_id=1, source_target_pairs={{0,4},{8,12},{4,0},{12,8},{1,5},{9,13},{5,1},{13,9},{2,6},{10,14},... | collective-permute-start | bytes 49160 | tf_op jit(solution)/shard_map/ppermute | solution.py:442
  8.4 4.9 %collective-permute-start.3 = (f32[32,128]{1,0:T(8,128)S(1)}, f32[32,128]{1,0:T(8,128)S(1)}, u32[]{:S(2)}, u32[]{:S(2)}) collective-permute-start(f32[32,128]{1,0:T(8,128)S(1)} %get-tuple-element.92), channel_id=1, source_target_pairs={{4,8},{12,0},{8,4},{0,12},{5,9},{13,1},{9,5},{1,13},{6,10},{14,2},... | collective-permute-start | bytes 49160 | tf_op jit(solution)/shard_map/ppermute | solution.py:442
  13.9 5.3 %collective-permute-start.6 = (f32[80,128]{1,0:T(8,128)S(1)}, f32[80,128]{1,0:T(8,128)S(1)}, u32[]{:S(2)}, u32[]{:S(2)}) collective-permute-start(f32[80,128]{1,0:T(8,128)S(1)} %get-tuple-element.108.refs_6_), channel_id=1, source_target_pairs={{0,3},{1,2},{2,1},{3,0},{4,7},{5,6},{6,5},{7,4},{8,11},{9,10},{10,... | collective-permute-start | bytes 122888 | tf_op jit(solution)/shard_map/ppermute | solution.py:446
  17.0 5.5 %collective-permute-start.5 = (f32[80,128]{1,0:T(8,128)S(1)}, f32[80,128]{1,0:T(8,128)S(1)}, u32[]{:S(2)}, u32[]{:S(2)}) collective-permute-start(f32[80,128]{1,0:T(8,128)S(1)} %get-tuple-element.108.refs_6_), channel_id=1, source_target_pairs={{0,2},{1,3},{2,0},{3,1},{4,6},{5,7},{6,4},{7,5},{8,10},{9,11},{10,... | collective-permute-start | bytes 122888 | tf_op jit(solution)/shard_map/ppermute | solution.py:446
  17.6 4.9 %collective-permute-start.4 = (f32[80,128]{1,0:T(8,128)S(1)}, f32[80,128]{1,0:T(8,128)S(1)}, u32[]{:S(2)}, u32[]{:S(2)}) collective-permute-start(f32[80,128]{1,0:T(8,128)S(1)} %get-tuple-element.108.refs_6_), channel_id=1, source_target_pairs={{0,1},{1,0},{2,3},{3,2},{4,5},{5,4},{6,7},{7,6},{8,9},{9,8},{10,11... | collective-permute-start | bytes 122888 | tf_op jit(solution)/shard_map/ppermute | solution.py:446
  23.0 6.4 %collective-permute-start.7 = (f32[128,128]{1,0:T(8,128)S(1)}, f32[128,128]{1,0:T(8,128)S(1)}, u32[]{:S(2)}, u32[]{:S(2)}) collective-permute-start(f32[128,128]{1,0:T(8,128)S(1)} %get-tuple-element.118), channel_id=1, source_target_pairs={{0,16},{32,48},{64,80},{96,112},{16,0},{48,32},{80,64},{112,96},{1... | collective-permute-start | bytes 196616 | tf_op jit(solution)/shard_map/ppermute | solution.py:442
  23.1 6.3 %collective-permute-start.8 = (f32[128,128]{1,0:T(8,128)S(1)}, f32[128,128]{1,0:T(8,128)S(1)}, u32[]{:S(2)}, u32[]{:S(2)}) collective-permute-start(f32[128,128]{1,0:T(8,128)S(1)} %get-tuple-element.119), channel_id=1, source_target_pairs={{16,32},{48,64},{80,96},{112,0},{32,16},{64,48},{96,80},{0,112},{1... | collective-permute-start | bytes 196616 | tf_op jit(solution)/shard_map/ppermute | solution.py:442
  23.6 4.9 %collective-permute-start.10 = (f32[32,128]{1,0:T(8,128)S(1)}, f32[32,128]{1,0:T(8,128)S(1)}, u32[]{:S(2)}, u32[]{:S(2)}) collective-permute-start(f32[32,128]{1,0:T(8,128)S(1)} %get-tuple-element.117.refs_8_), channel_id=1, source_target_pairs={{4,8},{12,0},{8,4},{0,12},{5,9},{13,1},{9,5},{1,13},{6,10},{14,2},... | collective-permute-start | bytes 49160 | tf_op jit(solution)/shard_map/ppermute | solution.py:442
  25.7 3.7 %collective-permute-start.9 = (f32[32,128]{1,0:T(8,128)S(1)}, f32[32,128]{1,0:T(8,128)S(1)}, u32[]{:S(2)}, u32[]{:S(2)}) collective-permute-start(f32[32,128]{1,0:T(8,128)S(1)} %get-tuple-element.117.refs_8_), channel_id=1, source_target_pairs={{0,4},{8,12},{4,0},{12,8},{1,5},{9,13},{5,1},{13,9},{2,6},{10,14},... | collective-permute-start | bytes 49160 | tf_op jit(solution)/shard_map/ppermute | solution.py:442
  29.9 5.0 %collective-permute-start.13 = (f32[32,128]{1,0:T(8,128)S(1)}, f32[32,128]{1,0:T(8,128)S(1)}, u32[]{:S(2)}, u32[]{:S(2)}) collective-permute-start(f32[32,128]{1,0:T(8,128)S(1)} %get-tuple-element.128.refs_6_), channel_id=1, source_target_pairs={{0,3},{1,2},{2,1},{3,0},{4,7},{5,6},{6,5},{7,4},{8,11},{9,10},{10,... | collective-permute-start | bytes 49160 | tf_op jit(solution)/shard_map/ppermute | solution.py:446
  31.3 5.2 %collective-permute-start.12 = (f32[32,128]{1,0:T(8,128)S(1)}, f32[32,128]{1,0:T(8,128)S(1)}, u32[]{:S(2)}, u32[]{:S(2)}) collective-permute-start(f32[32,128]{1,0:T(8,128)S(1)} %get-tuple-element.128.refs_6_), channel_id=1, source_target_pairs={{0,2},{1,3},{2,0},{3,1},{4,6},{5,7},{6,4},{7,5},{8,10},{9,11},{10,... | collective-permute-start | bytes 49160 | tf_op jit(solution)/shard_map/ppermute | solution.py:446
  32.2 4.3 %collective-permute-start.11 = (f32[32,128]{1,0:T(8,128)S(1)}, f32[32,128]{1,0:T(8,128)S(1)}, u32[]{:S(2)}, u32[]{:S(2)}) collective-permute-start(f32[32,128]{1,0:T(8,128)S(1)} %get-tuple-element.128.refs_6_), channel_id=1, source_target_pairs={{0,1},{1,0},{2,3},{3,2},{4,5},{5,4},{6,7},{7,6},{8,9},{9,8},{10,11... | collective-permute-start | bytes 49160 | tf_op jit(solution)/shard_map/ppermute | solution.py:446
  37.0 5.3 %collective-permute-start.14 = (f32[128,128]{1,0:T(8,128)S(1)}, f32[128,128]{1,0:T(8,128)S(1)}, u32[]{:S(2)}, u32[]{:S(2)}) collective-permute-start(f32[128,128]{1,0:T(8,128)S(1)} %get-tuple-element.136), channel_id=1, source_target_pairs={{0,16},{32,48},{64,80},{96,112},{16,0},{48,32},{80,64},{112,96},{1... | collective-permute-start | bytes 196616 | tf_op jit(solution)/shard_map/ppermute | solution.py:442
  37.0 5.2 %collective-permute-start.15 = (f32[128,128]{1,0:T(8,128)S(1)}, f32[128,128]{1,0:T(8,128)S(1)}, u32[]{:S(2)}, u32[]{:S(2)}) collective-permute-start(f32[128,128]{1,0:T(8,128)S(1)} %get-tuple-element.137), channel_id=1, source_target_pairs={{16,32},{48,64},{80,96},{112,0},{32,16},{64,48},{96,80},{0,112},{1... | collective-permute-start | bytes 196616 | tf_op jit(solution)/shard_map/ppermute | solution.py:442
  37.3 4.9 %collective-permute-start.17 = (f32[32,128]{1,0:T(8,128)S(1)}, f32[32,128]{1,0:T(8,128)S(1)}, u32[]{:S(2)}, u32[]{:S(2)}) collective-permute-start(f32[32,128]{1,0:T(8,128)S(1)} %get-tuple-element.135.refs_8_), channel_id=1, source_target_pairs={{4,8},{12,0},{8,4},{0,12},{5,9},{13,1},{9,5},{1,13},{6,10},{14,2},... | collective-permute-start | bytes 49160 | tf_op jit(solution)/shard_map/ppermute | solution.py:442
  38.5 3.8 %collective-permute-start.16 = (f32[32,128]{1,0:T(8,128)S(1)}, f32[32,128]{1,0:T(8,128)S(1)}, u32[]{:S(2)}, u32[]{:S(2)}) collective-permute-start(f32[32,128]{1,0:T(8,128)S(1)} %get-tuple-element.135.refs_8_), channel_id=1, source_target_pairs={{0,4},{8,12},{4,0},{12,8},{1,5},{9,13},{5,1},{13,9},{2,6},{10,14},... | collective-permute-start | bytes 49160 | tf_op jit(solution)/shard_map/ppermute | solution.py:442
  42.7 5.8 %collective-permute-start.20 = (f32[32,128]{1,0:T(8,128)S(1)}, f32[32,128]{1,0:T(8,128)S(1)}, u32[]{:S(2)}, u32[]{:S(2)}) collective-permute-start(f32[32,128]{1,0:T(8,128)S(1)} %get-tuple-element.149.refs_6_), channel_id=1, source_target_pairs={{0,3},{1,2},{2,1},{3,0},{4,7},{5,6},{6,5},{7,4},{8,11},{9,10},{10,... | collective-permute-start | bytes 49160 | tf_op jit(solution)/shard_map/ppermute | solution.py:446
  44.7 5.2 %collective-permute-start.19 = (f32[32,128]{1,0:T(8,128)S(1)}, f32[32,128]{1,0:T(8,128)S(1)}, u32[]{:S(2)}, u32[]{:S(2)}) collective-permute-start(f32[32,128]{1,0:T(8,128)S(1)} %get-tuple-element.149.refs_6_), channel_id=1, source_target_pairs={{0,2},{1,3},{2,0},{3,1},{4,6},{5,7},{6,4},{7,5},{8,10},{9,11},{10,... | collective-permute-start | bytes 49160 | tf_op jit(solution)/shard_map/ppermute | solution.py:446
  46.2 3.8 %collective-permute-start.18 = (f32[32,128]{1,0:T(8,128)S(1)}, f32[32,128]{1,0:T(8,128)S(1)}, u32[]{:S(2)}, u32[]{:S(2)}) collective-permute-start(f32[32,128]{1,0:T(8,128)S(1)} %get-tuple-element.149.refs_6_), channel_id=1, source_target_pairs={{0,1},{1,0},{2,3},{3,2},{4,5},{5,4},{6,7},{7,6},{8,9},{9,8},{10,11... | collective-permute-start | bytes 49160 | tf_op jit(solution)/shard_map/ppermute | solution.py:446

commit v6 on v5

--- a/solution.py
+++ b/solution.py
@@ -200,7 +200,17 @@
         yield start, pl.ds(NI * start, NI * BATCH), spread
 
 
-def inner(first, p, u, v, b_u, b_v, s, u_new, v_part, star_part):
+def inner(first, p, u, v, b_u, b_v, s, *refs):
+    if first:
+        u_new, v_part, star_part = refs
+    else:
+        w, a_w, top_w, u_new, v_part, star_part, sums = refs
+        sum_a = sum_t = jnp.zeros((NI, NL), F32)
+        for k in range(NK - 1, -1, -1):
+            sum_a = sum_a - a_w[level(k), :] * w[level(k), :]
+            sum_t = sum_t + top_w[level(k), :] * w[level(k), :]
+        sums[level(0), :] = sum_a
+        sums[level(1), :] = sum_t
     for k in range(NK):
         rows = pl.ds(STEP * k + 8, NI)
         if k == 0:
@@ -382,7 +392,7 @@
     if last:
         w_far, p_far, w, p, sems = refs
     else:
-        (a_w, top_w), (w, p, sums, to_chip, to_far, edges), refs = refs[:2], refs[2:8], refs[8:]
+        (w, p, to_chip, to_far, edges), refs = refs[:5], refs[5:]
     position = lax.axis_index("lev")
     others = [ref[...] for ref in (own, by1, by2, by3)]
     by_group = []
@@ -405,8 +415,6 @@
             at += count
     w_low, p_high = interface(position, by_group, statics)
     above = p_high
-    sum_a = jnp.zeros((NI, NL), F32)
-    sum_t = jnp.zeros((NI, NL), F32)
     copies = []
     for k in range(NK - 1, -1, -1):
         wn = y0[level(k), :] + y1[level(k), :] * w_low - inv[level(k), :] * above
@@ -420,14 +428,9 @@
                     copy = pltpu.make_async_copy(source.at[part, :], target.at[part, :], sems.at[len(copies)])
                     copy.start()
                     copies.append(copy)
-        else:
-            sum_a = sum_a - a_w[level(k), :] * wn
-            sum_t = sum_t + top_w[level(k), :] * wn
     for copy in copies:
         copy.wait()
     if not last:
-        sums[level(0), :] = sum_a
-        sums[level(1), :] = sum_t
         even = is_even("gx")
         for at, (i, j) in enumerate(((NI - 1, 0), (NI - 2, 1))):
             up, down = p[block_row(i), :], p[block_row(j), :]
@@ -465,7 +468,13 @@
         far = swap(to_far, "gx", 1)
         by_first = swap(to_first, "gy", 0)
         by_second = swap(to_second, "gy", 1)
-        u_part, v_part, star_part = call(functools.partial(inner, first), [PADDED, BLOCK, BLOCK], [p, u, v, b, b_v, s])
+        u_part, v_part, star_part, *fresh = call(
+            functools.partial(inner, first),
+            [PADDED, BLOCK, BLOCK] + ([] if first else [(2 * NI, NL)]),
+            [p, u, v, b, b_v, s] + ([] if first else [w, a_w, top_w]),
+        )
+        if not first:
+            sums = fresh[0]
         args = [p, u, b, star_part, s, a_p, top_p, sums, own, chip, far, by_first, by_second, side, u_part] + more
         outs = [PADDED, BLOCK, ((5 if first else 2) * NI, NL)]
         outs += [PACK] if last else [(2 * PACK[0], NL), (4 * NK, NL)]
@@ -503,9 +512,9 @@
                 limit=3,
             )
         else:
-            outs = [BLOCK, BLOCK, (2 * NI, NL), (2 * NK, NL), (2 * NK, NL), PACK]
+            outs = [BLOCK, BLOCK, (2 * NK, NL), (2 * NK, NL), PACK]
             outs += [(sum(COUNTS) * NI, NL)] if first else []
-            w, p, sums, to_chip, to_far, own, *fixed = call(body, outs, args + [a_w, top_w])
+            w, p, to_chip, to_far, own, *fixed = call(body, outs, args)
             to_first = to_second = own
             if first:
                 kept = fixed[0]

time: 51.3 us -> 51 us (level)
  no operation moved by 1% of the time
where the time goes in v6:
time: 51 us; the launch traced here: 50.9 us
  starting transfers between devices  24.6 us (48%)
  waiting for transfers between devices  14.5 us (28%)
  Pallas kernels  10.9 us (21%)
  between operations  0.79 us (2%)
    ppermute x9, starting transfers between devices, partner(): return lax.ppermute(block, 'lev', [(i, i ^ mask) for i in range(4)])  12.5 us
    ppermute x12, starting transfers between devices, swap(): return lax.ppermute(block, axis, pairs + [(j, i) for i, j in pairs])  12.1 us
    pallas_call x14, Pallas kernels, call(): pl.pallas_call(body, out_shape=tuple(((hbm if at < far_out else vmem)(*sh...  10.9 us
    ppermute x9, waiting for transfers between devices, partner(): return lax.ppermute(block, 'lev', [(i, i ^ mask) for i in range(4)])  7.53 us
    ppermute x12, waiting for transfers between devices, swap(): return lax.ppermute(block, axis, pairs + [(j, i) for i, j in pairs])  6.96 us
  transfers between devices with their start and end apart: 21, of which 9 were waited for; matrix products, arithmetic and copies ran while one was open for 0% of the time, Pallas kernels for 11%

profile of v6, /device:TPU:0, one launch (start us, length us, event | category | flops | bytes accessed | tf_op | source)
XLA Modules:
  0.0 50.9 jit_solution(4753969875975124845)
XLA Ops:
  0.7 1.9 %shard_map.93 = (f32[1024,128]{1,0:T(8,128)S(1)}, f32[1024,128]{1,0:T(8,128)S(1)}, f32[1024,128]{1,0:T(8,128)S(1)}, f32[1560,128]{1,0:T(8,128)S(1)}, f32[192,128...) custom-call(f32[1024,128]{1,0:T(8,128)} %bitcast.17, ...), custom_call_target="tpu_custom_call" | custom-call | tf_op jit(solution)/shard_map/pallas_call | solution.py:54
  2.7 4.3 %collective-permute-start.1 = (f32[192,128]{1,0:T(8,128)S(1)}, f32[192,128]{1,0:T(8,128)S(1)}, u32[]{:S(2)}, u32[]{:S(2)}) collective-permute-start(f32[192,128]{1,0:T(8,128)S(1)} %get-tuple-element.90), channel_id=1, source_target_pairs={{16,32},{48,64},{80,96},{112,0},{32,16},{64,48},{96,80},{0,112},{1... | collective-permute-start | bytes 294920 | tf_op jit(solution)/shard_map/ppermute | solution.py:445
  6.9 1.5 %collective-permute-start.2 = (f32[32,128]{1,0:T(8,128)S(1)}, f32[32,128]{1,0:T(8,128)S(1)}, u32[]{:S(2)}, u32[]{:S(2)}) collective-permute-start(f32[32,128]{1,0:T(8,128)S(1)} %get-tuple-element.91), channel_id=1, source_target_pairs={{0,4},{8,12},{4,0},{12,8},{1,5},{9,13},{5,1},{13,9},{2,6},{10,14},... | collective-permute-start | bytes 49160 | tf_op jit(solution)/shard_map/ppermute | solution.py:445
  8.4 2.1 %collective-permute-start.3 = (f32[32,128]{1,0:T(8,128)S(1)}, f32[32,128]{1,0:T(8,128)S(1)}, u32[]{:S(2)}, u32[]{:S(2)}) collective-permute-start(f32[32,128]{1,0:T(8,128)S(1)} %get-tuple-element.92), channel_id=1, source_target_pairs={{4,8},{12,0},{8,4},{0,12},{5,9},{13,1},{9,5},{1,13},{6,10},{14,2},... | collective-permute-start | bytes 49160 | tf_op jit(solution)/shard_map/ppermute | solution.py:445
  10.5 1.0 %shard_map.94 = (f32[1024,128]{1,0:T(8,128)S(1)}, f32[1024,128]{1,0:T(8,128)S(1)}, f32[1024,128]{1,0:T(8,128)S(1)}, f32[1024,128]{1,0:T(8,128)S(1)}, f32[1024,12...) custom-call(f32[1024,128]{1,0:T(8,128)S(1)} %bitcast.8, ...), custom_call_target="tpu_custom_call" | custom-call | tf_op jit(solution)/shard_map/pallas_call | solution.py:54
  12.3 1.1 %collective-permute-done.3.refs_12_.refs_11_ = f32[32,128]{1,0:T(8,128)S(1)} collective-permute-done((f32[32,128]{1,0:T(8,128)S(1)}, f32[32,128]{1,0:T(8,128)S(1)}, u32[]{:S(2)}, u32[]{:S(2)}) %collective-permute-start.3) | collective-permute-done | bytes 16416 | tf_op jit(solution)/shard_map/ppermute | solution.py:445
  13.9 3.1 %collective-permute-start.6 = (f32[80,128]{1,0:T(8,128)S(1)}, f32[80,128]{1,0:T(8,128)S(1)}, u32[]{:S(2)}, u32[]{:S(2)}) collective-permute-start(f32[80,128]{1,0:T(8,128)S(1)} %get-tuple-element.108.refs_6_), channel_id=1, source_target_pairs={{0,3},{1,2},{2,1},{3,0},{4,7},{5,6},{6,5},{7,4},{8,11},{9,10},{10,... | collective-permute-start | bytes 122888 | tf_op jit(solution)/shard_map/ppermute | solution.py:449
  19.2 3.3 %collective-permute-done.5.refs_8_ = f32[80,128]{1,0:T(8,128)S(1)} collective-permute-done((f32[80,128]{1,0:T(8,128)S(1)}, f32[80,128]{1,0:T(8,128)S(1)}, u32[]{:S(2)}, u32[]{:S(2)}) %collective-permute-start.5) | collective-permute-done | bytes 40992 | tf_op jit(solution)/shard_map/ppermute | solution.py:449
  23.4 2.1 %collective-permute-start.10 = (f32[32,128]{1,0:T(8,128)S(1)}, f32[32,128]{1,0:T(8,128)S(1)}, u32[]{:S(2)}, u32[]{:S(2)}) collective-permute-start(f32[32,128]{1,0:T(8,128)S(1)} %get-tuple-element.118.refs_8_), channel_id=1, source_target_pairs={{4,8},{12,0},{8,4},{0,12},{5,9},{13,1},{9,5},{1,13},{6,10},{14,2},... | collective-permute-start | bytes 49160 | tf_op jit(solution)/shard_map/ppermute | solution.py:445
  25.5 0.8 %shard_map.99 = (f32[1560,128]{1,0:T(8,128)S(1)}, f32[1024,128]{1,0:T(8,128)S(1)}, f32[1024,128]{1,0:T(8,128)S(1)}, f32[32,128]{1,0:T(8,128)S(1)}) custom-call(f32[1024,128]{1,0:T(8,128)S(1)} %get-tuple-element.109.p.refs_0_, f32[1560,128]{1,0:T(8,128)S(1)} %get-tuple-element.110.u.refs_1_, f32[1024,128]{1,0:T(8,128)S(1)} %get-tuple-element.111.v, ...), custom_call_target="tpu_custom_call" | custom-call | tf_op jit(solution)/shard_map/pallas_call | solution.py:54
  26.3 2.1 %collective-permute-done.10.refs_12_ = f32[32,128]{1,0:T(8,128)S(1)} collective-permute-done((f32[32,128]{1,0:T(8,128)S(1)}, f32[32,128]{1,0:T(8,128)S(1)}, u32[]{:S(2)}, u32[]{:S(2)}) %collective-permute-start.10) | collective-permute-done | bytes 16416 | tf_op jit(solution)/shard_map/ppermute | solution.py:445
  28.4 0.9 %collective-permute-done.9.refs_11_ = f32[32,128]{1,0:T(8,128)S(1)} collective-permute-done((f32[32,128]{1,0:T(8,128)S(1)}, f32[32,128]{1,0:T(8,128)S(1)}, u32[]{:S(2)}, u32[]{:S(2)}) %collective-permute-start.9) | collective-permute-done | bytes 16416 | tf_op jit(solution)/shard_map/ppermute | solution.py:445
  29.8 1.4 %collective-permute-start.13 = (f32[32,128]{1,0:T(8,128)S(1)}, f32[32,128]{1,0:T(8,128)S(1)}, u32[]{:S(2)}, u32[]{:S(2)}) collective-permute-start(f32[32,128]{1,0:T(8,128)S(1)} %get-tuple-element.128.refs_6_), channel_id=1, source_target_pairs={{0,3},{1,2},{2,1},{3,0},{4,7},{5,6},{6,5},{7,4},{8,11},{9,10},{10,... | collective-permute-start | bytes 49160 | tf_op jit(solution)/shard_map/ppermute | solution.py:449
  31.1 0.9 %collective-permute-start.12 = (f32[32,128]{1,0:T(8,128)S(1)}, f32[32,128]{1,0:T(8,128)S(1)}, u32[]{:S(2)}, u32[]{:S(2)}) collective-permute-start(f32[32,128]{1,0:T(8,128)S(1)} %get-tuple-element.128.refs_6_), channel_id=1, source_target_pairs={{0,2},{1,3},{2,0},{3,1},{4,6},{5,7},{6,4},{7,5},{8,10},{9,11},{10,... | collective-permute-start | bytes 49160 | tf_op jit(solution)/shard_map/ppermute | solution.py:449
  32.0 1.9 %collective-permute-start.11 = (f32[32,128]{1,0:T(8,128)S(1)}, f32[32,128]{1,0:T(8,128)S(1)}, u32[]{:S(2)}, u32[]{:S(2)}) collective-permute-start(f32[32,128]{1,0:T(8,128)S(1)} %get-tuple-element.128.refs_6_), channel_id=1, source_target_pairs={{0,1},{1,0},{2,3},{3,2},{4,5},{5,4},{6,7},{7,6},{8,9},{9,8},{10,11... | collective-permute-start | bytes 49160 | tf_op jit(solution)/shard_map/ppermute | solution.py:449
  34.8 1.6 %collective-permute-done.12.refs_8_ = f32[32,128]{1,0:T(8,128)S(1)} collective-permute-done((f32[32,128]{1,0:T(8,128)S(1)}, f32[32,128]{1,0:T(8,128)S(1)}, u32[]{:S(2)}, u32[]{:S(2)}) %collective-permute-start.12) | collective-permute-done | bytes 16416 | tf_op jit(solution)/shard_map/ppermute | solution.py:449
  37.0 1.2 %collective-permute-start.17 = (f32[32,128]{1,0:T(8,128)S(1)}, f32[32,128]{1,0:T(8,128)S(1)}, u32[]{:S(2)}, u32[]{:S(2)}) collective-permute-start(f32[32,128]{1,0:T(8,128)S(1)} %get-tuple-element.136.refs_8_), channel_id=1, source_target_pairs={{4,8},{12,0},{8,4},{0,12},{5,9},{13,1},{9,5},{1,13},{6,10},{14,2},... | collective-permute-start | bytes 49160 | tf_op jit(solution)/shard_map/ppermute | solution.py:445
  38.2 0.8 %shard_map.103 = (f32[1560,128]{1,0:T(8,128)S(1)}, f32[1024,128]{1,0:T(8,128)S(1)}, f32[1024,128]{1,0:T(8,128)S(1)}, f32[32,128]{1,0:T(8,128)S(1)}) custom-call(f32[1024,128]{1,0:T(8,128)S(1)} %get-tuple-element.130.p.refs_0_, f32[1560,128]{1,0:T(8,128)S(1)} %get-tuple-element.131.u.refs_1_, f32[1024,128]{1,0:T(8,128)S(1)} %get-tuple-element.132.v, ...), custom_call_target="tpu_custom_call" | custom-call | tf_op jit(solution)/shard_map/pallas_call | solution.py:54
  39.1 2.9 %collective-permute-done.17.refs_12_ = f32[32,128]{1,0:T(8,128)S(1)} collective-permute-done((f32[32,128]{1,0:T(8,128)S(1)}, f32[32,128]{1,0:T(8,128)S(1)}, u32[]{:S(2)}, u32[]{:S(2)}) %collective-permute-start.17) | collective-permute-done | bytes 16416 | tf_op jit(solution)/shard_map/ppermute | solution.py:445
  42.4 2.0 %collective-permute-start.20 = (f32[32,128]{1,0:T(8,128)S(1)}, f32[32,128]{1,0:T(8,128)S(1)}, u32[]{:S(2)}, u32[]{:S(2)}) collective-permute-start(f32[32,128]{1,0:T(8,128)S(1)} %get-tuple-element.149.refs_6_), channel_id=1, source_target_pairs={{0,3},{1,2},{2,1},{3,0},{4,7},{5,6},{6,5},{7,4},{8,11},{9,10},{10,... | collective-permute-start | bytes 49160 | tf_op jit(solution)/shard_map/ppermute | solution.py:449
  44.5 1.4 %collective-permute-start.19 = (f32[32,128]{1,0:T(8,128)S(1)}, f32[32,128]{1,0:T(8,128)S(1)}, u32[]{:S(2)}, u32[]{:S(2)}) collective-permute-start(f32[32,128]{1,0:T(8,128)S(1)} %get-tuple-element.149.refs_6_), channel_id=1, source_target_pairs={{0,2},{1,3},{2,0},{3,1},{4,6},{5,7},{6,4},{7,5},{8,10},{9,11},{10,... | collective-permute-start | bytes 49160 | tf_op jit(solution)/shard_map/ppermute | solution.py:449
  46.6 1.6 %shard_map.105 = (f32[64,16,128]{2,1,0:T(8,128)}, f32[1024,128]{1,0:T(8,128)}, f32[1024,128]{1,0:T(8,128)S(1)}, f32[1024,128]{1,0:T(8,128)S(1)}) custom-call(f32[1024,128]{1,0:T(8,128)S(1)} %get-tuple-element.141.refs_0_, f32[1024,128]{1,0:T(8,128)S(1)} %get-tuple-element.133.refs_0_.refs_1_, f32[1024,128]{1,0:T(8,128)S(1)} %get-tuple-element.97.refs_2_, ...), custom_call_target="tpu_custom_call" | custom-call | tf_op jit(solution)/shard_map/pallas_call | solution.py:54
  48.3 1.4 %collective-permute-done.19.refs_8_ = f32[32,128]{1,0:T(8,128)S(1)} collective-permute-done((f32[32,128]{1,0:T(8,128)S(1)}, f32[32,128]{1,0:T(8,128)S(1)}, u32[]{:S(2)}, u32[]{:S(2)}) %collective-permute-start.19) | collective-permute-done | bytes 16416 | tf_op jit(solution)/shard_map/ppermute | solution.py:449
  49.7 1.1 %shard_map.106 = (f32[1024,128]{1,0:T(8,128)}, f32[1024,128]{1,0:T(8,128)}) custom-call(f32[1024,128]{1,0:T(8,128)S(1)} %get-tuple-element.147.refs_0_, f32[1024,128]{1,0:T(8,128)S(1)} %get-tuple-element.148.refs_1_, f32[1024,128]{1,0:T(8,128)S(1)} %get-tuple-element.106.refs_2_, f32[1024,128]{1,0:T(8,128)S(1)} %get-tuple-element.107.refs_3_, ...), custom_call_target="tpu_custom_call" | custom-call | tf_op jit(solution)/shard_map/pallas_call | solution.py:54
  (36 shorter events, 7.6 us)
Async XLA Ops:
  0.6 9.9 %copy-start = (f32[64,16,128]{2,1,0:T(8,128)S(1)}, f32[64,16,128]{2,1,0:T(8,128)}, u32[]{:S(2)}) copy-start(f32[64,16,128]{2,1,0:T(8,128)} %param.11) | copy-start | bytes 1572868
  0.6 9.9 %copy-start.1 = (f32[64,16,128]{2,1,0:T(8,128)S(1)}, f32[64,16,128]{2,1,0:T(8,128)}, u32[]{:S(2)}) copy-start(f32[64,16,128]{2,1,0:T(8,128)} %param.8) | copy-start | bytes 1572868
  2.6 10.8 %collective-permute-start = (f32[192,128]{1,0:T(8,128)S(1)}, f32[192,128]{1,0:T(8,128)S(1)}, u32[]{:S(2)}, u32[]{:S(2)}) collective-permute-start(f32[192,128]{1,0:T(8,128)S(1)} %get-tuple-element.89), channel_id=1, source_target_pairs={{0,16},{32,48},{64,80},{96,112},{16,0},{48,32},{80,64},{112,96},{1... | collective-permute-start | bytes 294920 | tf_op jit(solution)/shard_map/ppermute | solution.py:445
  2.7 10.7 %collective-permute-start.1 = (f32[192,128]{1,0:T(8,128)S(1)}, f32[192,128]{1,0:T(8,128)S(1)}, u32[]{:S(2)}, u32[]{:S(2)}) collective-permute-start(f32[192,128]{1,0:T(8,128)S(1)} %get-tuple-element.90), channel_id=1, source_target_pairs={{16,32},{48,64},{80,96},{112,0},{32,16},{64,48},{96,80},{0,112},{1... | collective-permute-start | bytes 294920 | tf_op jit(solution)/shard_map/ppermute | solution.py:445
  6.9 5.4 %collective-permute-start.2 = (f32[32,128]{1,0:T(8,128)S(1)}, f32[32,128]{1,0:T(8,128)S(1)}, u32[]{:S(2)}, u32[]{:S(2)}) collective-permute-start(f32[32,128]{1,0:T(8,128)S(1)} %get-tuple-element.91), channel_id=1, source_target_pairs={{0,4},{8,12},{4,0},{12,8},{1,5},{9,13},{5,1},{13,9},{2,6},{10,14},... | collective-permute-start | bytes 49160 | tf_op jit(solution)/shard_map/ppermute | solution.py:445
  8.4 4.9 %collective-permute-start.3 = (f32[32,128]{1,0:T(8,128)S(1)}, f32[32,128]{1,0:T(8,128)S(1)}, u32[]{:S(2)}, u32[]{:S(2)}) collective-permute-start(f32[32,128]{1,0:T(8,128)S(1)} %get-tuple-element.92), channel_id=1, source_target_pairs={{4,8},{12,0},{8,4},{0,12},{5,9},{13,1},{9,5},{1,13},{6,10},{14,2},... | collective-permute-start | bytes 49160 | tf_op jit(solution)/shard_map/ppermute | solution.py:445
  13.9 5.3 %collective-permute-start.6 = (f32[80,128]{1,0:T(8,128)S(1)}, f32[80,128]{1,0:T(8,128)S(1)}, u32[]{:S(2)}, u32[]{:S(2)}) collective-permute-start(f32[80,128]{1,0:T(8,128)S(1)} %get-tuple-element.108.refs_6_), channel_id=1, source_target_pairs={{0,3},{1,2},{2,1},{3,0},{4,7},{5,6},{6,5},{7,4},{8,11},{9,10},{10,... | collective-permute-start | bytes 122888 | tf_op jit(solution)/shard_map/ppermute | solution.py:449
  17.0 5.5 %collective-permute-start.5 = (f32[80,128]{1,0:T(8,128)S(1)}, f32[80,128]{1,0:T(8,128)S(1)}, u32[]{:S(2)}, u32[]{:S(2)}) collective-permute-start(f32[80,128]{1,0:T(8,128)S(1)} %get-tuple-element.108.refs_6_), channel_id=1, source_target_pairs={{0,2},{1,3},{2,0},{3,1},{4,6},{5,7},{6,4},{7,5},{8,10},{9,11},{10,... | collective-permute-start | bytes 122888 | tf_op jit(solution)/shard_map/ppermute | solution.py:449
  17.6 4.9 %collective-permute-start.4 = (f32[80,128]{1,0:T(8,128)S(1)}, f32[80,128]{1,0:T(8,128)S(1)}, u32[]{:S(2)}, u32[]{:S(2)}) collective-permute-start(f32[80,128]{1,0:T(8,128)S(1)} %get-tuple-element.108.refs_6_), channel_id=1, source_target_pairs={{0,1},{1,0},{2,3},{3,2},{4,5},{5,4},{6,7},{7,6},{8,9},{9,8},{10,11... | collective-permute-start | bytes 122888 | tf_op jit(solution)/shard_map/ppermute | solution.py:449
  22.8 6.4 %collective-permute-start.7 = (f32[128,128]{1,0:T(8,128)S(1)}, f32[128,128]{1,0:T(8,128)S(1)}, u32[]{:S(2)}, u32[]{:S(2)}) collective-permute-start(f32[128,128]{1,0:T(8,128)S(1)} %get-tuple-element.119), channel_id=1, source_target_pairs={{0,16},{32,48},{64,80},{96,112},{16,0},{48,32},{80,64},{112,96},{1... | collective-permute-start | bytes 196616 | tf_op jit(solution)/shard_map/ppermute | solution.py:445
  22.9 6.3 %collective-permute-start.8 = (f32[128,128]{1,0:T(8,128)S(1)}, f32[128,128]{1,0:T(8,128)S(1)}, u32[]{:S(2)}, u32[]{:S(2)}) collective-permute-start(f32[128,128]{1,0:T(8,128)S(1)} %get-tuple-element.120), channel_id=1, source_target_pairs={{16,32},{48,64},{80,96},{112,0},{32,16},{64,48},{96,80},{0,112},{1... | collective-permute-start | bytes 196616 | tf_op jit(solution)/shard_map/ppermute | solution.py:445
  23.4 4.9 %collective-permute-start.10 = (f32[32,128]{1,0:T(8,128)S(1)}, f32[32,128]{1,0:T(8,128)S(1)}, u32[]{:S(2)}, u32[]{:S(2)}) collective-permute-start(f32[32,128]{1,0:T(8,128)S(1)} %get-tuple-element.118.refs_8_), channel_id=1, source_target_pairs={{4,8},{12,0},{8,4},{0,12},{5,9},{13,1},{9,5},{1,13},{6,10},{14,2},... | collective-permute-start | bytes 49160 | tf_op jit(solution)/shard_map/ppermute | solution.py:445
  25.5 3.7 %collective-permute-start.9 = (f32[32,128]{1,0:T(8,128)S(1)}, f32[32,128]{1,0:T(8,128)S(1)}, u32[]{:S(2)}, u32[]{:S(2)}) collective-permute-start(f32[32,128]{1,0:T(8,128)S(1)} %get-tuple-element.118.refs_8_), channel_id=1, source_target_pairs={{0,4},{8,12},{4,0},{12,8},{1,5},{9,13},{5,1},{13,9},{2,6},{10,14},... | collective-permute-start | bytes 49160 | tf_op jit(solution)/shard_map/ppermute | solution.py:445
  29.8 5.0 %collective-permute-start.13 = (f32[32,128]{1,0:T(8,128)S(1)}, f32[32,128]{1,0:T(8,128)S(1)}, u32[]{:S(2)}, u32[]{:S(2)}) collective-permute-start(f32[32,128]{1,0:T(8,128)S(1)} %get-tuple-element.128.refs_6_), channel_id=1, source_target_pairs={{0,3},{1,2},{2,1},{3,0},{4,7},{5,6},{6,5},{7,4},{8,11},{9,10},{10,... | collective-permute-start | bytes 49160 | tf_op jit(solution)/shard_map/ppermute | solution.py:449
  31.1 5.2 %collective-permute-start.12 = (f32[32,128]{1,0:T(8,128)S(1)}, f32[32,128]{1,0:T(8,128)S(1)}, u32[]{:S(2)}, u32[]{:S(2)}) collective-permute-start(f32[32,128]{1,0:T(8,128)S(1)} %get-tuple-element.128.refs_6_), channel_id=1, source_target_pairs={{0,2},{1,3},{2,0},{3,1},{4,6},{5,7},{6,4},{7,5},{8,10},{9,11},{10,... | collective-permute-start | bytes 49160 | tf_op jit(solution)/shard_map/ppermute | solution.py:449
  32.0 4.3 %collective-permute-start.11 = (f32[32,128]{1,0:T(8,128)S(1)}, f32[32,128]{1,0:T(8,128)S(1)}, u32[]{:S(2)}, u32[]{:S(2)}) collective-permute-start(f32[32,128]{1,0:T(8,128)S(1)} %get-tuple-element.128.refs_6_), channel_id=1, source_target_pairs={{0,1},{1,0},{2,3},{3,2},{4,5},{5,4},{6,7},{7,6},{8,9},{9,8},{10,11... | collective-permute-start | bytes 49160 | tf_op jit(solution)/shard_map/ppermute | solution.py:449
  36.7 5.3 %collective-permute-start.14 = (f32[128,128]{1,0:T(8,128)S(1)}, f32[128,128]{1,0:T(8,128)S(1)}, u32[]{:S(2)}, u32[]{:S(2)}) collective-permute-start(f32[128,128]{1,0:T(8,128)S(1)} %get-tuple-element.137), channel_id=1, source_target_pairs={{0,16},{32,48},{64,80},{96,112},{16,0},{48,32},{80,64},{112,96},{1... | collective-permute-start | bytes 196616 | tf_op jit(solution)/shard_map/ppermute | solution.py:445
  36.8 5.2 %collective-permute-start.15 = (f32[128,128]{1,0:T(8,128)S(1)}, f32[128,128]{1,0:T(8,128)S(1)}, u32[]{:S(2)}, u32[]{:S(2)}) collective-permute-start(f32[128,128]{1,0:T(8,128)S(1)} %get-tuple-element.138), channel_id=1, source_target_pairs={{16,32},{48,64},{80,96},{112,0},{32,16},{64,48},{96,80},{0,112},{1... | collective-permute-start | bytes 196616 | tf_op jit(solution)/shard_map/ppermute | solution.py:445
  37.0 4.9 %collective-permute-start.17 = (f32[32,128]{1,0:T(8,128)S(1)}, f32[32,128]{1,0:T(8,128)S(1)}, u32[]{:S(2)}, u32[]{:S(2)}) collective-permute-start(f32[32,128]{1,0:T(8,128)S(1)} %get-tuple-element.136.refs_8_), channel_id=1, source_target_pairs={{4,8},{12,0},{8,4},{0,12},{5,9},{13,1},{9,5},{1,13},{6,10},{14,2},... | collective-permute-start | bytes 49160 | tf_op jit(solution)/shard_map/ppermute | solution.py:445
  38.2 3.8 %collective-permute-start.16 = (f32[32,128]{1,0:T(8,128)S(1)}, f32[32,128]{1,0:T(8,128)S(1)}, u32[]{:S(2)}, u32[]{:S(2)}) collective-permute-start(f32[32,128]{1,0:T(8,128)S(1)} %get-tuple-element.136.refs_8_), channel_id=1, source_target_pairs={{0,4},{8,12},{4,0},{12,8},{1,5},{9,13},{5,1},{13,9},{2,6},{10,14},... | collective-permute-start | bytes 49160 | tf_op jit(solution)/shard_map/ppermute | solution.py:445
  42.4 5.8 %collective-permute-start.20 = (f32[32,128]{1,0:T(8,128)S(1)}, f32[32,128]{1,0:T(8,128)S(1)}, u32[]{:S(2)}, u32[]{:S(2)}) collective-permute-start(f32[32,128]{1,0:T(8,128)S(1)} %get-tuple-element.149.refs_6_), channel_id=1, source_target_pairs={{0,3},{1,2},{2,1},{3,0},{4,7},{5,6},{6,5},{7,4},{8,11},{9,10},{10,... | collective-permute-start | bytes 49160 | tf_op jit(solution)/shard_map/ppermute | solution.py:449
  44.5 5.2 %collective-permute-start.19 = (f32[32,128]{1,0:T(8,128)S(1)}, f32[32,128]{1,0:T(8,128)S(1)}, u32[]{:S(2)}, u32[]{:S(2)}) collective-permute-start(f32[32,128]{1,0:T(8,128)S(1)} %get-tuple-element.149.refs_6_), channel_id=1, source_target_pairs={{0,2},{1,3},{2,0},{3,1},{4,6},{5,7},{6,4},{7,5},{8,10},{9,11},{10,... | collective-permute-start | bytes 49160 | tf_op jit(solution)/shard_map/ppermute | solution.py:449
  45.9 3.8 %collective-permute-start.18 = (f32[32,128]{1,0:T(8,128)S(1)}, f32[32,128]{1,0:T(8,128)S(1)}, u32[]{:S(2)}, u32[]{:S(2)}) collective-permute-start(f32[32,128]{1,0:T(8,128)S(1)} %get-tuple-element.149.refs_6_), channel_id=1, source_target_pairs={{0,1},{1,0},{2,3},{3,2},{4,5},{5,4},{6,7},{7,6},{8,9},{9,8},{10,11... | collective-permute-start | bytes 49160 | tf_op jit(solution)/shard_map/ppermute | solution.py:449
